TPU v7x, 512 devices: a whole 4x4x16 slice. The times are simulated.
512 devices in a mesh: section: 8 (over x, core), dp: 32 (over z, y_lo), mp: 2 (over y_hi).
Axes of the slice: x: 4, y: 4 (y_hi: 2, y_lo: 2; y = y_hi * 2 + y_lo), z: 16, core: 2. Of those that a mesh axis runs over, the one named last changes fastest.
Arguments:
- layer_inputs: bfloat16 [8, 128, 4096], P('section', None, 'mp'), may hold values from -6 to 6
- pre_act: bfloat16 [8, 128, 8192], P('section', None, 'dp'), may hold values from -6 to 6
- out_grad: bfloat16 [128, 4096], P(None, 'mp'), may hold values from -4 to 4
- w_in: bfloat16 [32, 8, 32, 4096], P('dp', 'section', None, 'mp'), may hold values from -0.09375 to 0.09375
- w_out: bfloat16 [32, 8, 32, 4096], P('dp', 'section', None, 'mp'), may hold values from -0.0625 to 0.0625
Outputs:
- in_grads: bfloat16 [8, 128, 4096], P('section', None, 'mp')
- grad_in: float32 [32, 8, 32, 4096], P('dp', 'section', None, 'mp')
- grad_out: float32 [32, 8, 32, 4096], P('dp', 'section', None, 'mp')
All inputs are finite; a program needn't handle non-finite values.
Results may differ from a plain program's by a relative error of at most 0.035.
Values may be sent and summed in bfloat16 or wider, within the bound.
A program may use at most 64 MiB of HBM per device.

v0:
```python
import contextlib

import jax
import jax.numpy as jnp
from jax import lax
from jax.experimental import pallas as pl
from jax.experimental.pallas import tpu as pltpu
from jax.sharding import Mesh
from jax.sharding import PartitionSpec as P

AXES = ("x", "core", "z", "ylo", "yhi")
MESH_ID = pl.DeviceIdType.MESH
BF16, F32 = jnp.bfloat16, jnp.float32
LANES = 128
PROFILE = False


def scope(name):
    return jax.named_scope(name) if PROFILE else contextlib.nullcontext()


def gelu_parts(v):
    cdf = 0.5 * (1.0 + lax.erf(v * 0.7071067811865476))
    dens = jnp.exp(-0.5 * v * v) * 0.3989422804014327
    return cdf, dens


def kernel(
    li_hbm, pa_hbm, og_hbm, wi_hbm, wo_hbm,
    ig_out, gi_out, go_out,
    wbuf, pa, pa_all, pb, pc, slope, h_t, hall, li, og,
    xs, a_buf, b_buf, gbuf, gz, gt, up, gsum,
    lsem, wx_s, wx_r, wz_s, wz_r, st_s, st_r, ph_s, ph_r, li_s, li_r,
    g_s, g_r, uz_s, uz_r, ux_s, ux_r, ud_s, ud_r, o_s,
):
    nx, nz = lax.axis_size("x"), lax.axis_size("z")
    nsec = 2 * nx
    fb, width = wi_hbm.shape
    fe = width // 2
    tok = nz * 8
    tiles = nz * fb // LANES
    per_tile = LANES // fb
    x, core, z = lax.axis_index("x"), lax.axis_index("core"), lax.axis_index("z")
    ylo, yhi = lax.axis_index("ylo"), lax.axis_index("yhi")
    sec = x * 2 + core
    y = yhi * 2 + ylo
    other = 1 - ylo
    partner = yhi * 2 + other

    def dev(sec_=None, z_=None, y_=None):
        sec_ = sec if sec_ is None else sec_
        y_ = y if y_ is None else y_
        return (sec_ // 2, lax.rem(sec_, 2), z if z_ is None else z_, lax.rem(y_, 2), y_ // 2)

    def copy(src, dst, ssem, rsem, to):
        return pltpu.make_async_remote_copy(
            src_ref=src, dst_ref=dst, send_sem=ssem, recv_sem=rsem, device_id=to, device_id_type=MESH_ID
        )

    def send(*args):
        cp = copy(*args)
        cp.start()
        return cp

    def await_bytes(ref, sem):
        pltpu.make_async_copy(ref, ref, sem).wait()

    def zat(d):
        return lax.rem(z + d + nz, nz)

    def sat(d):
        return lax.rem(sec + d, nsec)

    def xat(d):
        return lax.rem(x + d + nx, nx) * 2 + core

    def yat(d):
        return lax.rem(y + d, 4)

    y_order = (2, 1, 3)
    sec_order = sorted(((dx, dc) for dx in range(nx) for dc in range(2) if dx or dc), key=lambda p: -min(p[0], nx - p[0]))
    x_order = [dx for dx, dc in sec_order if dc == 0]

    def peer(dx, dc):
        return lax.rem(x + dx, nx) * 2 + (1 - core if dc else core)

    mine = pl.ds(pl.multiple_of(ylo * fe, LANES), fe)
    theirs = pl.ds(pl.multiple_of(other * fe, LANES), fe)

    w_hbm = (wi_hbm, wo_hbm)
    local = [pltpu.make_async_copy(pa_hbm, pa, lsem.at[0])]
    for m in range(2):
        local.append(pltpu.make_async_copy(w_hbm[m].at[:, mine], wbuf.at[m, ylo, z], lsem.at[1 + m]))
    local.append(pltpu.make_async_copy(og_hbm, og, lsem.at[3]))
    local.append(pltpu.make_async_copy(li_hbm, li.at[core, x], lsem.at[4]))
    for cp in local:
        cp.start()

    barrier = pltpu.get_barrier_semaphore()
    greeted = 0
    for to in (
        [dev(z_=zat(d)) for d in range(1, nz)] + [dev(sec_=sat(d)) for d in range(1, nsec)] + [dev(y_=yat(d)) for d in range(1, 4)]
    ):
        pl.semaphore_signal(barrier, inc=1, device_id=to, device_id_type=MESH_ID)
        greeted += 1
    local[0].wait()
    v = pa[...].astype(F32).reshape(tok, nsec * fb)
    h_t[...] = jnp.swapaxes(v * gelu_parts(v)[0], 0, 1).astype(BF16).reshape(nsec, fb, tok)
    with scope("barrier"):
        pl.semaphore_wait(barrier, greeted)

    for d in range(1, nz):
        send(pa.at[zat(d)], pa_all.at[z], st_s.at[0], st_r.at[0], dev(z_=zat(d)))
    swaps = [
        send(w_hbm[m].at[:, theirs], wbuf.at[m, ylo, z], wx_s.at[m], wx_r.at[m], dev(y_=partner))
        for m in range(2)
    ]
    for d in range(1, nsec):
        send(h_t.at[sat(d)], hall.at[sec], st_s.at[3], st_r.at[3], dev(sec_=sat(d)))
    hall[sec] = h_t[sec]
    pa_all[z] = pa[z]

    half = nz // 2

    def hop(k):
        last = k == half
        for which in range(2):
            l = ylo if which == 0 else other
            for m in range(2):
                if k == 1:
                    if which == 0:
                        local[1 + m].wait()
                    else:
                        swaps[m].wait_recv()
                for way, step in ((0, 1), (1, -1)):
                    if k > 1:
                        await_bytes(wbuf.at[m, l, 0], wz_r.at[way, k - 2, m, l])
                    if last and way != m:
                        continue
                    src = wbuf.at[m, l, zat(-step * (k - 1))]
                    send(src, src, wz_s.at[way], wz_r.at[way, k - 1, m, l], dev(z_=zat(step)))

    def stage_b():
        await_bytes(pa_all.at[pl.ds(0, nz - 1)], st_r.at[0])
        group = lax.broadcasted_iota(jnp.int32, (8, LANES), 1) // fb
        for ct in range(nsec // per_tile):
            for t in range(tiles):
                out = [jnp.zeros((8, LANES), F32)] * per_tile
                for j in range(per_tile):
                    v = pa_all[t * per_tile + j, :, ct * LANES:(ct + 1) * LANES].astype(F32)
                    for k in range(per_tile):
                        shift = (j - k) * fb % LANES
                        r = pltpu.roll(v, shift, 1) if shift else v
                        out[k] = jnp.where(group == j, r, out[k])
                for k in range(per_tile):
                    pb[ct * per_tile + k, t] = out[k].astype(BF16)
        for d in range(1, nsec):
            send(pb.at[sat(d)], pc.at[ylo, sec], st_s.at[1], st_r.at[1], dev(sec_=sat(d)))
        pc[ylo, sec] = pb[sec]

    def stage_c():
        await_bytes(pc.at[0, pl.ds(0, nsec - 1)], st_r.at[1])
        send(pc.at[ylo], pc.at[ylo], st_s.at[2], st_r.at[2], dev(y_=partner))

    def stage_d():
        await_bytes(pc.at[0], st_r.at[2])

        def one(s, carry):
            for l in range(2):
                v = pc[l, s].astype(F32)
                cdf, dens = gelu_parts(v)
                slope[s, l * tiles:(l + 1) * tiles] = cdf + v * dens
            return carry

        lax.fori_loop(0, nsec, one, 0)

    cut = tok // 2
    lo, hi = pl.ds(0, cut), pl.ds(cut, cut)
    ring = nx > 2

    def li_first():
        local[4].wait()
        src = li.at[core, x]
        send(src, src, li_s.at[0], li_r.at[0], dev(sec_=xat(1)))
        if ring:
            send(src, src, li_s.at[1], li_r.at[1], dev(sec_=xat(-1)))

    def li_second():
        await_bytes(li.at[0, 0], li_r.at[0])
        if ring:
            src = li.at[core, lax.rem(x + nx - 1, nx), lo]
            send(src, src, li_s.at[2], li_r.at[2], dev(sec_=xat(1)))
            await_bytes(li.at[0, 0], li_r.at[1])
            src = li.at[core, lax.rem(x + 1, nx), hi]
            send(src, src, li_s.at[3], li_r.at[3], dev(sec_=xat(-1)))

    def li_third():
        if ring:
            await_bytes(li.at[0, 0, lo], li_r.at[2])
            await_bytes(li.at[0, 0, hi], li_r.at[3])
        send(li.at[core], li.at[core], li_s.at[4], li_r.at[4], dev(sec_=peer(0, 1)))

    def first_term():
        local[3].wait()
        await_bytes(hall.at[pl.ds(0, nsec - 1)], st_r.at[3])
        gsum[0] = jnp.dot(hall[nsec - 1], og[...].reshape(tok, width), preferred_element_type=F32)
        gsum[1] = jnp.zeros((fb, width), F32)
        for j in range(nsec):
            xs[nsec - 1, j] = og[z, :, pl.ds(pl.multiple_of(ylo * fe + j * LANES, LANES), LANES)]

    plan = [(2, first_term), (3, stage_b), (3, li_first), (5, stage_c), (6, stage_d), (6, li_second)]
    for k in range(1, half + 1):
        with scope(f"hop{k}"):
            hop(k)
        with scope(f"stage{k}"):
            for at, f in plan:
                if min(at, half) == k:
                    f()
    with scope("gather_end"):
        for l in range(2):
            for way in range(2):
                await_bytes(wbuf.at[way, l, 0], wz_r.at[way, half - 1, way, l])
    li_third()

    def slot(t, core_, x_, ylo_=0, z_=0):
        return (((t * 2 + core_) * nx + x_) * 2 + ylo_) * nz + z_

    def spread_z(t):
        src = xs.at[t - 1 if isinstance(t, int) and t > 0 else lax.rem(t + nsec, nsec + 1), sec]
        dst = up.at[slot(t, core, x, ylo, z)]

        def to(d, c):
            send(src, dst, uz_s.at[0], uz_r.at[t], dev(z_=zat(d)))
            return c

        def to_partner(d, c):
            send(src, dst, uz_s.at[0], uz_r.at[t], dev(z_=zat(d), y_=partner))
            return c

        lax.fori_loop(1, nz, to, 0)
        lax.fori_loop(0, nz, to_partner, 0)
        dst[...] = src[...]

    def await_z(t):
        await_bytes(up.at[pl.ds(0, 2 * nz - 1)], uz_r.at[t])

    block = 2 * nz

    def spread_x(t):
        await_z(t)
        src = up.at[pl.ds(slot(t, core, x), block)]
        for dx in x_order:
            send(src, src, ux_s.at[0], ux_r.at[t], dev(sec_=peer(dx, 0)))

    def spread_core(t):
        await_bytes(up.at[pl.ds(0, (nx - 1) * block)], ux_r.at[t])
        src = up.at[pl.ds(slot(t, core, 0), nx * block)]
        send(src, src, ud_s.at[0], ud_r.at[t], dev(sec_=peer(0, 1)))

    def write_out(t):
        for l in range(2):
            for k in range(nsec):
                pltpu.make_async_copy(
                    up.at[pl.ds(slot(t, k % 2, k // 2, l), nz)],
                    ig_out.at[:, :, pl.ds(l * fe + k * LANES, LANES)],
                    o_s.at[0],
                ).start()

    def out_term(t):
        await_bytes(up.at[pl.ds(0, nx * block)], ud_r.at[t])
        rows = hall[t - 1]
        for l in range(2):
            rhs = jnp.concatenate(
                [up[pl.ds(slot(t, k % 2, k // 2, l), nz)].reshape(tok, LANES) for k in range(nsec)], axis=1
            )
            gsum[0, :, l * fe:(l + 1) * fe] += jnp.dot(rows, rhs, preferred_element_type=F32)

        @pl.when(sec == t)
        def _():
            write_out(t)

    def spread_g(t):
        def to(d, c):
            send(gbuf.at[t, ylo * tiles + zat(d) // per_tile], gz.at[t * nz + z], g_s.at[0], g_r.at[t], dev(z_=zat(d)))
            return c

        lax.fori_loop(1, nz, to, 0)
        gz[t * nz + z] = gbuf[t, ylo * tiles + z // per_tile]

    def in_term(t):
        await_bytes(gz.at[pl.ds(0, nz - 1)], g_r.at[t])
        gt[...] = jnp.swapaxes(gz[pl.ds(t * nz, nz)].astype(F32).reshape(tok, LANES), 0, 1)
        rows = gt[pl.ds(pl.multiple_of(lax.rem(z, per_tile) * fb, fb), fb), :].astype(BF16)
        gsum[1] += jnp.dot(rows, li[lax.rem(t, 2), t // 2], preferred_element_type=F32)

    def application(i, carry):
        s = nsec - 1 - i
        with scope("a_mm"):
            upper = xs[s]
            lhs = jnp.concatenate([upper[j] for j in range(nsec)], axis=1)
            w_out = wbuf[1].reshape(2 * nz * fb, fe)
            part = lax.dot_general(lhs, w_out, (((1,), (1,)), ((), ())), preferred_element_type=F32).astype(BF16)
            a_buf[s, y] = part
        for d in y_order:
            send(a_buf.at[s, y], a_buf.at[s, y], ph_s.at[0, s], ph_r.at[0, s], dev(y_=yat(d)))

        with scope("bg_a"):
            @pl.when(s <= nsec - 2)
            def _():
                spread_z(s + 1)

            @pl.when(s <= nsec - 3)
            def _():
                spread_x(s + 2)

            @pl.when(s <= nsec - 3)
            def _():
                @pl.when(s == nsec - 3)
                def _():
                    await_bytes(li.at[0], li_r.at[4])

                in_term(s + 2)

            @pl.when(s <= nsec - 4)
            def _():
                out_term(s + 3)

        with scope("wait_a"):
            await_bytes(a_buf.at[s, pl.ds(0, 3)], ph_r.at[0, s])
        with scope("b_mm"):
            back = a_buf[s, 0].astype(F32)
            for k in range(1, 4):
                back = back + a_buf[s, k].astype(F32)
            g = []
            for t in range(2 * tiles):
                g_tile = (back[:, t * LANES:(t + 1) * LANES] * slope[s, t]).astype(BF16)
                gbuf[s, t] = g_tile
                g.append(g_tile)
            g = jnp.concatenate(g, axis=1)
            w_in = wbuf[0].reshape(2 * nz * fb, fe)
            b_buf[s * nsec + sec] = jnp.dot(g, w_in, preferred_element_type=F32).astype(BF16)
        for dx, dc in sec_order:
            send(b_buf.at[s * nsec + sec], b_buf.at[s * nsec + sec], ph_s.at[1, s], ph_r.at[1, s], dev(sec_=peer(dx, dc)))

        with scope("bg_b"):
            spread_g(s)

            @pl.when(s <= nsec - 3)
            def _():
                spread_core(s + 2)

        with scope("wait_b"):
            await_bytes(b_buf.at[pl.ds(0, nsec - 1)], ph_r.at[1, s])
        with scope("sum_b"):
            for j in range(nsec):
                total = upper[j].astype(F32)
                for k in range(nsec):
                    total = total + b_buf[s * nsec + k, :, j * LANES:(j + 1) * LANES].astype(F32)
                xs[lax.rem(s + nsec, nsec + 1), j] = total.astype(BF16)
        return carry

    lax.fori_loop(0, nsec, application, 0)

    with scope("t_z0"):
        spread_z(0)
    with scope("t_x1"):
        spread_x(1)
    with scope("t_terms"):
        in_term(1)
        out_term(2)
    with scope("t_in0"):
        in_term(0)
        outs = [pltpu.make_async_copy(gsum.at[1], gi_out, o_s.at[1])]
        outs[0].start()
    with scope("t_core1"):
        spread_core(1)
    with scope("t_z0w"):
        await_z(0)

    @pl.when(sec != 0)
    def _():
        src = up.at[pl.ds(slot(0, core, x), block)]
        send(src, src, ux_s.at[1], ux_r.at[0], dev(sec_=0))

    with scope("t_out1"):
        out_term(1)
        outs.append(pltpu.make_async_copy(gsum.at[0], go_out, o_s.at[2]))
        outs[1].start()
    with scope("t_x0w"):
        @pl.when(sec == 0)
        def _():
            await_bytes(up.at[pl.ds(0, (nsec - 1) * block)], ux_r.at[0])
            write_out(0)

    with scope("drain"):
        await_bytes(pa_all.at[pl.ds(0, nz - 1)], st_s.at[0])
        await_bytes(pc.at[0, pl.ds(0, nsec - 1)], st_s.at[1])
        await_bytes(pc.at[0], st_s.at[2])
        await_bytes(hall.at[pl.ds(0, nsec - 1)], st_s.at[3])
        for cp in swaps:
            cp.wait_send()
        for way in range(2):
            await_bytes(wbuf.at[0, :, pl.ds(0, nz - 1)], wz_s.at[way])
        await_bytes(li.at[0, 0], li_s.at[0])
        if ring:
            await_bytes(li.at[0, 0], li_s.at[1])
            await_bytes(li.at[0, 0, lo], li_s.at[2])
            await_bytes(li.at[0, 0, hi], li_s.at[3])
        await_bytes(li.at[0], li_s.at[4])

        def sent(s, c):
            await_bytes(a_buf.at[0, pl.ds(0, 3)], ph_s.at[0, s])
            await_bytes(b_buf.at[pl.ds(0, nsec - 1)], ph_s.at[1, s])
            return c

        lax.fori_loop(0, nsec, sent, 0)
        await_bytes(gz.at[pl.ds(0, nsec * (nz - 1))], g_s.at[0])
        await_bytes(up.at[pl.ds(0, nsec * (2 * nz - 1))], uz_s.at[0])
        await_bytes(up.at[pl.ds(0, (nsec - 1) * (nx - 1) * block)], ux_s.at[0])
        await_bytes(up.at[pl.ds(0, (nsec - 1) * nx * block)], ud_s.at[0])

        @pl.when(sec != 0)
        def _():
            await_bytes(up.at[pl.ds(0, block)], ux_s.at[1])

        for cp in outs:
            cp.wait()
        await_bytes(up.at[pl.ds(0, nsec * block)], o_s.at[0])


def body(layer_inputs, pre_act, out_grad, w_in, w_out):
    nz, nx = lax.axis_size("z"), lax.axis_size("x")
    nsec = 2 * nx
    tok, width = out_grad.shape
    fb = w_in.shape[2]
    hid = pre_act.shape[2]
    fe = width // 2
    tiles = nz * fb // LANES
    half = nz // 2
    dma = pltpu.SemaphoreType.DMA
    vmem = pltpu.VMEM
    scratch = [
        vmem((2, 2, nz, fb, fe), BF16),
        vmem((nz, 8, hid), BF16),
        vmem((nz, 8, hid), BF16),
        vmem((nsec, tiles, 8, LANES), BF16),
        vmem((2, nsec, tiles, 8, LANES), BF16),
        vmem((nsec, 2 * tiles, 8, LANES), F32),
        vmem((nsec, fb, tok), BF16),
        vmem((nsec, fb, tok), BF16),
        vmem((2, nx, tok, width), BF16),
        vmem((nz, 8, width), BF16),
        vmem((nsec + 1, nsec, 8, LANES), BF16),
        vmem((nsec, 4, 8, 2 * nz * fb), BF16),
        vmem((nsec * nsec, 8, fe), BF16),
        vmem((nsec, 2 * tiles, 8, LANES), BF16),
        vmem((nsec * nz, 8, LANES), BF16),
        vmem((LANES, tok), F32),
        vmem((nsec * nsec * 2 * nz, 8, LANES), BF16),
        vmem((2, fb, width), F32),
        dma((5,)),
        dma((2,)), dma((2,)),
        dma((2,)), dma((2, half, 2, 2)),
        dma((4,)), dma((4,)),
        dma((2, nsec)), dma((2, nsec)),
        dma((5,)), dma((5,)),
        dma((1,)), dma((nsec,)),
        dma((1,)), dma((nsec,)),
        dma((2,)), dma((nsec,)),
        dma((1,)), dma((nsec,)),
        dma((3,)),
    ]
    any_ = pl.BlockSpec(memory_space=pltpu.HBM)
    ig, gi, go = pl.pallas_call(
        kernel,
        out_shape=(
            jax.ShapeDtypeStruct((nz, 8, width), BF16),
            jax.ShapeDtypeStruct((fb, width), F32),
            jax.ShapeDtypeStruct((fb, width), F32),
        ),
        in_specs=[any_] * 5,
        out_specs=(any_,) * 3,
        scratch_shapes=scratch,
        name="chain",
        compiler_params=pltpu.CompilerParams(
            collective_id=0, has_side_effects=True, vmem_limit_bytes=67043328
        ),
    )(
        layer_inputs.reshape(tok, width),
        pre_act.reshape(nz, 8, hid),
        out_grad.reshape(nz, 8, width),
        w_in.reshape(fb, width),
        w_out.reshape(fb, width),
    )
    return (
        ig.reshape(1, tok, width),
        gi.reshape(1, 1, fb, width),
        go.reshape(1, 1, fb, width),
    )


def solution(mesh):
    shape = mesh.shape
    split = Mesh(
        mesh.devices.reshape(shape["section"] // 2, 2, shape["dp"] // 2, 2, shape["mp"]), AXES
    )
    sec, dp = ("x", "core"), ("z", "ylo")
    placed = (
        P(sec, None, "yhi"),
        P(sec, None, dp),
        P(None, "yhi"),
        P(dp, sec, None, "yhi"),
        P(dp, sec, None, "yhi"),
    )
    return jax.shard_map(
        body,
        mesh=split,
        in_specs=placed,
        out_specs=(P(sec, None, "yhi"), P(dp, sec, None, "yhi"), P(dp, sec, None, "yhi")),
        check_vma=False,
    )
```

profile of v0, /device:TPU:24, one launch (start us, length us, event | category | flops | bytes accessed | tf_op | source)
XLA Modules:
  0.0 148.3 jit_solution(6019473253329412307)
XLA Ops:
  0.6 144.0 %chain.1 = (bf16[16,8,2048]{2,1,0:T(8,128)(2,1)}, f32[32,2048]{1,0:T(8,128)}, f32[32,2048]{1,0:T(8,128)}) custom-call(bf16[128,2048]{1,0:T(8,128)(2,1)} %bitcast.8, bf16[16,8,256]{2,1,0:T(8,128)(2,1)} %bitcast.15, bf16[16,8,2048]{2,1,0:T(8,128)(2,1)} %bitcast.9, bf16[32,2048]{1,0:T(8,128)(2,1)} %bitcast.13, bf16[32,2048]{1,0:T(8,128)(2,1)} %bitcast.14), custom_call_target="tpu_custom_call" | custom-call | tf_op jit(solution)/shard_map/chain/pallas_call | solution.py:474
  144.6 0.0 copy-start.1
  144.7 1.9 %copy.11 = bf16[1,128,2048]{2,1,0:T(8,128)(2,1)} copy(bf16[1,128,2048]{2,1,0:T(8,128)(2,1)} %bitcast.10) | data formatting | bytes 1048576
  146.6 0.0 copy-done.1
  146.6 0.0 copy-start
  146.6 0.7 copy.12
  147.3 0.3 copy-done
  147.6 0.7 copy.13
Async XLA Ops:
  144.6 1.9 %copy-start.1 = (f32[32,2048]{1,0:T(8,128)S(1)}, f32[32,2048]{1,0:T(8,128)}, u32[]{:S(2)}) copy-start(f32[32,2048]{1,0:T(8,128)} %get-tuple-element.7) | copy-start | bytes 786436
  146.6 1.0 copy-start
where the time goes:
time: 149 us; the launch traced here: 148 us
  Pallas kernels  144 us (97%)
  local copies, waits for them, and re-layouts  3.67 us (2%)
    pallas_call x1, Pallas kernels, body(): pl.pallas_call(kernel, out_shape=(jax.ShapeDtypeStruct((nz, 8, width), BF...  144 us
    unnamed x7, local copies, waits for them, and re-layouts  3.67 us

commit v1 on v0

--- a/solution.py
+++ b/solution.py
@@ -29,9 +29,9 @@
     li_hbm, pa_hbm, og_hbm, wi_hbm, wo_hbm,
     ig_out, gi_out, go_out,
     wbuf, pa, pa_all, pb, pc, slope, h_t, hall, li, og,
-    xs, a_buf, b_buf, gbuf, gz, gt, up, gsum,
+    xs, a_buf, b_buf, gbuf, gz, gt, up,
     lsem, wx_s, wx_r, wz_s, wz_r, st_s, st_r, ph_s, ph_r, li_s, li_r,
-    g_s, g_r, uz_s, uz_r, ux_s, ux_r, ud_s, ud_r, o_s,
+    g_s, g_r, uz_s, uz_r, ux_s, ux_r, ud_s, ud_r,
 ):
     nx, nz = lax.axis_size("x"), lax.axis_size("z")
     nsec = 2 * nx
@@ -203,8 +203,8 @@
     def first_term():
         local[3].wait()
         await_bytes(hall.at[pl.ds(0, nsec - 1)], st_r.at[3])
-        gsum[0] = jnp.dot(hall[nsec - 1], og[...].reshape(tok, width), preferred_element_type=F32)
-        gsum[1] = jnp.zeros((fb, width), F32)
+        go_out[...] = jnp.dot(hall[nsec - 1], og[...].reshape(tok, width), preferred_element_type=F32)
+        gi_out[...] = jnp.zeros((fb, width), F32)
         for j in range(nsec):
             xs[nsec - 1, j] = og[z, :, pl.ds(pl.multiple_of(ylo * fe + j * LANES, LANES), LANES)]
 
@@ -226,19 +226,22 @@
         return (((t * 2 + core_) * nx + x_) * 2 + ylo_) * nz + z_
 
     def spread_z(t):
-        src = xs.at[t - 1 if isinstance(t, int) and t > 0 else lax.rem(t + nsec, nsec + 1), sec]
+        src = xs.at[nsec if isinstance(t, int) and t == 0 else t - 1, sec]
         dst = up.at[slot(t, core, x, ylo, z)]
 
-        def to(d, c):
+        def both(d):
+            send(src, dst, uz_s.at[0], uz_r.at[t], dev(z_=zat(d), y_=partner))
             send(src, dst, uz_s.at[0], uz_r.at[t], dev(z_=zat(d)))
+
+        both(nz // 2)
+
+        def pair(i, c):
+            both(nz // 2 - i)
+            both(nz // 2 + i)
             return c
 
-        def to_partner(d, c):
-            send(src, dst, uz_s.at[0], uz_r.at[t], dev(z_=zat(d), y_=partner))
-            return c
-
-        lax.fori_loop(1, nz, to, 0)
-        lax.fori_loop(0, nz, to_partner, 0)
+        lax.fori_loop(1, nz // 2, pair, 0)
+        send(src, dst, uz_s.at[0], uz_r.at[t], dev(y_=partner))
         dst[...] = src[...]
 
     def await_z(t):
@@ -260,11 +263,7 @@
     def write_out(t):
         for l in range(2):
             for k in range(nsec):
-                pltpu.make_async_copy(
-                    up.at[pl.ds(slot(t, k % 2, k // 2, l), nz)],
-                    ig_out.at[:, :, pl.ds(l * fe + k * LANES, LANES)],
-                    o_s.at[0],
-                ).start()
+                ig_out[:, :, l * fe + k * LANES:l * fe + (k + 1) * LANES] = up[pl.ds(slot(t, k % 2, k // 2, l), nz)]
 
     def out_term(t):
         await_bytes(up.at[pl.ds(0, nx * block)], ud_r.at[t])
@@ -273,7 +272,7 @@
             rhs = jnp.concatenate(
                 [up[pl.ds(slot(t, k % 2, k // 2, l), nz)].reshape(tok, LANES) for k in range(nsec)], axis=1
             )
-            gsum[0, :, l * fe:(l + 1) * fe] += jnp.dot(rows, rhs, preferred_element_type=F32)
+            go_out[:, l * fe:(l + 1) * fe] += jnp.dot(rows, rhs, preferred_element_type=F32)
 
         @pl.when(sec == t)
         def _():
@@ -291,10 +290,9 @@
         await_bytes(gz.at[pl.ds(0, nz - 1)], g_r.at[t])
         gt[...] = jnp.swapaxes(gz[pl.ds(t * nz, nz)].astype(F32).reshape(tok, LANES), 0, 1)
         rows = gt[pl.ds(pl.multiple_of(lax.rem(z, per_tile) * fb, fb), fb), :].astype(BF16)
-        gsum[1] += jnp.dot(rows, li[lax.rem(t, 2), t // 2], preferred_element_type=F32)
-
-    def application(i, carry):
-        s = nsec - 1 - i
+        gi_out[...] += jnp.dot(rows, li[lax.rem(t, 2), t // 2], preferred_element_type=F32)
+
+    def application(s, final):
         with scope("a_mm"):
             upper = xs[s]
             lhs = jnp.concatenate([upper[j] for j in range(nsec)], axis=1)
@@ -313,8 +311,6 @@
             def _():
                 spread_x(s + 2)
 
-            @pl.when(s <= nsec - 3)
-            def _():
                 @pl.when(s == nsec - 3)
                 def _():
                     await_bytes(li.at[0], li_r.at[4])
@@ -338,9 +334,16 @@
                 g.append(g_tile)
             g = jnp.concatenate(g, axis=1)
             w_in = wbuf[0].reshape(2 * nz * fb, fe)
-            b_buf[s * nsec + sec] = jnp.dot(g, w_in, preferred_element_type=F32).astype(BF16)
-        for dx, dc in sec_order:
-            send(b_buf.at[s * nsec + sec], b_buf.at[s * nsec + sec], ph_s.at[1, s], ph_r.at[1, s], dev(sec_=peer(dx, dc)))
+            part = jnp.dot(g, w_in, preferred_element_type=F32).astype(BF16)
+            for j in range(nsec):
+                b_buf[s, sec, j] = part[:, j * LANES:(j + 1) * LANES]
+        if final:
+            for dx, dc in sec_order:
+                to = peer(dx, dc)
+                send(b_buf.at[s, sec, to], b_buf.at[s, sec, to], ph_s.at[1, s], ph_r.at[1, s], dev(sec_=to))
+        else:
+            for dx, dc in sec_order:
+                send(b_buf.at[s, sec], b_buf.at[s, sec], ph_s.at[1, s], ph_r.at[1, s], dev(sec_=peer(dx, dc)))
 
         with scope("bg_b"):
             spread_g(s)
@@ -350,16 +353,23 @@
                 spread_core(s + 2)
 
         with scope("wait_b"):
-            await_bytes(b_buf.at[pl.ds(0, nsec - 1)], ph_r.at[1, s])
+            if final:
+                await_bytes(b_buf.at[0, 0, pl.ds(0, nsec - 1)], ph_r.at[1, s])
+            else:
+                await_bytes(b_buf.at[0, pl.ds(0, nsec - 1)], ph_r.at[1, s])
         with scope("sum_b"):
-            for j in range(nsec):
-                total = upper[j].astype(F32)
+            for j in [sec] if final else range(nsec):
+                total = xs[s, j].astype(F32)
                 for k in range(nsec):
-                    total = total + b_buf[s * nsec + k, :, j * LANES:(j + 1) * LANES].astype(F32)
-                xs[lax.rem(s + nsec, nsec + 1), j] = total.astype(BF16)
+                    total = total + b_buf[s, k, j].astype(F32)
+                xs[nsec if final else s - 1, j] = total.astype(BF16)
+
+    def step(i, carry):
+        application(nsec - 1 - i, False)
         return carry
 
-    lax.fori_loop(0, nsec, application, 0)
+    lax.fori_loop(0, nsec - 1, step, 0)
+    application(0, True)
 
     with scope("t_z0"):
         spread_z(0)
@@ -370,27 +380,36 @@
         out_term(2)
     with scope("t_in0"):
         in_term(0)
-        outs = [pltpu.make_async_copy(gsum.at[1], gi_out, o_s.at[1])]
-        outs[0].start()
     with scope("t_core1"):
         spread_core(1)
     with scope("t_z0w"):
         await_z(0)
 
+    def columns(l):
+        return pl.ds(pl.multiple_of(l * fe + sec * LANES, LANES), LANES)
+
     @pl.when(sec != 0)
     def _():
-        src = up.at[pl.ds(slot(0, core, x), block)]
-        send(src, src, ux_s.at[1], ux_r.at[0], dev(sec_=0))
+        for l in range(2):
+            send(
+                up.at[pl.ds(slot(0, core, x, l), nz)],
+                ig_out.at[:, :, columns(l)],
+                ux_s.at[1],
+                ux_r.at[0],
+                dev(sec_=0),
+            )
+
+    @pl.when(sec == 0)
+    def _():
+        for l in range(2):
+            ig_out[:, :, l * fe:l * fe + LANES] = up[pl.ds(slot(0, 0, 0, l), nz)]
 
     with scope("t_out1"):
         out_term(1)
-        outs.append(pltpu.make_async_copy(gsum.at[0], go_out, o_s.at[2]))
-        outs[1].start()
     with scope("t_x0w"):
         @pl.when(sec == 0)
         def _():
             await_bytes(up.at[pl.ds(0, (nsec - 1) * block)], ux_r.at[0])
-            write_out(0)
 
     with scope("drain"):
         await_bytes(pa_all.at[pl.ds(0, nz - 1)], st_s.at[0])
@@ -410,10 +429,12 @@
 
         def sent(s, c):
             await_bytes(a_buf.at[0, pl.ds(0, 3)], ph_s.at[0, s])
-            await_bytes(b_buf.at[pl.ds(0, nsec - 1)], ph_s.at[1, s])
+            await_bytes(b_buf.at[0, pl.ds(0, nsec - 1)], ph_s.at[1, s])
             return c
 
-        lax.fori_loop(0, nsec, sent, 0)
+        lax.fori_loop(1, nsec, sent, 0)
+        await_bytes(a_buf.at[0, pl.ds(0, 3)], ph_s.at[0, 0])
+        await_bytes(b_buf.at[0, 0, pl.ds(0, nsec - 1)], ph_s.at[1, 0])
         await_bytes(gz.at[pl.ds(0, nsec * (nz - 1))], g_s.at[0])
         await_bytes(up.at[pl.ds(0, nsec * (2 * nz - 1))], uz_s.at[0])
         await_bytes(up.at[pl.ds(0, (nsec - 1) * (nx - 1) * block)], ux_s.at[0])
@@ -423,9 +444,13 @@
         def _():
             await_bytes(up.at[pl.ds(0, block)], ux_s.at[1])
 
-        for cp in outs:
-            cp.wait()
-        await_bytes(up.at[pl.ds(0, nsec * block)], o_s.at[0])
+
+def finish(ig, gi, go, ig_out, gi_out, go_out, sems):
+    copies = [pltpu.make_async_copy(src, dst, sems.at[k]) for k, (src, dst) in enumerate(((ig, ig_out), (gi, gi_out), (go, go_out)))]
+    for cp in copies:
+        cp.start()
+    for cp in copies:
+        cp.wait()
 
 
 def body(layer_inputs, pre_act, out_grad, w_in, w_out):
@@ -452,12 +477,11 @@
         vmem((nz, 8, width), BF16),
         vmem((nsec + 1, nsec, 8, LANES), BF16),
         vmem((nsec, 4, 8, 2 * nz * fb), BF16),
-        vmem((nsec * nsec, 8, fe), BF16),
+        vmem((nsec, nsec, nsec, 8, LANES), BF16),
         vmem((nsec, 2 * tiles, 8, LANES), BF16),
         vmem((nsec * nz, 8, LANES), BF16),
         vmem((LANES, tok), F32),
         vmem((nsec * nsec * 2 * nz, 8, LANES), BF16),
-        vmem((2, fb, width), F32),
         dma((5,)),
         dma((2,)), dma((2,)),
         dma((2,)), dma((2, half, 2, 2)),
@@ -468,30 +492,39 @@
         dma((1,)), dma((nsec,)),
         dma((2,)), dma((nsec,)),
         dma((1,)), dma((nsec,)),
-        dma((3,)),
     ]
-    any_ = pl.BlockSpec(memory_space=pltpu.HBM)
-    ig, gi, go = pl.pallas_call(
-        kernel,
-        out_shape=(
-            jax.ShapeDtypeStruct((nz, 8, width), BF16),
-            jax.ShapeDtypeStruct((fb, width), F32),
-            jax.ShapeDtypeStruct((fb, width), F32),
-        ),
-        in_specs=[any_] * 5,
-        out_specs=(any_,) * 3,
-        scratch_shapes=scratch,
-        name="chain",
-        compiler_params=pltpu.CompilerParams(
-            collective_id=0, has_side_effects=True, vmem_limit_bytes=67043328
-        ),
-    )(
+    hbm, on_chip = pl.BlockSpec(memory_space=pltpu.HBM), pl.BlockSpec(memory_space=pltpu.VMEM)
+    shapes = (
+        jax.ShapeDtypeStruct((nz, 8, width), BF16),
+        jax.ShapeDtypeStruct((fb, width), F32),
+        jax.ShapeDtypeStruct((fb, width), F32),
+    )
+    operands = (
         layer_inputs.reshape(tok, width),
         pre_act.reshape(nz, 8, hid),
         out_grad.reshape(nz, 8, width),
         w_in.reshape(fb, width),
         w_out.reshape(fb, width),
     )
+    results = pl.pallas_call(
+        kernel,
+        out_shape=shapes,
+        in_specs=[hbm] * 5,
+        out_specs=(on_chip,) * 3,
+        scratch_shapes=scratch,
+        name="chain",
+        compiler_params=pltpu.CompilerParams(
+            collective_id=0, has_side_effects=True, vmem_limit_bytes=32 * 1024 * 1024
+        ),
+    )(*(pltpu.with_memory_space_constraint(v, pltpu.HBM) for v in operands))
+    ig, gi, go = pl.pallas_call(
+        finish,
+        out_shape=shapes,
+        in_specs=[on_chip] * 3,
+        out_specs=(hbm,) * 3,
+        scratch_shapes=[dma((3,))],
+        name="finish",
+    )(*(pltpu.with_memory_space_constraint(v, pltpu.VMEM) for v in results))
     return (
         ig.reshape(1, tok, width),
         gi.reshape(1, 1, fb, width),

time: 149 us -> 145 us (0.973)
  local copies, waits for them, and re-layouts: 3.67 us -> 0 us
    unnamed x7 -> x0, local copies, waits for them, and re-layouts: 3.67 us -> none
    pallas_call x1 -> x2, Pallas kernels: 144 us -> 144 us  [the longest x1 143 us: body(): pl.pallas_call(kernel, out_shape=shapes, in_specs=[hbm] * 5, out_specs=(o...]
where the time goes in v1:
time: 145 us; the launch traced here: 144 us
  Pallas kernels  144 us (99%)
    pallas_call x1, Pallas kernels, body(): pl.pallas_call(kernel, out_shape=shapes, in_specs=[hbm] * 5, out_specs=(o...  143 us

profile of v1, /device:TPU:24, one launch (start us, length us, event | category | flops | bytes accessed | tf_op | source)
XLA Modules:
  0.0 144.2 jit_solution(4249387881155820023)
XLA Ops:
  0.6 142.6 %chain.1 = (bf16[16,8,2048]{2,1,0:T(8,128)(2,1)S(1)}, f32[32,2048]{1,0:T(8,128)S(1)}, f32[32,2048]{1,0:T(8,128)S(1)}) custom-call(bf16[128,2048]{1,0:T(8,128)(2,1)} %bitcast.8, bf16[16,8,256]{2,1,0:T(8,128)(2,1)} %bitcast.12, bf16[16,8,2048]{2,1,0:T(8,128)(2,1)} %bitcast.9, bf16[32,2048]{1,0:T(8,128)(2,1)} %bitcast.10, bf16[32,2048]{1,0:T(8,128)(2,1)} %bitcast.11), custom_call_target="tpu_custom_call" | custom-call | tf_op jit(solution)/shard_map/chain/pallas_call | solution.py:509
  143.2 1.0 finish.1

commit v2 on v1

--- a/solution.py
+++ b/solution.py
@@ -28,9 +28,10 @@
 def kernel(
     li_hbm, pa_hbm, og_hbm, wi_hbm, wo_hbm,
     ig_out, gi_out, go_out,
-    wbuf, pa, pa_all, pb, pc, slope, h_t, hall, li, og,
+    wbuf, pa, pa_all, pb, pc, slope, pa_t, pre_t, hall, li, og,
+    a_top, b_top, r_top, q_top, z_top, g_top,
     xs, a_buf, b_buf, gbuf, gz, gt, up,
-    lsem, wx_s, wx_r, wz_s, wz_r, st_s, st_r, ph_s, ph_r, li_s, li_r,
+    lsem, wx_s, wx_r, wz_s, wz_r, st_s, st_r, top_s, top_r, ph_s, ph_r, li_s, li_r,
     g_s, g_r, uz_s, uz_r, ux_s, ux_r, ud_s, ud_r,
 ):
     nx, nz = lax.axis_size("x"), lax.axis_size("z")
@@ -105,7 +106,7 @@
         greeted += 1
     local[0].wait()
     v = pa[...].astype(F32).reshape(tok, nsec * fb)
-    h_t[...] = jnp.swapaxes(v * gelu_parts(v)[0], 0, 1).astype(BF16).reshape(nsec, fb, tok)
+    pa_t[...] = jnp.swapaxes(v, 0, 1).astype(BF16).reshape(nsec, fb, tok)
     with scope("barrier"):
         pl.semaphore_wait(barrier, greeted)
 
@@ -115,9 +116,10 @@
         send(w_hbm[m].at[:, theirs], wbuf.at[m, ylo, z], wx_s.at[m], wx_r.at[m], dev(y_=partner))
         for m in range(2)
     ]
+    top = nsec - 1
     for d in range(1, nsec):
-        send(h_t.at[sat(d)], hall.at[sec], st_s.at[3], st_r.at[3], dev(sec_=sat(d)))
-    hall[sec] = h_t[sec]
+        send(pa_t.at[sat(d)], pre_t.at[sec], st_s.at[3], st_r.at[3], dev(sec_=sat(d)))
+    pre_t[sec] = pa_t[sec]
     pa_all[z] = pa[z]
 
     half = nz // 2
@@ -200,15 +202,89 @@
             await_bytes(li.at[0, 0, hi], li_r.at[3])
         send(li.at[core], li.at[core], li_s.at[4], li_r.at[4], dev(sec_=peer(0, 1)))
 
+    def slot(t, core_, x_, ylo_=0, z_=0):
+        return (((t * 2 + core_) * nx + x_) * 2 + ylo_) * nz + z_
+
+    def spread_z(t):
+        src = xs.at[nsec if isinstance(t, int) and t == 0 else t - 1, sec]
+        dst = up.at[slot(t, core, x, ylo, z)]
+
+        def both(d):
+            send(src, dst, uz_s.at[0], uz_r.at[t], dev(z_=zat(d), y_=partner))
+            send(src, dst, uz_s.at[0], uz_r.at[t], dev(z_=zat(d)))
+
+        both(nz // 2)
+
+        def pair(i, c):
+            both(nz // 2 - i)
+            both(nz // 2 + i)
+            return c
+
+        lax.fori_loop(1, nz // 2, pair, 0)
+        send(src, dst, uz_s.at[0], uz_r.at[t], dev(y_=partner))
+        dst[...] = src[...]
+
+    def top_first():
+        local[3].wait()
+        rows = wbuf[1, :, z].reshape(2 * fb, fe)
+        a_top[y] = lax.dot_general(
+            rows, og[:, :, mine].reshape(tok, fe), (((1,), (1,)), ((), ())), preferred_element_type=F32
+        ).astype(BF16)
+        for d in y_order:
+            send(a_top.at[y], a_top.at[y], top_s.at[0], top_r.at[0], dev(y_=yat(d)))
+        await_bytes(pre_t.at[pl.ds(0, nsec - 1)], st_r.at[3])
+        send(pre_t.at[top], pre_t.at[nsec], st_s.at[4], st_r.at[4], dev(y_=partner))
+
+    def top_second():
+        await_bytes(pre_t.at[0], st_r.at[4])
+        own, theirs_ = pre_t[top].astype(F32), pre_t[nsec].astype(F32)
+        v = jnp.concatenate([jnp.where(ylo == 0, own, theirs_), jnp.where(ylo == 0, theirs_, own)], axis=0)
+        cdf, dens = gelu_parts(v)
+        await_bytes(a_top.at[pl.ds(0, 3)], top_r.at[0])
+        back = a_top[0].astype(F32)
+        for k in range(1, 4):
+            back = back + a_top[k].astype(F32)
+        g = (back * (cdf + v * dens)).astype(BF16)
+        g_top[...] = jnp.where(ylo == 0, g[:fb], g[fb:])
+        rows = jnp.swapaxes(g.astype(F32), 0, 1).astype(BF16)
+        part = jnp.dot(rows, wbuf[0, :, z].reshape(2 * fb, fe), preferred_element_type=F32).astype(BF16)
+        for j in range(nsec):
+            b_top[j] = part[:, j * LANES:(j + 1) * LANES].reshape(nz, 8, LANES)
+        for dx, dc in sec_order:
+            to = peer(dx, dc)
+            send(b_top.at[to], r_top.at[sec], top_s.at[1], top_r.at[1], dev(sec_=to))
+        r_top[sec] = b_top[sec]
+
+    def top_third():
+        await_bytes(r_top.at[pl.ds(0, nsec - 1)], top_r.at[1])
+        total = r_top[0].astype(F32)
+        for k in range(1, nsec):
+            total = total + r_top[k].astype(F32)
+        q_top[...] = total.astype(BF16)
+        for d in sorted(range(1, nz), key=lambda d: -min(d, nz - d)):
+            send(q_top.at[zat(d)], z_top.at[z], top_s.at[2], top_r.at[2], dev(z_=zat(d)))
+        z_top[z] = q_top[z]
+
+    def top_fourth():
+        await_bytes(z_top.at[pl.ds(0, nz - 1)], top_r.at[2])
+        total = og[z, :, pl.ds(pl.multiple_of(ylo * fe + sec * LANES, LANES), LANES)].astype(F32)
+        for k in range(nz):
+            total = total + z_top[k].astype(F32)
+        src = xs.at[top - 1, sec]
+        src[...] = total.astype(BF16)
+        for dx, dc in sec_order:
+            send(src, src, top_s.at[3], top_r.at[3], dev(sec_=peer(dx, dc)))
+
     def first_term():
-        local[3].wait()
-        await_bytes(hall.at[pl.ds(0, nsec - 1)], st_r.at[3])
-        go_out[...] = jnp.dot(hall[nsec - 1], og[...].reshape(tok, width), preferred_element_type=F32)
-        gi_out[...] = jnp.zeros((fb, width), F32)
-        for j in range(nsec):
-            xs[nsec - 1, j] = og[z, :, pl.ds(pl.multiple_of(ylo * fe + j * LANES, LANES), LANES)]
-
-    plan = [(2, first_term), (3, stage_b), (3, li_first), (5, stage_c), (6, stage_d), (6, li_second)]
+        for s in range(nsec):
+            v = pre_t[s].astype(F32)
+            hall[s] = (v * gelu_parts(v)[0]).astype(BF16)
+        go_out[...] = jnp.dot(hall[top], og[...].reshape(tok, width), preferred_element_type=F32)
+
+    plan = [
+        (1, top_first), (2, top_second), (3, stage_b), (3, li_first), (4, top_third), (5, stage_c), (5, first_term),
+        (6, stage_d), (6, li_second), (7, top_fourth),
+    ]
     for k in range(1, half + 1):
         with scope(f"hop{k}"):
             hop(k)
@@ -220,29 +296,9 @@
         for l in range(2):
             for way in range(2):
                 await_bytes(wbuf.at[way, l, 0], wz_r.at[way, half - 1, way, l])
+    with scope("top_end"):
+        await_bytes(xs.at[0, pl.ds(0, nsec - 1)], top_r.at[3])
     li_third()
-
-    def slot(t, core_, x_, ylo_=0, z_=0):
-        return (((t * 2 + core_) * nx + x_) * 2 + ylo_) * nz + z_
-
-    def spread_z(t):
-        src = xs.at[nsec if isinstance(t, int) and t == 0 else t - 1, sec]
-        dst = up.at[slot(t, core, x, ylo, z)]
-
-        def both(d):
-            send(src, dst, uz_s.at[0], uz_r.at[t], dev(z_=zat(d), y_=partner))
-            send(src, dst, uz_s.at[0], uz_r.at[t], dev(z_=zat(d)))
-
-        both(nz // 2)
-
-        def pair(i, c):
-            both(nz // 2 - i)
-            both(nz // 2 + i)
-            return c
-
-        lax.fori_loop(1, nz // 2, pair, 0)
-        send(src, dst, uz_s.at[0], uz_r.at[t], dev(y_=partner))
-        dst[...] = src[...]
 
     def await_z(t):
         await_bytes(up.at[pl.ds(0, 2 * nz - 1)], uz_r.at[t])
@@ -303,22 +359,20 @@
             send(a_buf.at[s, y], a_buf.at[s, y], ph_s.at[0, s], ph_r.at[0, s], dev(y_=yat(d)))
 
         with scope("bg_a"):
-            @pl.when(s <= nsec - 2)
-            def _():
-                spread_z(s + 1)
-
-            @pl.when(s <= nsec - 3)
+            spread_z(s + 1)
+
+            @pl.when(s <= top - 2)
             def _():
                 spread_x(s + 2)
 
-                @pl.when(s == nsec - 3)
-                def _():
-                    await_bytes(li.at[0], li_r.at[4])
-
+            @pl.when(s == top - 2)
+            def _():
+                await_bytes(li.at[0], li_r.at[4])
+                gi_out[...] = jnp.dot(g_top[...], li[top % 2, top // 2], preferred_element_type=F32)
+
+            @pl.when(s <= top - 3)
+            def _():
                 in_term(s + 2)
-
-            @pl.when(s <= nsec - 4)
-            def _():
                 out_term(s + 3)
 
         with scope("wait_a"):
@@ -348,7 +402,7 @@
         with scope("bg_b"):
             spread_g(s)
 
-            @pl.when(s <= nsec - 3)
+            @pl.when(s <= top - 2)
             def _():
                 spread_core(s + 2)
 
@@ -365,10 +419,10 @@
                 xs[nsec if final else s - 1, j] = total.astype(BF16)
 
     def step(i, carry):
-        application(nsec - 1 - i, False)
+        application(top - 1 - i, False)
         return carry
 
-    lax.fori_loop(0, nsec - 1, step, 0)
+    lax.fori_loop(0, top - 1, step, 0)
     application(0, True)
 
     with scope("t_z0"):
@@ -415,7 +469,12 @@
         await_bytes(pa_all.at[pl.ds(0, nz - 1)], st_s.at[0])
         await_bytes(pc.at[0, pl.ds(0, nsec - 1)], st_s.at[1])
         await_bytes(pc.at[0], st_s.at[2])
-        await_bytes(hall.at[pl.ds(0, nsec - 1)], st_s.at[3])
+        await_bytes(pre_t.at[pl.ds(0, nsec - 1)], st_s.at[3])
+        await_bytes(pre_t.at[0], st_s.at[4])
+        await_bytes(a_top.at[pl.ds(0, 3)], top_s.at[0])
+        await_bytes(r_top.at[pl.ds(0, nsec - 1)], top_s.at[1])
+        await_bytes(z_top.at[pl.ds(0, nz - 1)], top_s.at[2])
+        await_bytes(xs.at[0, pl.ds(0, nsec - 1)], top_s.at[3])
         for cp in swaps:
             cp.wait_send()
         for way in range(2):
@@ -432,10 +491,10 @@
             await_bytes(b_buf.at[0, pl.ds(0, nsec - 1)], ph_s.at[1, s])
             return c
 
-        lax.fori_loop(1, nsec, sent, 0)
+        lax.fori_loop(1, top, sent, 0)
         await_bytes(a_buf.at[0, pl.ds(0, 3)], ph_s.at[0, 0])
         await_bytes(b_buf.at[0, 0, pl.ds(0, nsec - 1)], ph_s.at[1, 0])
-        await_bytes(gz.at[pl.ds(0, nsec * (nz - 1))], g_s.at[0])
+        await_bytes(gz.at[pl.ds(0, top * (nz - 1))], g_s.at[0])
         await_bytes(up.at[pl.ds(0, nsec * (2 * nz - 1))], uz_s.at[0])
         await_bytes(up.at[pl.ds(0, (nsec - 1) * (nx - 1) * block)], ux_s.at[0])
         await_bytes(up.at[pl.ds(0, (nsec - 1) * nx * block)], ud_s.at[0])
@@ -472,9 +531,16 @@
         vmem((2, nsec, tiles, 8, LANES), BF16),
         vmem((nsec, 2 * tiles, 8, LANES), F32),
         vmem((nsec, fb, tok), BF16),
+        vmem((nsec + 1, fb, tok), BF16),
         vmem((nsec, fb, tok), BF16),
         vmem((2, nx, tok, width), BF16),
         vmem((nz, 8, width), BF16),
+        vmem((4, 2 * fb, tok), BF16),
+        vmem((nsec, nz, 8, LANES), BF16),
+        vmem((nsec, nz, 8, LANES), BF16),
+        vmem((nz, 8, LANES), BF16),
+        vmem((nz, 8, LANES), BF16),
+        vmem((fb, tok), BF16),
         vmem((nsec + 1, nsec, 8, LANES), BF16),
         vmem((nsec, 4, 8, 2 * nz * fb), BF16),
         vmem((nsec, nsec, nsec, 8, LANES), BF16),
@@ -485,6 +551,7 @@
         dma((5,)),
         dma((2,)), dma((2,)),
         dma((2,)), dma((2, half, 2, 2)),
+        dma((5,)), dma((5,)),
         dma((4,)), dma((4,)),
         dma((2, nsec)), dma((2, nsec)),
         dma((5,)), dma((5,)),

time: 145 us -> 139 us (0.959)
  Pallas kernels: 144 us -> 137 us
    pallas_call x1, Pallas kernels: 143 us -> 136 us  [body(): pl.pallas_call(kernel, out_shape=shapes, in_specs=[hbm] * 5, out_specs=(o...]
where the time goes in v2:
time: 139 us; the launch traced here: 138 us
  Pallas kernels  137 us (99%)
    pallas_call x1, Pallas kernels, body(): pl.pallas_call(kernel, out_shape=shapes, in_specs=[hbm] * 5, out_specs=(o...  136 us

profile of v2, /device:TPU:24, one launch (start us, length us, event | category | flops | bytes accessed | tf_op | source)
XLA Modules:
  0.0 137.6 jit_solution(6141256549707568576)
XLA Ops:
  0.6 136.0 %chain.1 = (bf16[16,8,2048]{2,1,0:T(8,128)(2,1)S(1)}, f32[32,2048]{1,0:T(8,128)S(1)}, f32[32,2048]{1,0:T(8,128)S(1)}) custom-call(bf16[128,2048]{1,0:T(8,128)(2,1)} %bitcast.8, bf16[16,8,256]{2,1,0:T(8,128)(2,1)} %bitcast.12, bf16[16,8,2048]{2,1,0:T(8,128)(2,1)} %bitcast.9, bf16[32,2048]{1,0:T(8,128)(2,1)} %bitcast.10, bf16[32,2048]{1,0:T(8,128)(2,1)} %bitcast.11), custom_call_target="tpu_custom_call" | custom-call | tf_op jit(solution)/shard_map/chain/pallas_call | solution.py:576
  136.6 1.0 finish.1

commit v3 on v1

v3 whole, which is shorter than its diff:
```python
import contextlib

import jax
import jax.numpy as jnp
from jax import lax
from jax.experimental import pallas as pl
from jax.experimental.pallas import tpu as pltpu
from jax.sharding import Mesh
from jax.sharding import PartitionSpec as P

AXES = ("x", "core", "z", "ylo", "yhi")
MESH_ID = pl.DeviceIdType.MESH
BF16, F32 = jnp.bfloat16, jnp.float32
LANES = 128
PROFILE = False


def scope(name):
    return jax.named_scope(name) if PROFILE else contextlib.nullcontext()


def gelu_parts(v):
    cdf = 0.5 * (1.0 + lax.erf(v * 0.7071067811865476))
    dens = jnp.exp(-0.5 * v * v) * 0.3989422804014327
    return cdf, dens


def kernel(
    li_hbm, pa_hbm, og_hbm, wi_hbm, wo_hbm,
    ig_out, gi_out, go_out,
    wbuf, pa, pa_all, pb, pc, slope, pa_t, pre_t, pre_top, hall, li, og,
    a_top, b_top, r_top, q_top, z_top, g_top, g_pass,
    w_t, xs, a_buf, b_buf, a_acc, b_acc, gbuf, gz, gt, up, x_end,
    lsem, wx_s, wx_r, wd_s, wd_r, wz_s, wz_r, st_s, st_r, pt_s, pt_r, top_s, top_r, ph_s, ph_r, li_s, li_r,
    g_s, g_r, uz_s, uz_r, ux_s, ux_r, ud_s, ud_r, go,
):
    nx, nz = lax.axis_size("x"), lax.axis_size("z")
    nsec = 2 * nx
    top = nsec - 1
    fb, width = wi_hbm.shape
    fe = width // 2
    tok = nz * 8
    tiles = nz * fb // LANES
    per_tile = LANES // fb
    x, core, z = lax.axis_index("x"), lax.axis_index("core"), lax.axis_index("z")
    ylo, yhi = lax.axis_index("ylo"), lax.axis_index("yhi")
    sec = x * 2 + core
    y = yhi * 2 + ylo
    other = 1 - ylo
    partner = yhi * 2 + other

    def dev(x_=None, core_=None, z_=None, y_=None):
        y_ = y if y_ is None else y_
        return (
            x if x_ is None else x_,
            core if core_ is None else core_,
            z if z_ is None else z_,
            lax.rem(y_, 2),
            y_ // 2,
        )

    def send(src, dst, ssem, rsem, to):
        cp = pltpu.make_async_remote_copy(
            src_ref=src, dst_ref=dst, send_sem=ssem, recv_sem=rsem, device_id=to, device_id_type=MESH_ID
        )
        cp.start()
        return cp

    def await_bytes(ref, sem):
        pltpu.make_async_copy(ref, ref, sem).wait()

    def zat(d):
        return lax.rem(z + d + nz, nz)

    def xat(d):
        return lax.rem(x + d + nx, nx)

    def yat(d):
        return lax.rem(y + d, 4)

    y_order = (2, 1, 3)
    x_order = sorted(range(1, nx), key=lambda d: -min(d, nx - d))
    z_order = sorted(range(1, nz), key=lambda d: -min(d, nz - d))
    sections = [(d, False) for d in x_order] + [(d, True) for d in x_order] + [(0, True)]

    def peer(d, cross):
        return xat(d), (1 - core if cross else core)

    mine = pl.ds(pl.multiple_of(ylo * fe, LANES), fe)
    theirs = pl.ds(pl.multiple_of(other * fe, LANES), fe)

    w_hbm = (wi_hbm, wo_hbm)
    pa_in = pltpu.make_async_copy(pa_hbm, pa, lsem.at[0])
    w_in_ = [pltpu.make_async_copy(w_hbm[m].at[:, mine], wbuf.at[m, ylo, 1, z], lsem.at[1 + m]) for m in range(2)]
    og_in = pltpu.make_async_copy(og_hbm, og, lsem.at[3])
    li_in = pltpu.make_async_copy(li_hbm, li.at[core, x], lsem.at[4])
    pa_in.start()

    @pl.when(core == 1)
    def _():
        for cp in w_in_:
            cp.start()

    og_in.start()
    li_in.start()

    barrier = pltpu.get_barrier_semaphore()
    greeted = [dev(z_=zat(d)) for d in range(1, nz)] + [dev(*peer(*p)) for p in sections]
    greeted += [dev(y_=yat(d)) for d in range(1, 4)] + [dev(core_=1 - core, y_=partner)]
    for to in greeted:
        pl.semaphore_signal(barrier, inc=1, device_id=to, device_id_type=MESH_ID)
    pa_in.wait()
    v = pa[...].astype(F32).reshape(tok, nsec * fb)
    pa_t[...] = jnp.swapaxes(v, 0, 1).astype(BF16).reshape(nsec, fb, tok)
    with scope("barrier"):
        pl.semaphore_wait(barrier, len(greeted))

    for d in z_order:
        send(pa.at[zat(d)], pa_all.at[z], st_s.at[0], st_r.at[0], dev(z_=zat(d)))
    pa_all[z] = pa[z]

    swaps = [
        send(w_hbm[m].at[:, theirs], wbuf.at[m, ylo, core, z], wx_s.at[m], wx_r.at[core, m], dev(core_=1, y_=partner))
        for m in range(2)
    ]

    @pl.when(core == 0)
    def _():
        for m in range(2):
            send(w_hbm[m].at[:, mine], wbuf.at[m, ylo, 0, z], wd_s.at[m], wd_r.at[m], dev(core_=1))

    for p in sections:
        to = peer(*p)
        send(pa_t.at[to[0] * 2 + to[1]], pre_t.at[sec], st_s.at[3], st_r.at[3], dev(*to))
    pre_t[sec] = pa_t[sec]

    def spread_pre():
        await_bytes(pre_t.at[pl.ds(0, nsec - 1)], st_r.at[3])
        dst = pre_top.at[ylo, core]
        send(pre_t.at[top], dst, pt_s.at[0], pt_r.at[0], dev(core_=1, y_=partner))

        @pl.when(core == 0)
        def _():
            send(pre_t.at[top], dst, pt_s.at[1], pt_r.at[0], dev(core_=1))

        @pl.when(core == 1)
        def _():
            dst[...] = pre_t[top]

    def stage_b():
        await_bytes(pa_all.at[pl.ds(0, nz - 1)], st_r.at[0])
        group = lax.broadcasted_iota(jnp.int32, (8, LANES), 1) // fb
        for ct in range(nsec // per_tile):
            for t in range(tiles):
                out = [jnp.zeros((8, LANES), F32)] * per_tile
                for j in range(per_tile):
                    v = pa_all[t * per_tile + j, :, ct * LANES:(ct + 1) * LANES].astype(F32)
                    for k in range(per_tile):
                        shift = (j - k) * fb % LANES
                        r = pltpu.roll(v, shift, 1) if shift else v
                        out[k] = jnp.where(group == j, r, out[k])
                for k in range(per_tile):
                    c = ct * per_tile + k
                    pb[c // 2, c % 2, t] = out[k].astype(BF16)
        dst = pc.at[ylo, sec]
        for d in x_order:
            send(pb.at[xat(d)], dst, st_s.at[1], st_r.at[1], dev(x_=xat(d), core_=1))

        @pl.when(core == 0)
        def _():
            send(pb.at[x], dst, st_s.at[5], st_r.at[1], dev(core_=1))

        @pl.when(core == 1)
        def _():
            dst[...] = pb[x]

    cut = tok // 2
    lo, hi = pl.ds(0, cut), pl.ds(cut, cut)
    ring = nx > 2

    def li_first():
        li_in.wait()
        src = li.at[core, x]
        send(src, src, li_s.at[0], li_r.at[0], dev(x_=xat(1)))
        if ring:
            send(src, src, li_s.at[1], li_r.at[1], dev(x_=xat(-1)))

    def li_second():
        await_bytes(li.at[0, 0], li_r.at[0])
        if ring:
            src = li.at[core, xat(-1), lo]
            send(src, src, li_s.at[2], li_r.at[2], dev(x_=xat(1)))
            await_bytes(li.at[0, 0], li_r.at[1])
            src = li.at[core, xat(1), hi]
            send(src, src, li_s.at[3], li_r.at[3], dev(x_=xat(-1)))

    def li_third():
        if ring:
            await_bytes(li.at[0, 0, lo], li_r.at[2])
            await_bytes(li.at[0, 0, hi], li_r.at[3])
        send(li.at[core], li.at[core], li_s.at[4], li_r.at[4], dev(core_=1 - core))

    def first_out_term():
        for s in range(nsec):
            v = pre_t[s].astype(F32)
            hall[s] = (v * gelu_parts(v)[0]).astype(BF16)
        go_out[...] = jnp.dot(hall[top], og[...].reshape(tok, width), preferred_element_type=F32)

    def first_in_term():
        await_bytes(li.at[0], li_r.at[4])
        gi_out[...] = jnp.dot(g_top[...], li[top % 2, top // 2], preferred_element_type=F32)

    block = 4 * nz

    def slot(t, x_, ylo_=0, z_=0):
        return ((((t * nx + x_) * 2 + ylo_) * nz) + z_) * 2

    def columns(t, x_, l):
        return up[pl.ds(slot(t, x_, l), 2 * nz)].reshape(nz, 2, 8, LANES)

    def out_term(t):
        rows = hall[t - 1]
        for l in range(2):
            parts = []
            for k in range(nx):
                v = columns(t, k, l)
                parts += [v[:, c].reshape(tok, LANES) for c in range(2)]
            go_out[:, l * fe:(l + 1) * fe] += jnp.dot(rows, jnp.concatenate(parts, axis=1), preferred_element_type=F32)

        @pl.when(sec == t)
        def _():
            for l in range(2):
                for k in range(nx):
                    v = columns(t, k, l)
                    for c in range(2):
                        at = l * fe + (2 * k + c) * LANES
                        ig_out[:, :, at:at + LANES] = v[:, c]

    def in_term(t):
        @pl.when(core == 1)
        def _():
            await_bytes(gz.at[pl.ds(0, nz - 1)], g_r.at[t])

        @pl.when(core == 0)
        def _():
            await_bytes(gz.at[pl.ds(0, nz)], g_r.at[t])

        gt[...] = jnp.swapaxes(gz[pl.ds(t * nz, nz)].astype(F32).reshape(tok, LANES), 0, 1)
        rows = gt[pl.ds(pl.multiple_of(lax.rem(z, per_tile) * fb, fb), fb), :].astype(BF16)
        gi_out[...] += jnp.dot(rows, li[lax.rem(t, 2), t // 2], preferred_element_type=F32)

    half = nz // 2
    hu, hn, hj = 2 * nz * fb, fe // 2, nsec // 2

    def hop(k):
        last = k == half
        for which in range(2):
            l = ylo if which == 0 else other
            for m in range(2):
                if k == 1:
                    if which == 0:
                        w_in_[m].wait()
                        await_bytes(wbuf.at[m, 0, 0, 0], wd_r.at[m])
                    else:
                        for c in range(2):
                            await_bytes(wbuf.at[m, 0, 0, 0], wx_r.at[c, m])
                for way, step in ((0, 1), (1, -1)):
                    if k > 1:
                        await_bytes(wbuf.at[m, 0, :, 0], wz_r.at[way, k - 2, m, l])
                    if last and way != m:
                        continue
                    src = wbuf.at[m, l, :, zat(-step * (k - 1))]
                    send(src, src, wz_s.at[way], wz_r.at[way, k - 1, m, l], dev(z_=zat(step)))

    def stage_c():
        await_bytes(pc.at[0, pl.ds(0, nsec - 1)], st_r.at[1])
        send(pc.at[ylo], pc.at[ylo], st_s.at[2], st_r.at[2], dev(y_=partner))

    def stage_d():
        await_bytes(pc.at[0], st_r.at[2])

        def one(s, carry):
            for l in range(2):
                v = pc[l, s].astype(F32)
                cdf, dens = gelu_parts(v)
                slope[s, l] = (cdf + v * dens).reshape(2 * tiles, 8, LANES)
            return carry

        lax.fori_loop(0, top, one, 0)

    def top_first():
        og_in.wait()
        rows = wbuf[1, :, :, z].reshape(4 * fb, fe)
        a_top[y] = lax.dot_general(
            rows, og[:, :, mine].reshape(tok, fe), (((1,), (1,)), ((), ())), preferred_element_type=F32
        ).astype(BF16)
        for d in y_order:
            send(a_top.at[y], a_top.at[y], top_s.at[0], top_r.at[0], dev(y_=yat(d)))
        spread_pre()

    def top_second():
        await_bytes(pre_t.at[pl.ds(0, 3)], pt_r.at[0])
        v = pre_top[...].astype(F32).reshape(4 * fb, tok)
        cdf, dens = gelu_parts(v)
        await_bytes(a_top.at[pl.ds(0, 3)], top_r.at[0])
        back = a_top[0].astype(F32)
        for k in range(1, 4):
            back = back + a_top[k].astype(F32)
        g = (back * (cdf + v * dens)).astype(BF16)
        g_pass[...] = jnp.where(ylo == 0, g[:fb], g[2 * fb:3 * fb])
        send(g_pass, g_top, top_s.at[4], top_r.at[4], dev(core_=0))
        g_top[...] = jnp.where(ylo == 0, g[fb:2 * fb], g[3 * fb:])
        rows = jnp.swapaxes(g.astype(F32), 0, 1).astype(BF16)
        part = jnp.dot(rows, wbuf[0, :, :, z].reshape(4 * fb, fe), preferred_element_type=F32).astype(BF16)
        for j in range(nsec):
            b_top[j // 2, :, j % 2] = part[:, j * LANES:(j + 1) * LANES].reshape(nz, 8, LANES)
        for d in x_order:
            send(b_top.at[xat(d)], r_top.at[x], top_s.at[1], top_r.at[1], dev(x_=xat(d)))
        r_top[x] = b_top[x]

    def top_third():
        await_bytes(r_top.at[pl.ds(0, nx - 1)], top_r.at[1])
        total = r_top[0].astype(F32)
        for k in range(1, nx):
            total = total + r_top[k].astype(F32)
        q_top[...] = total.astype(BF16)
        for d in z_order:
            send(q_top.at[zat(d)], z_top.at[z], top_s.at[2], top_r.at[2], dev(z_=zat(d)))
        z_top[z] = q_top[z]

    own = pl.ds(2 * x, 2)

    def top_fourth():
        await_bytes(z_top.at[pl.ds(0, nz - 1)], top_r.at[2])
        for c in range(2):
            at = pl.multiple_of(ylo * fe + (2 * x + c) * LANES, LANES)
            total = og[z, :, pl.ds(at, LANES)].astype(F32)
            for k in range(nz):
                total = total + z_top[k, c].astype(F32)
            xs[top - 1, 2 * x + c] = total.astype(BF16)
        src = xs.at[top - 1, own]
        for d in x_order:
            send(src, src, top_s.at[3], top_r.at[3], dev(x_=xat(d)))

    def spread_z(t):
        src = xs.at[nsec if isinstance(t, int) and t == 0 else t - 1, own]
        dst = up.at[pl.ds(slot(t, x, ylo, z), 2)]

        def both(d):
            for to in (partner, y):
                send(src, dst, uz_s.at[0], uz_r.at[t], dev(core_=0, z_=zat(d), y_=to))

        both(half)

        def pair(i, c):
            both(half - i)
            both(half + i)
            return c

        lax.fori_loop(1, half, pair, 0)
        both(0)

    def spread_g(t):
        def to(d, c):
            tile = zat(d) // per_tile
            for c_ in range(2):
                send(gbuf.at[t, ylo, c_ * tiles + tile], gz.at[t * nz + z], g_s.at[0], g_r.at[t], dev(core_=c_, z_=zat(d)))
            return c

        lax.fori_loop(1, nz, to, 0)
        tile = z // per_tile
        send(gbuf.at[t, ylo, tile], gz.at[t * nz + z], g_s.at[0], g_r.at[t], dev(core_=0))
        gz[t * nz + z] = gbuf[t, ylo, tiles + tile]

    def turn(away):
        t = lax.rem(z // per_tile + away + tiles, tiles)

        def one(i, c):
            l, c_ = i // 2, lax.rem(i, 2)
            v = wbuf[1, l, c_, pl.ds(t * per_tile, per_tile)].reshape(LANES, fe)
            w_t[l, c_ * tiles + t] = jnp.swapaxes(v, 0, 1)
            return c

        lax.fori_loop(0, 4, one, 0)

    def a_half(s, l, part):
        a_buf[s, l, y] = part.astype(BF16)
        for d in y_order:
            send(a_buf.at[s, l, y], a_buf.at[s, l, y], ph_s.at[0, l, s], ph_r.at[0, l, s], dev(y_=yat(d)))

    def a_part(s, l, n):
        lhs = jnp.concatenate([xs[s, n * hj + j] for j in range(hj)], axis=1)
        w_out = jnp.concatenate([w_t[l, t, n * hn:(n + 1) * hn] for t in range(2 * tiles)], axis=1)
        return jnp.dot(lhs, w_out, preferred_element_type=F32)

    def a_first(s, l):
        lhs = jnp.concatenate([xs[s, j] for j in range(nsec)], axis=1)
        return lax.dot_general(lhs, wbuf[1, l].reshape(hu, fe), (((1,), (1,)), ((), ())), preferred_element_type=F32)

    def release(t):
        pl.semaphore_signal(go.at[t], inc=1, device_id=dev(core_=0), device_id_type=MESH_ID)

    def await_up(t):
        await_bytes(up.at[pl.ds(0, nx * block)], ud_r.at[t])

    def application(s, final):
        with scope("bg_a"):
            @pl.when(s <= top - 2)
            def _():
                release(s + 2)

            spread_z(s + 1)

            @pl.when(s == top - 2)
            def _():
                first_in_term()

            @pl.when(s == top - 1)
            def _():
                turn(tiles // 2)

            @pl.when(s <= top - 3)
            def _():
                in_term(s + 2)
                await_up(s + 3)
                out_term(s + 3)

        for l in range(2):
            with scope(f"wait_a{l}"):
                await_bytes(a_buf.at[s, l, pl.ds(0, 3)], ph_r.at[0, l, s])
            with scope(f"b_mm{l}"):
                back = a_buf[s, l, 0].astype(F32)
                for k in range(1, 4):
                    back = back + a_buf[s, l, k].astype(F32)
                g = []
                for t in range(2 * tiles):
                    g_tile = (back[:, t * LANES:(t + 1) * LANES] * slope[s, l, t]).astype(BF16)
                    gbuf[s, l, t] = g_tile
                    g.append(g_tile)
                g = jnp.concatenate(g, axis=1)
                if l == 0:
                    for n in range(2):
                        w_in = wbuf[0, l, :, :, :, n * hn:(n + 1) * hn].reshape(hu, hn)
                        b_acc[n] = jnp.dot(g, w_in, preferred_element_type=F32)
        for n in range(2):
            w_in = wbuf[0, 1, :, :, :, n * hn:(n + 1) * hn].reshape(hu, hn)
            part = (b_acc[n] + jnp.dot(g, w_in, preferred_element_type=F32)).astype(BF16)
            for j in range(hj):
                b_buf[s, n, x, j] = part[:, j * LANES:(j + 1) * LANES]
            if not final:
                src = b_buf.at[s, n, x]
                for d in x_order:
                    send(src, src, ph_s.at[1, n, s], ph_r.at[1, n, s], dev(x_=xat(d)))
        hx = nx // 2
        if final:
            for d in x_order:
                to = xat(d)
                src = b_buf.at[s, to // hx, x, pl.ds(2 * lax.rem(to, hx), 2)]
                send(src, src, ph_s.at[1, 0, s], ph_r.at[1, 0, s], dev(x_=to))

        with scope("bg_b"):
            spread_g(s)

        if final:
            with scope("wait_b"):
                await_bytes(gz.at[pl.ds(0, 2 * (nx - 1))], ph_r.at[1, 0, s])
            for c in range(2):
                total = xs[s, 2 * x + c].astype(F32)
                for k in range(nx):
                    total = total + b_buf[s, x // hx, k, 2 * lax.rem(x, hx) + c].astype(F32)
                xs[nsec, 2 * x + c] = total.astype(BF16)
            return
        for n in range(2):
            with scope(f"wait_b{n}"):
                await_bytes(b_buf.at[s, n, pl.ds(0, nx - 1)], ph_r.at[1, n, s])
            with scope(f"a_mm{n}"):
                for j in range(hj):
                    total = xs[s, n * hj + j].astype(F32)
                    for k in range(nx):
                        total = total + b_buf[s, n, k, j].astype(F32)
                    xs[s - 1, n * hj + j] = total.astype(BF16)
                if n == 0:
                    for l in range(2):
                        a_acc[l] = a_part(s - 1, l, 0)
        for l in range(2):
            with scope(f"a_last{l}"):
                a_half(s - 1, l, a_acc[l] + a_part(s - 1, l, 1))

    @pl.when(core == 1)
    def _():
        plan = [
            (1, top_first), (2, top_second), (3, stage_b), (3, li_first), (4, top_third), (5, stage_c), (5, first_out_term),
            (6, stage_d), (6, li_second), (7, top_fourth),
        ]
        plan += [(half if d else 5, lambda d=d: turn(d)) for d in (0, -1, 1) if d % tiles != tiles // 2]
        for k in range(1, half + 1):
            with scope(f"hop{k}"):
                hop(k)
            with scope(f"stage{k}"):
                for at, f in plan:
                    if min(at, half) == k:
                        f()
        with scope("gather_end"):
            for l in range(2):
                for way in range(2):
                    await_bytes(wbuf.at[way, 0, :, 0], wz_r.at[way, half - 1, way, l])
        with scope("top_end"):
            await_bytes(xs.at[0, pl.ds(0, 2 * (nx - 1))], top_r.at[3])
        for l in range(2):
            a_half(top - 1, l, a_first(top - 1, l))
        li_third()

        def step(i, carry):
            application(top - 1 - i, False)
            return carry

        lax.fori_loop(0, top - 1, step, 0)
        application(0, True)

        with scope("t_z0"):
            spread_z(0)
            release(1)
        with scope("t_terms"):
            in_term(1)
            await_up(2)
            out_term(2)
        with scope("t_in0"):
            in_term(0)
        with scope("t_up1"):
            await_up(1)
        with scope("t_out1"):
            out_term(1)

        with scope("drain"):
            await_bytes(pc.at[0, pl.ds(0, nx - 1)], st_s.at[1])
            await_bytes(pc.at[0], st_s.at[2])
            await_bytes(a_top.at[pl.ds(0, 3)], top_s.at[0])
            await_bytes(r_top.at[pl.ds(0, nx - 1)], top_s.at[1])
            await_bytes(z_top.at[pl.ds(0, nz - 1)], top_s.at[2])
            await_bytes(xs.at[0, pl.ds(0, 2 * (nx - 1))], top_s.at[3])
            await_bytes(g_top, top_s.at[4])
            for way in range(2):
                await_bytes(wbuf.at[0, :, :, pl.ds(0, nz - 1)], wz_s.at[way])

            def sent(s, c):
                for h in range(2):
                    await_bytes(a_buf.at[0, h, pl.ds(0, 3)], ph_s.at[0, h, s])
                    await_bytes(b_buf.at[0, h, pl.ds(0, nx - 1)], ph_s.at[1, h, s])
                return c

            lax.fori_loop(1, top, sent, 0)
            for h in range(2):
                await_bytes(a_buf.at[0, h, pl.ds(0, 3)], ph_s.at[0, h, 0])
            await_bytes(gz.at[pl.ds(0, 2 * (nx - 1))], ph_s.at[1, 0, 0])
            await_bytes(up.at[pl.ds(0, top * (2 * nz - 1))], g_s.at[0])
            await_bytes(up.at[pl.ds(0, nsec * block)], uz_s.at[0])

    def await_z(t):
        await_bytes(up.at[pl.ds(0, block)], uz_r.at[t])

    def spread_x(t):
        await_z(t)
        pl.semaphore_wait(go.at[t], 1)
        src = up.at[pl.ds(slot(t, x), block)]
        for d in x_order:
            send(src, src, ux_s.at[0], ux_r.at[t], dev(x_=xat(d)))

    def spread_core(t):
        await_bytes(up.at[pl.ds(0, (nx - 1) * block)], ux_r.at[t])
        src = up.at[pl.ds(slot(t, 0), nx * block)]
        send(src, src, ud_s.at[0], ud_r.at[t], dev(core_=1))

    @pl.when(core == 0)
    def _():
        spread_pre()
        stage_b()
        li_first()
        og_in.wait()
        first_out_term()
        li_second()
        li_third()
        await_bytes(g_top, top_r.at[4])
        first_in_term()

        def move(i, carry):
            t = top - i
            with scope("s_x"):
                spread_x(t)
            with scope("s_in"):
                @pl.when(t < top)
                def _():
                    in_term(t)

            with scope("s_core"):
                spread_core(t)
            with scope("s_out"):
                out_term(t)
            return carry

        lax.fori_loop(0, top - 1, move, 0)
        with scope("s_x1"):
            spread_x(1)
        with scope("s_in01"):
            in_term(1)
            in_term(0)
        with scope("s_core1"):
            spread_core(1)
        with scope("s_z0"):
            await_z(0)
        for l in range(2):
            v = columns(0, x, l)
            for c in range(2):
                at = pl.multiple_of(l * fe + (2 * x + c) * LANES, LANES)

                @pl.when(x == 0)
                def _():
                    ig_out[:, :, pl.ds(at, LANES)] = v[:, c]

                @pl.when(x != 0)
                def _():
                    x_end[l, c] = v[:, c]
                    send(x_end.at[l, c], ig_out.at[:, :, pl.ds(at, LANES)], ux_s.at[1], ux_r.at[0], dev(x_=0))

        with scope("s_out1"):
            out_term(1)
        with scope("s_x0w"):
            @pl.when(x == 0)
            def _():
                await_bytes(up.at[pl.ds(0, (nx - 1) * block)], ux_r.at[0])

        with scope("s_drain"):
            await_bytes(pc.at[0, pl.ds(0, nx - 1)], st_s.at[1])
            await_bytes(pc.at[0, 0], st_s.at[5])
            for m in range(2):
                await_bytes(wbuf.at[m, 0, 0, 0], wd_s.at[m])
            await_bytes(pre_t.at[0], pt_s.at[1])
            await_bytes(up.at[pl.ds(0, top * (nx - 1) * block)], ux_s.at[0])
            await_bytes(up.at[pl.ds(0, top * nx * block)], ud_s.at[0])

            @pl.when(x != 0)
            def _():
                await_bytes(up.at[pl.ds(0, block)], ux_s.at[1])

    await_bytes(pa_all.at[pl.ds(0, nz - 1)], st_s.at[0])
    await_bytes(pre_t.at[pl.ds(0, nsec - 1)], st_s.at[3])
    await_bytes(pre_t.at[0], pt_s.at[0])
    for cp in swaps:
        cp.wait_send()
    await_bytes(li.at[0, 0], li_s.at[0])
    if ring:
        await_bytes(li.at[0, 0], li_s.at[1])
        await_bytes(li.at[0, 0, lo], li_s.at[2])
        await_bytes(li.at[0, 0, hi], li_s.at[3])
    await_bytes(li.at[0], li_s.at[4])


def finish(ig, gi, go, ig_out, gi_out, go_out, sems):
    copies = [pltpu.make_async_copy(src, dst, sems.at[k]) for k, (src, dst) in enumerate(((ig, ig_out), (gi, gi_out), (go, go_out)))]
    for cp in copies:
        cp.start()
    for cp in copies:
        cp.wait()


def body(layer_inputs, pre_act, out_grad, w_in, w_out):
    nz, nx = lax.axis_size("z"), lax.axis_size("x")
    nsec = 2 * nx
    tok, width = out_grad.shape
    fb = w_in.shape[2]
    hid = pre_act.shape[2]
    fe = width // 2
    tiles = nz * fb // LANES
    half = nz // 2
    dma = pltpu.SemaphoreType.DMA
    vmem = pltpu.VMEM
    scratch = [
        vmem((2, 2, 2, nz, fb, fe), BF16),
        vmem((nz, 8, hid), BF16),
        vmem((nz, 8, hid), BF16),
        vmem((nx, 2, tiles, 8, LANES), BF16),
        vmem((2, nsec, 2, tiles, 8, LANES), BF16),
        vmem((nsec, 2, 2 * tiles, 8, LANES), F32),
        vmem((nsec, fb, tok), BF16),
        vmem((nsec, fb, tok), BF16),
        vmem((2, 2, fb, tok), BF16),
        vmem((nsec, fb, tok), BF16),
        vmem((2, nx, tok, width), BF16),
        vmem((nz, 8, width), BF16),
        vmem((4, 4 * fb, tok), BF16),
        vmem((nx, nz, 2, 8, LANES), BF16),
        vmem((nx, nz, 2, 8, LANES), BF16),
        vmem((nz, 2, 8, LANES), BF16),
        vmem((nz, 2, 8, LANES), BF16),
        vmem((fb, tok), BF16),
        vmem((fb, tok), BF16),
        vmem((2, 2 * tiles, fe, LANES), BF16),
        vmem((nsec + 1, nsec, 8, LANES), BF16),
        vmem((nsec, 2, 4, 8, 2 * nz * fb), BF16),
        vmem((nsec, 2, nx, nx, 8, LANES), BF16),
        vmem((2, 8, 2 * nz * fb), F32),
        vmem((2, 8, fe // 2), F32),
        vmem((nsec, 2, 2 * tiles, 8, LANES), BF16),
        vmem((nsec * nz, 8, LANES), BF16),
        vmem((LANES, tok), F32),
        vmem((nsec * nx * 4 * nz, 8, LANES), BF16),
        vmem((2, 2, nz, 8, LANES), BF16),
        dma((5,)),
        dma((2,)), dma((2, 2)),
        dma((2,)), dma((2,)),
        dma((2,)), dma((2, half, 2, 2)),
        dma((6,)), dma((4,)),
        dma((2,)), dma((1,)),
        dma((5,)), dma((5,)),
        dma((2, 2, nsec)), dma((2, 2, nsec)),
        dma((5,)), dma((5,)),
        dma((1,)), dma((nsec,)),
        dma((1,)), dma((nsec,)),
        dma((2,)), dma((nsec,)),
        dma((1,)), dma((nsec,)),
        pltpu.SemaphoreType.REGULAR((nsec,)),
    ]
    hbm, on_chip = pl.BlockSpec(memory_space=pltpu.HBM), pl.BlockSpec(memory_space=pltpu.VMEM)
    shapes = (
        jax.ShapeDtypeStruct((nz, 8, width), BF16),
        jax.ShapeDtypeStruct((fb, width), F32),
        jax.ShapeDtypeStruct((fb, width), F32),
    )
    operands = (
        layer_inputs.reshape(tok, width),
        pre_act.reshape(nz, 8, hid),
        out_grad.reshape(nz, 8, width),
        w_in.reshape(fb, width),
        w_out.reshape(fb, width),
    )
    results = pl.pallas_call(
        kernel,
        out_shape=shapes,
        in_specs=[hbm] * 5,
        out_specs=(on_chip,) * 3,
        scratch_shapes=scratch,
        name="chain",
        compiler_params=pltpu.CompilerParams(
            collective_id=0, has_side_effects=True, vmem_limit_bytes=40 * 1024 * 1024
        ),
    )(*(pltpu.with_memory_space_constraint(v, pltpu.HBM) for v in operands))
    ig, gi, go = pl.pallas_call(
        finish,
        out_shape=shapes,
        in_specs=[on_chip] * 3,
        out_specs=(hbm,) * 3,
        scratch_shapes=[dma((3,))],
        name="finish",
    )(*(pltpu.with_memory_space_constraint(v, pltpu.VMEM) for v in results))
    return (
        ig.reshape(1, tok, width),
        gi.reshape(1, 1, fb, width),
        go.reshape(1, 1, fb, width),
    )


def solution(mesh):
    shape = mesh.shape
    split = Mesh(
        mesh.devices.reshape(shape["section"] // 2, 2, shape["dp"] // 2, 2, shape["mp"]), AXES
    )
    sec, dp = ("x", "core"), ("z", "ylo")
    placed = (
        P(sec, None, "yhi"),
        P(sec, None, dp),
        P(None, "yhi"),
        P(dp, sec, None, "yhi"),
        P(dp, sec, None, "yhi"),
    )
    return jax.shard_map(
        body,
        mesh=split,
        in_specs=placed,
        out_specs=(P(sec, None, "yhi"), P(dp, sec, None, "yhi"), P(dp, sec, None, "yhi")),
        check_vma=False,
    )
```

time: 145 us -> 131 us (0.903)
  Pallas kernels: 144 us -> 129 us
    pallas_call x1, Pallas kernels: 143 us -> 128 us  [body(): pl.pallas_call(kernel, out_shape=shapes, in_specs=[hbm] * 5, out_specs=(o...]
where the time goes in v3:
time: 131 us; the launch traced here: 130 us
  Pallas kernels  129 us (98%)
    pallas_call x1, Pallas kernels, body(): pl.pallas_call(kernel, out_shape=shapes, in_specs=[hbm] * 5, out_specs=(o...  128 us

profile of v3, /device:TPU:24, one launch (start us, length us, event | category | flops | bytes accessed | tf_op | source)
XLA Modules:
  0.0 129.7 jit_solution(1438198937643385367)
XLA Ops:
  0.6 128.0 %chain.1 = (bf16[16,8,2048]{2,1,0:T(8,128)(2,1)S(1)}, f32[32,2048]{1,0:T(8,128)S(1)}, f32[32,2048]{1,0:T(8,128)S(1)}) custom-call(bf16[128,2048]{1,0:T(8,128)(2,1)} %bitcast.8, bf16[16,8,256]{2,1,0:T(8,128)(2,1)} %bitcast.12, bf16[16,8,2048]{2,1,0:T(8,128)(2,1)} %bitcast.9, bf16[32,2048]{1,0:T(8,128)(2,1)} %bitcast.10, bf16[32,2048]{1,0:T(8,128)(2,1)} %bitcast.11), custom_call_target="tpu_custom_call" | custom-call | tf_op jit(solution)/shard_map/chain/pallas_call | solution.py:735
  128.7 1.0 finish.1

commit v4 on v3

--- a/solution.py
+++ b/solution.py
@@ -32,7 +32,7 @@
     a_top, b_top, r_top, q_top, z_top, g_top, g_pass,
     w_t, xs, a_buf, b_buf, a_acc, b_acc, gbuf, gz, gt, up, x_end,
     lsem, wx_s, wx_r, wd_s, wd_r, wz_s, wz_r, st_s, st_r, pt_s, pt_r, top_s, top_r, ph_s, ph_r, li_s, li_r,
-    g_s, g_r, uz_s, uz_r, ux_s, ux_r, ud_s, ud_r, go,
+    g_s, g_r, uz_s, uz_r, ux_s, ux_r, ud_s, ud_r, go, near,
 ):
     nx, nz = lax.axis_size("x"), lax.axis_size("z")
     nsec = 2 * nx
@@ -90,7 +90,7 @@
     theirs = pl.ds(pl.multiple_of(other * fe, LANES), fe)
 
     w_hbm = (wi_hbm, wo_hbm)
-    pa_in = pltpu.make_async_copy(pa_hbm, pa, lsem.at[0])
+    pa_in = pltpu.make_async_copy(pa_hbm, pa.at[core], lsem.at[0])
     w_in_ = [pltpu.make_async_copy(w_hbm[m].at[:, mine], wbuf.at[m, ylo, 1, z], lsem.at[1 + m]) for m in range(2)]
     og_in = pltpu.make_async_copy(og_hbm, og, lsem.at[3])
     li_in = pltpu.make_async_copy(li_hbm, li.at[core, x], lsem.at[4])
@@ -105,19 +105,47 @@
     li_in.start()
 
     barrier = pltpu.get_barrier_semaphore()
-    greeted = [dev(z_=zat(d)) for d in range(1, nz)] + [dev(*peer(*p)) for p in sections]
+    greeted = [dev(z_=zat(d)) for d in (1, -1)] + [dev(*peer(*p)) for p in sections]
     greeted += [dev(y_=yat(d)) for d in range(1, 4)] + [dev(core_=1 - core, y_=partner)]
     for to in greeted:
         pl.semaphore_signal(barrier, inc=1, device_id=to, device_id_type=MESH_ID)
     pa_in.wait()
-    v = pa[...].astype(F32).reshape(tok, nsec * fb)
+    v = pa[core].astype(F32).reshape(tok, nsec * fb)
     pa_t[...] = jnp.swapaxes(v, 0, 1).astype(BF16).reshape(nsec, fb, tok)
     with scope("barrier"):
         pl.semaphore_wait(barrier, len(greeted))
 
-    for d in z_order:
-        send(pa.at[zat(d)], pa_all.at[z], st_s.at[0], st_r.at[0], dev(z_=zat(d)))
-    pa_all[z] = pa[z]
+    half = nz // 2
+
+    def meet(r):
+        for d in (1, -1):
+            pl.semaphore_signal(near.at[r], inc=1, device_id=dev(z_=zat(d)), device_id_type=MESH_ID)
+        pl.semaphore_wait(near.at[r], 2)
+
+    def pa_first():
+        await_bytes(pa.at[1], st_r.at[5])
+        for h in range(2):
+            @pl.when(yhi == h)
+            def _():
+                for d in z_order:
+                    if d % 2 == h:
+                        for c in range(2):
+                            dst = pa_all.at[c, lax.rem(z, 2), z // 2]
+                            send(pa.at[c, zat(d)], dst, st_s.at[0], st_r.at[0], dev(z_=zat(d)))
+                if h == 0:
+                    for c in range(2):
+                        pa_all[c, lax.rem(z, 2), z // 2] = pa[c, z]
+
+    def await_pa(sem):
+        for h in range(2):
+            @pl.when(yhi == h)
+            def _():
+                await_bytes(pa.at[0, pl.ds(0, 2 * (half - 1 + h))], sem)
+
+    def pa_second():
+        await_pa(st_r.at[0])
+        mine_ = pa_all.at[:, lax.rem(z + yhi, 2)]
+        send(mine_, mine_, st_s.at[6], st_r.at[4], dev(y_=yat(2)))
 
     swaps = [
         send(w_hbm[m].at[:, theirs], wbuf.at[m, ylo, core, z], wx_s.at[m], wx_r.at[core, m], dev(core_=1, y_=partner))
@@ -129,6 +157,10 @@
         for m in range(2):
             send(w_hbm[m].at[:, mine], wbuf.at[m, ylo, 0, z], wd_s.at[m], wd_r.at[m], dev(core_=1))
 
+    @pl.when(core == 1)
+    def _():
+        send(pa.at[1], pa.at[1], st_s.at[5], st_r.at[5], dev(core_=0))
+
     for p in sections:
         to = peer(*p)
         send(pa_t.at[to[0] * 2 + to[1]], pre_t.at[sec], st_s.at[3], st_r.at[3], dev(*to))
@@ -148,31 +180,24 @@
             dst[...] = pre_t[top]
 
     def stage_b():
-        await_bytes(pa_all.at[pl.ds(0, nz - 1)], st_r.at[0])
+        await_bytes(pa_all.at[:, 0], st_r.at[4])
         group = lax.broadcasted_iota(jnp.int32, (8, LANES), 1) // fb
-        for ct in range(nsec // per_tile):
-            for t in range(tiles):
-                out = [jnp.zeros((8, LANES), F32)] * per_tile
-                for j in range(per_tile):
-                    v = pa_all[t * per_tile + j, :, ct * LANES:(ct + 1) * LANES].astype(F32)
+        for c in range(2):
+            for ct in range(nsec // per_tile):
+                for t in range(tiles):
+                    out = [jnp.zeros((8, LANES), F32)] * per_tile
+                    for j in range(per_tile):
+                        at = t * per_tile + j
+                        v = pa_all[c, at % 2, at // 2, :, ct * LANES:(ct + 1) * LANES].astype(F32)
+                        for k in range(per_tile):
+                            shift = (j - k) * fb % LANES
+                            r = pltpu.roll(v, shift, 1) if shift else v
+                            out[k] = jnp.where(group == j, r, out[k])
                     for k in range(per_tile):
-                        shift = (j - k) * fb % LANES
-                        r = pltpu.roll(v, shift, 1) if shift else v
-                        out[k] = jnp.where(group == j, r, out[k])
-                for k in range(per_tile):
-                    c = ct * per_tile + k
-                    pb[c // 2, c % 2, t] = out[k].astype(BF16)
-        dst = pc.at[ylo, sec]
-        for d in x_order:
-            send(pb.at[xat(d)], dst, st_s.at[1], st_r.at[1], dev(x_=xat(d), core_=1))
-
-        @pl.when(core == 0)
-        def _():
-            send(pb.at[x], dst, st_s.at[5], st_r.at[1], dev(core_=1))
-
-        @pl.when(core == 1)
-        def _():
-            dst[...] = pb[x]
+                        to = ct * per_tile + k
+                        pb[to // 2, c, to % 2, t] = out[k].astype(BF16)
+        for d in x_order + [0]:
+            send(pb.at[xat(d)], pc.at[ylo, pl.ds(2 * x, 2)], st_s.at[1], st_r.at[1], dev(x_=xat(d), core_=1))
 
     cut = tok // 2
     lo, hi = pl.ds(0, cut), pl.ds(cut, cut)
@@ -249,31 +274,34 @@
         rows = gt[pl.ds(pl.multiple_of(lax.rem(z, per_tile) * fb, fb), fb), :].astype(BF16)
         gi_out[...] += jnp.dot(rows, li[lax.rem(t, 2), t // 2], preferred_element_type=F32)
 
-    half = nz // 2
     hu, hn, hj = 2 * nz * fb, fe // 2, nsec // 2
-
-    def hop(k):
-        last = k == half
-        for which in range(2):
-            l = ylo if which == 0 else other
-            for m in range(2):
-                if k == 1:
-                    if which == 0:
-                        w_in_[m].wait()
-                        await_bytes(wbuf.at[m, 0, 0, 0], wd_r.at[m])
-                    else:
-                        for c in range(2):
-                            await_bytes(wbuf.at[m, 0, 0, 0], wx_r.at[c, m])
-                for way, step in ((0, 1), (1, -1)):
-                    if k > 1:
-                        await_bytes(wbuf.at[m, 0, :, 0], wz_r.at[way, k - 2, m, l])
-                    if last and way != m:
-                        continue
-                    src = wbuf.at[m, l, :, zat(-step * (k - 1))]
-                    send(src, src, wz_s.at[way], wz_r.at[way, k - 1, m, l], dev(z_=zat(step)))
+    def hop(m, k, parts=(0, 1)):
+        for which in parts:
+            l = which if k == half else ylo if which == 0 else other
+            if k == 1:
+                if which == 0:
+                    w_in_[m].wait()
+                    await_bytes(wbuf.at[m, 0, 0, 0], wd_r.at[m])
+                else:
+                    for c in range(2):
+                        await_bytes(wbuf.at[m, 0, 0, 0], wx_r.at[c, m])
+            for way, step in ((0, 1), (1, -1)):
+                if k > 1:
+                    await_bytes(wbuf.at[m, 0, :, 0], wz_r.at[way, k - 2, m, l])
+                if k == half and way != which:
+                    continue
+                src = wbuf.at[m, l, :, zat(-step * (k - 1))]
+                send(src, src, wz_s.at[way], wz_r.at[way, k - 1, m, l], dev(z_=zat(step)))
+
+    def all_met():
+        pl.semaphore_wait(near.at[half - 1], 1)
+
+    def await_last(m):
+        for way in range(2):
+            await_bytes(wbuf.at[m, 0, :, 0], wz_r.at[way, half - 1, m, way])
 
     def stage_c():
-        await_bytes(pc.at[0, pl.ds(0, nsec - 1)], st_r.at[1])
+        await_bytes(pc.at[0], st_r.at[1])
         send(pc.at[ylo], pc.at[ylo], st_s.at[2], st_r.at[2], dev(y_=partner))
 
     def stage_d():
@@ -405,25 +433,26 @@
 
     def application(s, final):
         with scope("bg_a"):
+            @pl.when(s <= top - 3)
+            def _():
+                release(s + 3)
+
             @pl.when(s <= top - 2)
             def _():
-                release(s + 2)
-
-            spread_z(s + 1)
+                spread_z(s + 1)
 
             @pl.when(s == top - 2)
             def _():
                 first_in_term()
 
-            @pl.when(s == top - 1)
-            def _():
-                turn(tiles // 2)
-
             @pl.when(s <= top - 3)
             def _():
                 in_term(s + 2)
-                await_up(s + 3)
-                out_term(s + 3)
+
+            @pl.when(s <= top - 5)
+            def _():
+                await_up(s + 5)
+                out_term(s + 5)
 
         for l in range(2):
             with scope(f"wait_a{l}"):
@@ -461,6 +490,10 @@
         with scope("bg_b"):
             spread_g(s)
 
+            @pl.when(s == top - 1)
+            def _():
+                spread_z(top)
+
         if final:
             with scope("wait_b"):
                 await_bytes(gz.at[pl.ds(0, 2 * (nx - 1))], ph_r.at[1, 0, s])
@@ -489,25 +522,34 @@
     @pl.when(core == 1)
     def _():
         plan = [
-            (1, top_first), (2, top_second), (3, stage_b), (3, li_first), (4, top_third), (5, stage_c), (5, first_out_term),
-            (6, stage_d), (6, li_second), (7, top_fourth),
+            (1, top_first), (2, top_second), (2, li_first), (4, all_met), (4, top_third), (5, first_out_term), (6, li_second),
+            (6, stage_c), (7, stage_d), (7, top_fourth),
         ]
         plan += [(half if d else 5, lambda d=d: turn(d)) for d in (0, -1, 1) if d % tiles != tiles // 2]
         for k in range(1, half + 1):
             with scope(f"hop{k}"):
-                hop(k)
+                if k == 1:
+                    hop(1, 1, (0,))
+                    hop(0, 1, (0,))
+                    hop(1, 1, (1,))
+                else:
+                    hop(1, k)
+                    hop(0, k - 1, (1,) if k == 2 else (0, 1))
             with scope(f"stage{k}"):
                 for at, f in plan:
                     if min(at, half) == k:
                         f()
-        with scope("gather_end"):
-            for l in range(2):
-                for way in range(2):
-                    await_bytes(wbuf.at[way, 0, :, 0], wz_r.at[way, half - 1, way, l])
+        with scope("gather_out"):
+            await_last(1)
         with scope("top_end"):
             await_bytes(xs.at[0, pl.ds(0, 2 * (nx - 1))], top_r.at[3])
         for l in range(2):
             a_half(top - 1, l, a_first(top - 1, l))
+        with scope("hop_end"):
+            hop(0, half)
+            turn(tiles // 2)
+        with scope("gather_in"):
+            await_last(0)
         li_third()
 
         def step(i, carry):
@@ -519,20 +561,25 @@
 
         with scope("t_z0"):
             spread_z(0)
+            release(2)
             release(1)
         with scope("t_terms"):
             in_term(1)
+            for t in range(min(top, 4), 2, -1):
+                await_up(t)
+                out_term(t)
+        with scope("t_in0"):
+            in_term(0)
+        with scope("t_up2"):
             await_up(2)
             out_term(2)
-        with scope("t_in0"):
-            in_term(0)
         with scope("t_up1"):
             await_up(1)
         with scope("t_out1"):
             out_term(1)
 
         with scope("drain"):
-            await_bytes(pc.at[0, pl.ds(0, nx - 1)], st_s.at[1])
+            await_bytes(pa.at[1], st_s.at[5])
             await_bytes(pc.at[0], st_s.at[2])
             await_bytes(a_top.at[pl.ds(0, 3)], top_s.at[0])
             await_bytes(r_top.at[pl.ds(0, nx - 1)], top_s.at[1])
@@ -573,8 +620,13 @@
     @pl.when(core == 0)
     def _():
         spread_pre()
+        for r in range(half - 1):
+            meet(r)
+        pl.semaphore_signal(near.at[half - 1], inc=1, device_id=dev(core_=1), device_id_type=MESH_ID)
+        pa_first()
+        li_first()
+        pa_second()
         stage_b()
-        li_first()
         og_in.wait()
         first_out_term()
         li_second()
@@ -597,12 +649,16 @@
                 out_term(t)
             return carry
 
-        lax.fori_loop(0, top - 1, move, 0)
-        with scope("s_x1"):
+        lax.fori_loop(0, top - 2, move, 0)
+        with scope("s_x21"):
+            spread_x(2)
             spread_x(1)
-        with scope("s_in01"):
-            in_term(1)
-            in_term(0)
+        with scope("s_in"):
+            for t in (2, 1, 0):
+                in_term(t)
+        with scope("s_core2"):
+            spread_core(2)
+            out_term(2)
         with scope("s_core1"):
             spread_core(1)
         with scope("s_z0"):
@@ -629,8 +685,9 @@
                 await_bytes(up.at[pl.ds(0, (nx - 1) * block)], ux_r.at[0])
 
         with scope("s_drain"):
-            await_bytes(pc.at[0, pl.ds(0, nx - 1)], st_s.at[1])
-            await_bytes(pc.at[0, 0], st_s.at[5])
+            await_pa(st_s.at[0])
+            await_bytes(pa_all.at[:, 0], st_s.at[6])
+            await_bytes(pc.at[0], st_s.at[1])
             for m in range(2):
                 await_bytes(wbuf.at[m, 0, 0, 0], wd_s.at[m])
             await_bytes(pre_t.at[0], pt_s.at[1])
@@ -641,7 +698,6 @@
             def _():
                 await_bytes(up.at[pl.ds(0, block)], ux_s.at[1])
 
-    await_bytes(pa_all.at[pl.ds(0, nz - 1)], st_s.at[0])
     await_bytes(pre_t.at[pl.ds(0, nsec - 1)], st_s.at[3])
     await_bytes(pre_t.at[0], pt_s.at[0])
     for cp in swaps:
@@ -675,9 +731,9 @@
     vmem = pltpu.VMEM
     scratch = [
         vmem((2, 2, 2, nz, fb, fe), BF16),
-        vmem((nz, 8, hid), BF16),
-        vmem((nz, 8, hid), BF16),
-        vmem((nx, 2, tiles, 8, LANES), BF16),
+        vmem((2, nz, 8, hid), BF16),
+        vmem((2, 2, half, 8, hid), BF16),
+        vmem((nx, 2, 2, tiles, 8, LANES), BF16),
         vmem((2, nsec, 2, tiles, 8, LANES), BF16),
         vmem((nsec, 2, 2 * tiles, 8, LANES), F32),
         vmem((nsec, fb, tok), BF16),
@@ -708,7 +764,7 @@
         dma((2,)), dma((2, 2)),
         dma((2,)), dma((2,)),
         dma((2,)), dma((2, half, 2, 2)),
-        dma((6,)), dma((4,)),
+        dma((7,)), dma((6,)),
         dma((2,)), dma((1,)),
         dma((5,)), dma((5,)),
         dma((2, 2, nsec)), dma((2, 2, nsec)),
@@ -718,6 +774,7 @@
         dma((2,)), dma((nsec,)),
         dma((1,)), dma((nsec,)),
         pltpu.SemaphoreType.REGULAR((nsec,)),
+        pltpu.SemaphoreType.REGULAR((half,)),
     ]
     hbm, on_chip = pl.BlockSpec(memory_space=pltpu.HBM), pl.BlockSpec(memory_space=pltpu.VMEM)
     shapes = (

time: 131 us -> 128 us (0.977)
  Pallas kernels: 129 us -> 126 us
    pallas_call x1, Pallas kernels: 128 us -> 125 us  [body(): pl.pallas_call(kernel, out_shape=shapes, in_specs=[hbm] * 5, out_specs=(o...]
where the time goes in v4:
time: 128 us; the launch traced here: 127 us
  Pallas kernels  126 us (98%)
    pallas_call x1, Pallas kernels, body(): pl.pallas_call(kernel, out_shape=shapes, in_specs=[hbm] * 5, out_specs=(o...  125 us

profile of v4, /device:TPU:24, one launch (start us, length us, event | category | flops | bytes accessed | tf_op | source)
XLA Modules:
  0.0 127.1 jit_solution(4921251867618840232)
XLA Ops:
  0.6 125.5 %chain.1 = (bf16[16,8,2048]{2,1,0:T(8,128)(2,1)S(1)}, f32[32,2048]{1,0:T(8,128)S(1)}, f32[32,2048]{1,0:T(8,128)S(1)}) custom-call(bf16[128,2048]{1,0:T(8,128)(2,1)} %bitcast.8, bf16[16,8,256]{2,1,0:T(8,128)(2,1)} %bitcast.12, bf16[16,8,2048]{2,1,0:T(8,128)(2,1)} %bitcast.9, bf16[32,2048]{1,0:T(8,128)(2,1)} %bitcast.10, bf16[32,2048]{1,0:T(8,128)(2,1)} %bitcast.11), custom_call_target="tpu_custom_call" | custom-call | tf_op jit(solution)/shard_map/chain/pallas_call | solution.py:792
  126.1 1.0 finish.1

commit v5 on v4

--- a/solution.py
+++ b/solution.py
@@ -1,4 +1,5 @@
 import contextlib
+import math
 
 import jax
 import jax.numpy as jnp
@@ -28,11 +29,10 @@
 def kernel(
     li_hbm, pa_hbm, og_hbm, wi_hbm, wo_hbm,
     ig_out, gi_out, go_out,
-    wbuf, pa, pa_all, pb, pc, slope, pa_t, pre_t, pre_top, hall, li, og,
+    w_own, wbuf, pa, pa_all, pb, pc, slope, pa_t, pre_t, pre_top, hall, li, og,
     a_top, b_top, r_top, q_top, z_top, g_top, g_pass,
-    w_t, xs, a_buf, b_buf, a_acc, b_acc, gbuf, gz, gt, up, x_end,
-    lsem, wx_s, wx_r, wd_s, wd_r, wz_s, wz_r, st_s, st_r, pt_s, pt_r, top_s, top_r, ph_s, ph_r, li_s, li_r,
-    g_s, g_r, uz_s, uz_r, ux_s, ux_r, ud_s, ud_r, go, near,
+    w_t, xs, a_buf, b_buf, a_acc, b_acc, gbuf, gz, gt, up,
+    spare, lsem, out_s, wz_s, wx_r, wd_r, wz_r, st_r, pt_r, top_r, ph_r, li_r, g_r, uz_r, ux_r, ud_r, go, near,
 ):
     nx, nz = lax.axis_size("x"), lax.axis_size("z")
     nsec = 2 * nx
@@ -94,24 +94,26 @@
     w_in_ = [pltpu.make_async_copy(w_hbm[m].at[:, mine], wbuf.at[m, ylo, 1, z], lsem.at[1 + m]) for m in range(2)]
     og_in = pltpu.make_async_copy(og_hbm, og, lsem.at[3])
     li_in = pltpu.make_async_copy(li_hbm, li.at[core, x], lsem.at[4])
-    pa_in.start()
-
-    @pl.when(core == 1)
-    def _():
-        for cp in w_in_:
-            cp.start()
-
-    og_in.start()
-    li_in.start()
-
     barrier = pltpu.get_barrier_semaphore()
     greeted = [dev(z_=zat(d)) for d in (1, -1)] + [dev(*peer(*p)) for p in sections]
     greeted += [dev(y_=yat(d)) for d in range(1, 4)] + [dev(core_=1 - core, y_=partner)]
     for to in greeted:
         pl.semaphore_signal(barrier, inc=1, device_id=to, device_id_type=MESH_ID)
-    pa_in.wait()
-    v = pa[core].astype(F32).reshape(tok, nsec * fb)
-    pa_t[...] = jnp.swapaxes(v, 0, 1).astype(BF16).reshape(nsec, fb, tok)
+
+    first = (1, 0)
+    own_in = [pltpu.make_async_copy(w_hbm[m], w_own.at[m], lsem.at[5 + m]) for m in range(2)]
+    for m in first:
+        own_in[m].start()
+
+        @pl.when(core == 1)
+        def _():
+            w_in_[m].start()
+
+    pa_in.start()
+
+    og_in.start()
+    li_in.start()
+
     with scope("barrier"):
         pl.semaphore_wait(barrier, len(greeted))
 
@@ -131,7 +133,7 @@
                     if d % 2 == h:
                         for c in range(2):
                             dst = pa_all.at[c, lax.rem(z, 2), z // 2]
-                            send(pa.at[c, zat(d)], dst, st_s.at[0], st_r.at[0], dev(z_=zat(d)))
+                            send(pa.at[c, zat(d)], dst, out_s.at[0], st_r.at[0], dev(z_=zat(d)))
                 if h == 0:
                     for c in range(2):
                         pa_all[c, lax.rem(z, 2), z // 2] = pa[c, z]
@@ -145,35 +147,49 @@
     def pa_second():
         await_pa(st_r.at[0])
         mine_ = pa_all.at[:, lax.rem(z + yhi, 2)]
-        send(mine_, mine_, st_s.at[6], st_r.at[4], dev(y_=yat(2)))
-
-    swaps = [
-        send(w_hbm[m].at[:, theirs], wbuf.at[m, ylo, core, z], wx_s.at[m], wx_r.at[core, m], dev(core_=1, y_=partner))
-        for m in range(2)
-    ]
-
-    @pl.when(core == 0)
-    def _():
-        for m in range(2):
-            send(w_hbm[m].at[:, mine], wbuf.at[m, ylo, 0, z], wd_s.at[m], wd_r.at[m], dev(core_=1))
+        send(mine_, mine_, out_s.at[0], st_r.at[4], dev(y_=yat(2)))
+
+    def ring_send(src, m, l, k, way):
+        send(src, src, wz_s.at[way], wz_r.at[k - 1, m, l], dev(z_=zat(1 if way == 0 else -1)))
+
+    swaps = []
+    for m in first:
+        own_in[m].wait()
+
+        @pl.when(core == 0)
+        def _():
+            send(w_own.at[m, :, mine], wbuf.at[m, ylo, 0, z], out_s.at[0], wd_r.at[m], dev(core_=1))
+
+        @pl.when(core == 1)
+        def _():
+            w_in_[m].wait()
+            for way in range(2):
+                ring_send(wbuf.at[m, ylo, 1, z], m, ylo, 1, way)
+
+        dst = wbuf.at[m, ylo, core, z]
+        swaps.append(send(w_own.at[m, :, theirs], dst, out_s.at[0], wx_r.at[core, m], dev(core_=1, y_=partner)))
+
+    pa_in.wait()
 
     @pl.when(core == 1)
     def _():
-        send(pa.at[1], pa.at[1], st_s.at[5], st_r.at[5], dev(core_=0))
-
+        send(pa.at[1], pa.at[1], out_s.at[0], st_r.at[5], dev(core_=0))
+
+    v = pa[core].astype(F32).reshape(tok, nsec * fb)
+    pa_t[...] = jnp.swapaxes(v, 0, 1).astype(BF16).reshape(nsec, fb, tok)
     for p in sections:
         to = peer(*p)
-        send(pa_t.at[to[0] * 2 + to[1]], pre_t.at[sec], st_s.at[3], st_r.at[3], dev(*to))
+        send(pa_t.at[to[0] * 2 + to[1]], pre_t.at[sec], out_s.at[0], st_r.at[3], dev(*to))
     pre_t[sec] = pa_t[sec]
 
     def spread_pre():
         await_bytes(pre_t.at[pl.ds(0, nsec - 1)], st_r.at[3])
         dst = pre_top.at[ylo, core]
-        send(pre_t.at[top], dst, pt_s.at[0], pt_r.at[0], dev(core_=1, y_=partner))
+        send(pre_t.at[top], dst, out_s.at[0], pt_r.at[0], dev(core_=1, y_=partner))
 
         @pl.when(core == 0)
         def _():
-            send(pre_t.at[top], dst, pt_s.at[1], pt_r.at[0], dev(core_=1))
+            send(pre_t.at[top], dst, out_s.at[0], pt_r.at[0], dev(core_=1))
 
         @pl.when(core == 1)
         def _():
@@ -197,7 +213,7 @@
                         to = ct * per_tile + k
                         pb[to // 2, c, to % 2, t] = out[k].astype(BF16)
         for d in x_order + [0]:
-            send(pb.at[xat(d)], pc.at[ylo, pl.ds(2 * x, 2)], st_s.at[1], st_r.at[1], dev(x_=xat(d), core_=1))
+            send(pb.at[xat(d)], pc.at[ylo, pl.ds(2 * x, 2)], out_s.at[0], st_r.at[1], dev(x_=xat(d), core_=1))
 
     cut = tok // 2
     lo, hi = pl.ds(0, cut), pl.ds(cut, cut)
@@ -206,24 +222,24 @@
     def li_first():
         li_in.wait()
         src = li.at[core, x]
-        send(src, src, li_s.at[0], li_r.at[0], dev(x_=xat(1)))
+        send(src, src, out_s.at[1], li_r.at[0], dev(x_=xat(1)))
         if ring:
-            send(src, src, li_s.at[1], li_r.at[1], dev(x_=xat(-1)))
+            send(src, src, out_s.at[1], li_r.at[1], dev(x_=xat(-1)))
 
     def li_second():
         await_bytes(li.at[0, 0], li_r.at[0])
         if ring:
             src = li.at[core, xat(-1), lo]
-            send(src, src, li_s.at[2], li_r.at[2], dev(x_=xat(1)))
+            send(src, src, out_s.at[1], li_r.at[2], dev(x_=xat(1)))
             await_bytes(li.at[0, 0], li_r.at[1])
             src = li.at[core, xat(1), hi]
-            send(src, src, li_s.at[3], li_r.at[3], dev(x_=xat(-1)))
+            send(src, src, out_s.at[1], li_r.at[3], dev(x_=xat(-1)))
 
     def li_third():
         if ring:
             await_bytes(li.at[0, 0, lo], li_r.at[2])
             await_bytes(li.at[0, 0, hi], li_r.at[3])
-        send(li.at[core], li.at[core], li_s.at[4], li_r.at[4], dev(core_=1 - core))
+        send(li.at[core], li.at[core], out_s.at[1], li_r.at[4], dev(core_=1 - core))
 
     def first_out_term():
         for s in range(nsec):
@@ -275,34 +291,34 @@
         gi_out[...] += jnp.dot(rows, li[lax.rem(t, 2), t // 2], preferred_element_type=F32)
 
     hu, hn, hj = 2 * nz * fb, fe // 2, nsec // 2
-    def hop(m, k, parts=(0, 1)):
-        for which in parts:
-            l = which if k == half else ylo if which == 0 else other
-            if k == 1:
-                if which == 0:
-                    w_in_[m].wait()
-                    await_bytes(wbuf.at[m, 0, 0, 0], wd_r.at[m])
-                else:
-                    for c in range(2):
-                        await_bytes(wbuf.at[m, 0, 0, 0], wx_r.at[c, m])
-            for way, step in ((0, 1), (1, -1)):
-                if k > 1:
-                    await_bytes(wbuf.at[m, 0, :, 0], wz_r.at[way, k - 2, m, l])
-                if k == half and way != which:
-                    continue
-                src = wbuf.at[m, l, :, zat(-step * (k - 1))]
-                send(src, src, wz_s.at[way], wz_r.at[way, k - 1, m, l], dev(z_=zat(step)))
+    def hop(m, k, which):
+        l = ylo if which == 0 else other
+        if k == 1:
+            if which == 0:
+                await_bytes(wbuf.at[m, 0, 0, 0], wd_r.at[m])
+            else:
+                for c in range(2):
+                    await_bytes(wbuf.at[m, 0, 0, 0], wx_r.at[c, m])
+        if k > 1:
+            await_bytes(wbuf.at[m, 0, :, pl.ds(0, 2)], wz_r.at[k - 2, m, l])
+        for way, step in ((0, 1), (1, -1)):
+            if k == 1 and which == 0:
+                ring_send(wbuf.at[m, l, 0, z], m, l, 1, way)
+            elif k == half:
+                ring_send(wbuf.at[m, l, way, zat(-step * (k - 1))], m, l, k, way)
+            else:
+                ring_send(wbuf.at[m, l, :, zat(-step * (k - 1))], m, l, k, way)
+
+    def await_last(m):
+        for l in range(2):
+            await_bytes(wbuf.at[m, 0, :, 0], wz_r.at[half - 1, m, l])
 
     def all_met():
         pl.semaphore_wait(near.at[half - 1], 1)
 
-    def await_last(m):
-        for way in range(2):
-            await_bytes(wbuf.at[m, 0, :, 0], wz_r.at[way, half - 1, m, way])
-
     def stage_c():
         await_bytes(pc.at[0], st_r.at[1])
-        send(pc.at[ylo], pc.at[ylo], st_s.at[2], st_r.at[2], dev(y_=partner))
+        send(pc.at[ylo], pc.at[ylo], out_s.at[0], st_r.at[2], dev(y_=partner))
 
     def stage_d():
         await_bytes(pc.at[0], st_r.at[2])
@@ -323,7 +339,7 @@
             rows, og[:, :, mine].reshape(tok, fe), (((1,), (1,)), ((), ())), preferred_element_type=F32
         ).astype(BF16)
         for d in y_order:
-            send(a_top.at[y], a_top.at[y], top_s.at[0], top_r.at[0], dev(y_=yat(d)))
+            send(a_top.at[y], a_top.at[y], out_s.at[0], top_r.at[0], dev(y_=yat(d)))
         spread_pre()
 
     def top_second():
@@ -336,14 +352,14 @@
             back = back + a_top[k].astype(F32)
         g = (back * (cdf + v * dens)).astype(BF16)
         g_pass[...] = jnp.where(ylo == 0, g[:fb], g[2 * fb:3 * fb])
-        send(g_pass, g_top, top_s.at[4], top_r.at[4], dev(core_=0))
+        send(g_pass, g_top, out_s.at[0], top_r.at[4], dev(core_=0))
         g_top[...] = jnp.where(ylo == 0, g[fb:2 * fb], g[3 * fb:])
         rows = jnp.swapaxes(g.astype(F32), 0, 1).astype(BF16)
         part = jnp.dot(rows, wbuf[0, :, :, z].reshape(4 * fb, fe), preferred_element_type=F32).astype(BF16)
         for j in range(nsec):
             b_top[j // 2, :, j % 2] = part[:, j * LANES:(j + 1) * LANES].reshape(nz, 8, LANES)
         for d in x_order:
-            send(b_top.at[xat(d)], r_top.at[x], top_s.at[1], top_r.at[1], dev(x_=xat(d)))
+            send(b_top.at[xat(d)], r_top.at[x], out_s.at[0], top_r.at[1], dev(x_=xat(d)))
         r_top[x] = b_top[x]
 
     def top_third():
@@ -353,7 +369,7 @@
             total = total + r_top[k].astype(F32)
         q_top[...] = total.astype(BF16)
         for d in z_order:
-            send(q_top.at[zat(d)], z_top.at[z], top_s.at[2], top_r.at[2], dev(z_=zat(d)))
+            send(q_top.at[zat(d)], z_top.at[z], out_s.at[0], top_r.at[2], dev(z_=zat(d)))
         z_top[z] = q_top[z]
 
     own = pl.ds(2 * x, 2)
@@ -368,15 +384,15 @@
             xs[top - 1, 2 * x + c] = total.astype(BF16)
         src = xs.at[top - 1, own]
         for d in x_order:
-            send(src, src, top_s.at[3], top_r.at[3], dev(x_=xat(d)))
+            send(src, src, out_s.at[0], top_r.at[3], dev(x_=xat(d)))
 
     def spread_z(t):
-        src = xs.at[nsec if isinstance(t, int) and t == 0 else t - 1, own]
+        src = xs.at[t - 1, own]
         dst = up.at[pl.ds(slot(t, x, ylo, z), 2)]
 
         def both(d):
             for to in (partner, y):
-                send(src, dst, uz_s.at[0], uz_r.at[t], dev(core_=0, z_=zat(d), y_=to))
+                send(src, dst, out_s.at[0], uz_r.at[t], dev(core_=0, z_=zat(d), y_=to))
 
         both(half)
 
@@ -388,16 +404,48 @@
         lax.fori_loop(1, half, pair, 0)
         both(0)
 
+    reach = half // 2
+    far = [r for r in range(nz) if min(r, nz - r) > reach]
+    low, high = (0, far[0]), (far[-1] + 1, nz)
+
+    def last_z():
+        src = xs.at[nsec, own]
+        for d in [half] + [d for i in range(1, half) for d in (half - i, half + i)] + [0]:
+            r = (nz - d) % nz
+            dst = up.at[pl.ds(slot(0, x, ylo, r), 2)]
+            for to in (partner, y):
+                if d or to is partner:
+                    send(src, dst, out_s.at[0], uz_r.at[nsec if r in far else 0], dev(z_=zat(d), y_=to))
+        up[pl.ds(slot(0, x, ylo, 0), 2)] = src[...]
+
+    def last_x(kind):
+        for l in range(2):
+            for a, b in ((far[0], far[-1] + 1),) if kind else (low, high):
+                src = up.at[pl.ds(slot(0, x, l, a), 2 * (b - a))]
+                send(src, src, out_s.at[0], ux_r.at[nsec if kind else 0], dev(x_=0, core_=0))
+
+    near_tiles, far_tiles = 4 * (nz - len(far)), 4 * len(far)
+
+    def last_out(kind):
+        for r in range(nz):
+            if (r in far) == bool(kind):
+                row = zat(r)
+                for l in range(2):
+                    for k in range(nx):
+                        for c in range(2):
+                            at = l * fe + (2 * k + c) * LANES
+                            ig_out[row, :, at:at + LANES] = up[slot(0, k, l, r) + c]
+
     def spread_g(t):
         def to(d, c):
             tile = zat(d) // per_tile
             for c_ in range(2):
-                send(gbuf.at[t, ylo, c_ * tiles + tile], gz.at[t * nz + z], g_s.at[0], g_r.at[t], dev(core_=c_, z_=zat(d)))
+                send(gbuf.at[t, ylo, c_ * tiles + tile], gz.at[t * nz + z], out_s.at[0], g_r.at[t], dev(core_=c_, z_=zat(d)))
             return c
 
         lax.fori_loop(1, nz, to, 0)
         tile = z // per_tile
-        send(gbuf.at[t, ylo, tile], gz.at[t * nz + z], g_s.at[0], g_r.at[t], dev(core_=0))
+        send(gbuf.at[t, ylo, tile], gz.at[t * nz + z], out_s.at[0], g_r.at[t], dev(core_=0))
         gz[t * nz + z] = gbuf[t, ylo, tiles + tile]
 
     def turn(away):
@@ -411,19 +459,29 @@
 
         lax.fori_loop(0, 4, one, 0)
 
-    def a_half(s, l, part):
-        a_buf[s, l, y] = part.astype(BF16)
+    def a_half(s, l, part=None):
+        if part is not None:
+            a_buf[s, l, y] = part.astype(BF16)
         for d in y_order:
-            send(a_buf.at[s, l, y], a_buf.at[s, l, y], ph_s.at[0, l, s], ph_r.at[0, l, s], dev(y_=yat(d)))
+            send(a_buf.at[s, l, y], a_buf.at[s, l, y], out_s.at[0], ph_r.at[0, l, s % 2 if isinstance(s, int) else lax.rem(s, 2)], dev(y_=yat(d)))
 
     def a_part(s, l, n):
         lhs = jnp.concatenate([xs[s, n * hj + j] for j in range(hj)], axis=1)
         w_out = jnp.concatenate([w_t[l, t, n * hn:(n + 1) * hn] for t in range(2 * tiles)], axis=1)
         return jnp.dot(lhs, w_out, preferred_element_type=F32)
 
-    def a_first(s, l):
-        lhs = jnp.concatenate([xs[s, j] for j in range(nsec)], axis=1)
-        return lax.dot_general(lhs, wbuf[1, l].reshape(hu, fe), (((1,), (1,)), ((), ())), preferred_element_type=F32)
+    def a_tile(l, away, turned):
+        lhs = jnp.concatenate([xs[top - 1, j] for j in range(nsec)], axis=1)
+        t = lax.rem(z // per_tile + away + tiles, tiles)
+        if turned:
+            w_out = jnp.concatenate([w_t[l, c * tiles + t] for c in range(2)], axis=1)
+            part = jnp.dot(lhs, w_out, preferred_element_type=F32)
+        else:
+            w_out = wbuf[1, l, :, pl.ds(t * per_tile, per_tile)].reshape(2 * LANES, fe)
+            part = lax.dot_general(lhs, w_out, (((1,), (1,)), ((), ())), preferred_element_type=F32)
+        for c in range(2):
+            at = pl.multiple_of((c * tiles + t) * LANES, LANES)
+            a_buf[top - 1, l, y, :, pl.ds(at, LANES)] = part[:, c * LANES:(c + 1) * LANES].astype(BF16)
 
     def release(t):
         pl.semaphore_signal(go.at[t], inc=1, device_id=dev(core_=0), device_id_type=MESH_ID)
@@ -456,7 +514,7 @@
 
         for l in range(2):
             with scope(f"wait_a{l}"):
-                await_bytes(a_buf.at[s, l, pl.ds(0, 3)], ph_r.at[0, l, s])
+                await_bytes(a_buf.at[s, l, pl.ds(0, 3)], ph_r.at[0, l, s % 2 if isinstance(s, int) else lax.rem(s, 2)])
             with scope(f"b_mm{l}"):
                 back = a_buf[s, l, 0].astype(F32)
                 for k in range(1, 4):
@@ -479,16 +537,18 @@
             if not final:
                 src = b_buf.at[s, n, x]
                 for d in x_order:
-                    send(src, src, ph_s.at[1, n, s], ph_r.at[1, n, s], dev(x_=xat(d)))
+                    send(src, src, out_s.at[0], ph_r.at[1, n, s % 2 if isinstance(s, int) else lax.rem(s, 2)], dev(x_=xat(d)))
         hx = nx // 2
         if final:
             for d in x_order:
                 to = xat(d)
                 src = b_buf.at[s, to // hx, x, pl.ds(2 * lax.rem(to, hx), 2)]
-                send(src, src, ph_s.at[1, 0, s], ph_r.at[1, 0, s], dev(x_=to))
+                send(src, src, out_s.at[0], ph_r.at[1, 0, s % 2], dev(x_=to))
 
         with scope("bg_b"):
             spread_g(s)
+            if final:
+                release(2)
 
             @pl.when(s == top - 1)
             def _():
@@ -496,7 +556,7 @@
 
         if final:
             with scope("wait_b"):
-                await_bytes(gz.at[pl.ds(0, 2 * (nx - 1))], ph_r.at[1, 0, s])
+                await_bytes(gz.at[pl.ds(0, 2 * (nx - 1))], ph_r.at[1, 0, s % 2])
             for c in range(2):
                 total = xs[s, 2 * x + c].astype(F32)
                 for k in range(nx):
@@ -505,7 +565,7 @@
             return
         for n in range(2):
             with scope(f"wait_b{n}"):
-                await_bytes(b_buf.at[s, n, pl.ds(0, nx - 1)], ph_r.at[1, n, s])
+                await_bytes(b_buf.at[s, n, pl.ds(0, nx - 1)], ph_r.at[1, n, s % 2 if isinstance(s, int) else lax.rem(s, 2)])
             with scope(f"a_mm{n}"):
                 for j in range(hj):
                     total = xs[s, n * hj + j].astype(F32)
@@ -529,24 +589,32 @@
         for k in range(1, half + 1):
             with scope(f"hop{k}"):
                 if k == 1:
-                    hop(1, 1, (0,))
-                    hop(0, 1, (0,))
-                    hop(1, 1, (1,))
+                    blocks = ((1, 1, 0), (0, 1, 0), (1, 1, 1))
+                elif k == 2:
+                    blocks = ((1, 2, 0), (0, 1, 1), (1, 2, 1))
                 else:
-                    hop(1, k)
-                    hop(0, k - 1, (1,) if k == 2 else (0, 1))
+                    blocks = ((1, k, 0), (0, k - 1, 0), (1, k, 1), (0, k - 1, 1))
+                for b in blocks:
+                    hop(*b)
             with scope(f"stage{k}"):
                 for at, f in plan:
                     if min(at, half) == k:
                         f()
-        with scope("gather_out"):
-            await_last(1)
+        early = [d for d in (0, -1, 1) if d % tiles != tiles // 2]
         with scope("top_end"):
             await_bytes(xs.at[0, pl.ds(0, 2 * (nx - 1))], top_r.at[3])
-        for l in range(2):
-            a_half(top - 1, l, a_first(top - 1, l))
+            for l in range(2):
+                for d in early:
+                    a_tile(l, d, True)
+        with scope("gather_out"):
+            hop(0, half, 0)
+            await_last(1)
+        with scope("a_first"):
+            for l in range(2):
+                a_tile(l, tiles // 2, False)
+                a_half(top - 1, l)
         with scope("hop_end"):
-            hop(0, half)
+            hop(0, half, 1)
             turn(tiles // 2)
         with scope("gather_in"):
             await_last(0)
@@ -560,8 +628,7 @@
         application(0, True)
 
         with scope("t_z0"):
-            spread_z(0)
-            release(2)
+            last_z()
             release(1)
         with scope("t_terms"):
             in_term(1)
@@ -570,37 +637,18 @@
                 out_term(t)
         with scope("t_in0"):
             in_term(0)
+        with scope("t_near"):
+            await_bytes(up.at[pl.ds(0, near_tiles - 2)], uz_r.at[0])
+            last_x(0)
         with scope("t_up2"):
             await_up(2)
             out_term(2)
+        with scope("t_far"):
+            await_bytes(up.at[pl.ds(0, far_tiles)], uz_r.at[nsec])
+            last_x(1)
         with scope("t_up1"):
             await_up(1)
-        with scope("t_out1"):
             out_term(1)
-
-        with scope("drain"):
-            await_bytes(pa.at[1], st_s.at[5])
-            await_bytes(pc.at[0], st_s.at[2])
-            await_bytes(a_top.at[pl.ds(0, 3)], top_s.at[0])
-            await_bytes(r_top.at[pl.ds(0, nx - 1)], top_s.at[1])
-            await_bytes(z_top.at[pl.ds(0, nz - 1)], top_s.at[2])
-            await_bytes(xs.at[0, pl.ds(0, 2 * (nx - 1))], top_s.at[3])
-            await_bytes(g_top, top_s.at[4])
-            for way in range(2):
-                await_bytes(wbuf.at[0, :, :, pl.ds(0, nz - 1)], wz_s.at[way])
-
-            def sent(s, c):
-                for h in range(2):
-                    await_bytes(a_buf.at[0, h, pl.ds(0, 3)], ph_s.at[0, h, s])
-                    await_bytes(b_buf.at[0, h, pl.ds(0, nx - 1)], ph_s.at[1, h, s])
-                return c
-
-            lax.fori_loop(1, top, sent, 0)
-            for h in range(2):
-                await_bytes(a_buf.at[0, h, pl.ds(0, 3)], ph_s.at[0, h, 0])
-            await_bytes(gz.at[pl.ds(0, 2 * (nx - 1))], ph_s.at[1, 0, 0])
-            await_bytes(up.at[pl.ds(0, top * (2 * nz - 1))], g_s.at[0])
-            await_bytes(up.at[pl.ds(0, nsec * block)], uz_s.at[0])
 
     def await_z(t):
         await_bytes(up.at[pl.ds(0, block)], uz_r.at[t])
@@ -610,12 +658,12 @@
         pl.semaphore_wait(go.at[t], 1)
         src = up.at[pl.ds(slot(t, x), block)]
         for d in x_order:
-            send(src, src, ux_s.at[0], ux_r.at[t], dev(x_=xat(d)))
+            send(src, src, out_s.at[0], ux_r.at[t], dev(x_=xat(d)))
 
     def spread_core(t):
         await_bytes(up.at[pl.ds(0, (nx - 1) * block)], ux_r.at[t])
         src = up.at[pl.ds(slot(t, 0), nx * block)]
-        send(src, src, ud_s.at[0], ud_r.at[t], dev(core_=1))
+        send(src, src, out_s.at[2], ud_r.at[t], dev(core_=1))
 
     @pl.when(core == 0)
     def _():
@@ -661,53 +709,57 @@
             out_term(2)
         with scope("s_core1"):
             spread_core(1)
-        with scope("s_z0"):
-            await_z(0)
-        for l in range(2):
-            v = columns(0, x, l)
-            for c in range(2):
-                at = pl.multiple_of(l * fe + (2 * x + c) * LANES, LANES)
-
-                @pl.when(x == 0)
-                def _():
-                    ig_out[:, :, pl.ds(at, LANES)] = v[:, c]
-
-                @pl.when(x != 0)
-                def _():
-                    x_end[l, c] = v[:, c]
-                    send(x_end.at[l, c], ig_out.at[:, :, pl.ds(at, LANES)], ux_s.at[1], ux_r.at[0], dev(x_=0))
-
         with scope("s_out1"):
             out_term(1)
-        with scope("s_x0w"):
-            @pl.when(x == 0)
+
+        @pl.when(x == 0)
+        def _():
+            with scope("s_near"):
+                await_bytes(up.at[pl.ds(0, nx * near_tiles)], ux_r.at[0])
+                last_out(0)
+            with scope("s_far"):
+                await_bytes(up.at[pl.ds(0, nx * far_tiles)], ux_r.at[nsec])
+                last_out(1)
+
+    def size(*shape):
+        return math.prod(shape) // (8 * LANES)
+
+    li_block, row = size(tok, width), size(fb, tok)
+    both_cores = size(2, fb, fe) + nsec * row
+    by_core = (
+        size(2, fb, fe) + row + size(2, half, 8, nsec * fb) + nx * size(2, 2, tiles, 8, LANES) + top * (nx - 1) * block,
+        size(nz, 8, nsec * fb)
+        + size(nsec, 2, tiles, 8, LANES)
+        + 3 * size(4 * fb, tok)
+        + (nx - 1) * 2 * nz
+        + (nz - 1) * 2
+        + (nx - 1) * 2
+        + row
+        + top * 2 * 3 * size(8, hu)
+        + (top - 1) * 2 * (nx - 1) * hj
+        + (nx - 1) * 2
+        + top * (2 * nz - 1)
+        + nsec * block - 2
+        + block,
+    )
+    with scope("drain"):
+        await_bytes(spare.at[pl.ds(0, (nx + (3 if ring else 1)) * li_block)], out_s.at[1])
+
+        @pl.when(core == 1)
+        def _():
+            for way in range(2):
+                await_bytes(wbuf.at[0, :, :, pl.ds(0, nz - 1)], wz_s.at[way])
+            await_bytes(spare.at[pl.ds(0, both_cores + by_core[1])], out_s.at[0])
+
+        @pl.when(core == 0)
+        def _():
+            await_bytes(spare.at[pl.ds(0, top * nx * block)], out_s.at[2])
+
+        for h in range(2):
+            @pl.when((core == 0) & (yhi == h))
             def _():
-                await_bytes(up.at[pl.ds(0, (nx - 1) * block)], ux_r.at[0])
-
-        with scope("s_drain"):
-            await_pa(st_s.at[0])
-            await_bytes(pa_all.at[:, 0], st_s.at[6])
-            await_bytes(pc.at[0], st_s.at[1])
-            for m in range(2):
-                await_bytes(wbuf.at[m, 0, 0, 0], wd_s.at[m])
-            await_bytes(pre_t.at[0], pt_s.at[1])
-            await_bytes(up.at[pl.ds(0, top * (nx - 1) * block)], ux_s.at[0])
-            await_bytes(up.at[pl.ds(0, top * nx * block)], ud_s.at[0])
-
-            @pl.when(x != 0)
-            def _():
-                await_bytes(up.at[pl.ds(0, block)], ux_s.at[1])
-
-    await_bytes(pre_t.at[pl.ds(0, nsec - 1)], st_s.at[3])
-    await_bytes(pre_t.at[0], pt_s.at[0])
-    for cp in swaps:
-        cp.wait_send()
-    await_bytes(li.at[0, 0], li_s.at[0])
-    if ring:
-        await_bytes(li.at[0, 0], li_s.at[1])
-        await_bytes(li.at[0, 0, lo], li_s.at[2])
-        await_bytes(li.at[0, 0, hi], li_s.at[3])
-    await_bytes(li.at[0], li_s.at[4])
+                pa_tiles = 2 * (half - 1 + h) * size(8, nsec * fb)
+                await_bytes(spare.at[pl.ds(0, both_cores + by_core[0] + pa_tiles)], out_s.at[0])
 
 
 def finish(ig, gi, go, ig_out, gi_out, go_out, sems):
@@ -729,7 +781,9 @@
     half = nz // 2
     dma = pltpu.SemaphoreType.DMA
     vmem = pltpu.VMEM
+    spare = 2048
     scratch = [
+        vmem((2, fb, width), BF16),
         vmem((2, 2, 2, nz, fb, fe), BF16),
         vmem((2, nz, 8, hid), BF16),
         vmem((2, 2, half, 8, hid), BF16),
@@ -759,20 +813,21 @@
         vmem((nsec * nz, 8, LANES), BF16),
         vmem((LANES, tok), F32),
         vmem((nsec * nx * 4 * nz, 8, LANES), BF16),
-        vmem((2, 2, nz, 8, LANES), BF16),
+        vmem((spare, 8, LANES), BF16),
+        dma((7,)),
+        dma((3,)), dma((2,)),
+        dma((2, 2)),
+        dma((2,)),
+        dma((half, 2, 2)),
+        dma((6,)),
+        dma((1,)),
         dma((5,)),
-        dma((2,)), dma((2, 2)),
-        dma((2,)), dma((2,)),
-        dma((2,)), dma((2, half, 2, 2)),
-        dma((7,)), dma((6,)),
-        dma((2,)), dma((1,)),
-        dma((5,)), dma((5,)),
-        dma((2, 2, nsec)), dma((2, 2, nsec)),
-        dma((5,)), dma((5,)),
-        dma((1,)), dma((nsec,)),
-        dma((1,)), dma((nsec,)),
-        dma((2,)), dma((nsec,)),
-        dma((1,)), dma((nsec,)),
+        dma((2, 2, 2)),
+        dma((5,)),
+        dma((nsec,)),
+        dma((nsec + 1,)),
+        dma((nsec + 1,)),
+        dma((nsec,)),
         pltpu.SemaphoreType.REGULAR((nsec,)),
         pltpu.SemaphoreType.REGULAR((half,)),
     ]

time: 128 us -> 124 us (0.969)
  the two profiles are of different devices: /device:TPU:24 before, /device:TPU:1 now
where the time goes in v5:
time: 124 us
  Pallas kernels  123 us (99%)
    pallas_call x1, Pallas kernels, body(): pl.pallas_call(kernel, out_shape=shapes, in_specs=[hbm] * 5, out_specs=(o...  122 us

profile of v5, /device:TPU:1, one launch (start us, length us, event | category | flops | bytes accessed | tf_op | source)
XLA Modules:
  0.0 124.0 jit_solution(7673166362473343279)
XLA Ops:
  0.6 122.3 %chain.1 = (bf16[16,8,2048]{2,1,0:T(8,128)(2,1)S(1)}, f32[32,2048]{1,0:T(8,128)S(1)}, f32[32,2048]{1,0:T(8,128)S(1)}) custom-call(bf16[128,2048]{1,0:T(8,128)(2,1)} %bitcast.8, bf16[16,8,256]{2,1,0:T(8,128)(2,1)} %bitcast.12, bf16[16,8,2048]{2,1,0:T(8,128)(2,1)} %bitcast.9, bf16[32,2048]{1,0:T(8,128)(2,1)} %bitcast.10, bf16[32,2048]{1,0:T(8,128)(2,1)} %bitcast.11), custom_call_target="tpu_custom_call" | custom-call | tf_op jit(solution)/shard_map/chain/pallas_call | solution.py:847
  123.0 1.0 finish.1

commit v6 on v5

--- a/solution.py
+++ b/solution.py
@@ -32,7 +32,7 @@
     w_own, wbuf, pa, pa_all, pb, pc, slope, pa_t, pre_t, pre_top, hall, li, og,
     a_top, b_top, r_top, q_top, z_top, g_top, g_pass,
     w_t, xs, a_buf, b_buf, a_acc, b_acc, gbuf, gz, gt, up,
-    spare, lsem, out_s, wz_s, wx_r, wd_r, wz_r, st_r, pt_r, top_r, ph_r, li_r, g_r, uz_r, ux_r, ud_r, go, near,
+    spare, lsem, out_s, wz_s, wx_r, wd_r, wz_r, st_r, pt_r, top_r, ph_r, li_r, g_r, uz_r, ux_r, ud_r, last_r, go, near,
 ):
     nx, nz = lax.axis_size("x"), lax.axis_size("z")
     nsec = 2 * nx
@@ -404,9 +404,20 @@
         lax.fori_loop(1, half, pair, 0)
         both(0)
 
-    reach = half // 2
-    far = [r for r in range(nz) if min(r, nz - r) > reach]
-    low, high = (0, far[0]), (far[-1] + 1, nz)
+    bounds = sorted({half // 2, 3 * half // 4, half})
+    groups = [
+        [r for r in range(nz) if (bounds[i - 1] if i else -1) < min(r, nz - r) <= b] for i, b in enumerate(bounds)
+    ]
+    group_of = {r: i for i, g in enumerate(groups) for r in g}
+
+    def runs(g):
+        out = []
+        for r in g:
+            if out and out[-1][1] == r:
+                out[-1][1] = r + 1
+            else:
+                out.append([r, r + 1])
+        return out
 
     def last_z():
         src = xs.at[nsec, own]
@@ -415,26 +426,25 @@
             dst = up.at[pl.ds(slot(0, x, ylo, r), 2)]
             for to in (partner, y):
                 if d or to is partner:
-                    send(src, dst, out_s.at[0], uz_r.at[nsec if r in far else 0], dev(z_=zat(d), y_=to))
+                    send(src, dst, out_s.at[0], last_r.at[0, group_of[r]], dev(z_=zat(d), y_=to))
         up[pl.ds(slot(0, x, ylo, 0), 2)] = src[...]
 
-    def last_x(kind):
+    def last_x(i):
+        await_bytes(up.at[pl.ds(0, 4 * len(groups[i]) - (2 if i == 0 else 0))], last_r.at[0, i])
         for l in range(2):
-            for a, b in ((far[0], far[-1] + 1),) if kind else (low, high):
+            for a, b in runs(groups[i]):
                 src = up.at[pl.ds(slot(0, x, l, a), 2 * (b - a))]
-                send(src, src, out_s.at[0], ux_r.at[nsec if kind else 0], dev(x_=0, core_=0))
-
-    near_tiles, far_tiles = 4 * (nz - len(far)), 4 * len(far)
-
-    def last_out(kind):
-        for r in range(nz):
-            if (r in far) == bool(kind):
-                row = zat(r)
-                for l in range(2):
-                    for k in range(nx):
-                        for c in range(2):
-                            at = l * fe + (2 * k + c) * LANES
-                            ig_out[row, :, at:at + LANES] = up[slot(0, k, l, r) + c]
+                send(src, src, out_s.at[0], last_r.at[1, i], dev(x_=0, core_=0))
+
+    def last_out(i):
+        await_bytes(up.at[pl.ds(0, nx * 4 * len(groups[i]))], last_r.at[1, i])
+        for r in groups[i]:
+            row = zat(r)
+            for l in range(2):
+                for k in range(nx):
+                    for c in range(2):
+                        at = l * fe + (2 * k + c) * LANES
+                        ig_out[row, :, at:at + LANES] = up[slot(0, k, l, r) + c]
 
     def spread_g(t):
         def to(d, c):
@@ -489,11 +499,11 @@
     def await_up(t):
         await_bytes(up.at[pl.ds(0, nx * block)], ud_r.at[t])
 
-    def application(s, final):
+    def background_a(s):
         with scope("bg_a"):
             @pl.when(s <= top - 3)
             def _():
-                release(s + 3)
+                release(s + 2)
 
             @pl.when(s <= top - 2)
             def _():
@@ -507,31 +517,47 @@
             def _():
                 in_term(s + 2)
 
-            @pl.when(s <= top - 5)
+            @pl.when(s <= top - 4)
             def _():
-                await_up(s + 5)
-                out_term(s + 5)
-
-        for l in range(2):
-            with scope(f"wait_a{l}"):
-                await_bytes(a_buf.at[s, l, pl.ds(0, 3)], ph_r.at[0, l, s % 2 if isinstance(s, int) else lax.rem(s, 2)])
-            with scope(f"b_mm{l}"):
-                back = a_buf[s, l, 0].astype(F32)
-                for k in range(1, 4):
-                    back = back + a_buf[s, l, k].astype(F32)
-                g = []
-                for t in range(2 * tiles):
-                    g_tile = (back[:, t * LANES:(t + 1) * LANES] * slope[s, l, t]).astype(BF16)
-                    gbuf[s, l, t] = g_tile
-                    g.append(g_tile)
-                g = jnp.concatenate(g, axis=1)
-                if l == 0:
-                    for n in range(2):
-                        w_in = wbuf[0, l, :, :, :, n * hn:(n + 1) * hn].reshape(hu, hn)
-                        b_acc[n] = jnp.dot(g, w_in, preferred_element_type=F32)
+                await_up(s + 4)
+                out_term(s + 4)
+
+    def g_half(s, l):
+        with scope(f"wait_a{l}"):
+            await_bytes(a_buf.at[s, l, pl.ds(0, 3)], ph_r.at[0, l, s % 2 if isinstance(s, int) else lax.rem(s, 2)])
+        back = a_buf[s, l, 0].astype(F32)
+        for k in range(1, 4):
+            back = back + a_buf[s, l, k].astype(F32)
+        g = []
+        for t in range(2 * tiles):
+            g_tile = (back[:, t * LANES:(t + 1) * LANES] * slope[s, l, t]).astype(BF16)
+            gbuf[s, l, t] = g_tile
+            g.append(g_tile)
+        return jnp.concatenate(g, axis=1)
+
+    def b_tile(n, away):
+        t = lax.rem(z // per_tile + away + tiles, tiles)
+        pairs = [(l, c) for l in range(2) for c in range(2)]
+        lhs = jnp.concatenate([gbuf[top - 1, l, c * tiles + t] for l, c in pairs], axis=1)
+        rows = pl.ds(t * per_tile, per_tile)
+        w_in = jnp.concatenate([wbuf[0, l, c, rows, :, n * hn:(n + 1) * hn].reshape(LANES, hn) for l, c in pairs], axis=0)
+        return jnp.dot(lhs, w_in, preferred_element_type=F32)
+
+    def application(s, final=False, begin=False):
+        if not begin:
+            background_a(s)
+            g_first = g_half(s, 0)
+            for n in range(2):
+                w_in = wbuf[0, 0, :, :, :, n * hn:(n + 1) * hn].reshape(hu, hn)
+                b_acc[n] = jnp.dot(g_first, w_in, preferred_element_type=F32)
+            g = g_half(s, 1)
         for n in range(2):
-            w_in = wbuf[0, 1, :, :, :, n * hn:(n + 1) * hn].reshape(hu, hn)
-            part = (b_acc[n] + jnp.dot(g, w_in, preferred_element_type=F32)).astype(BF16)
+            if begin:
+                part = b_tile(n, tiles // 2)
+            else:
+                w_in = wbuf[0, 1, :, :, :, n * hn:(n + 1) * hn].reshape(hu, hn)
+                part = jnp.dot(g, w_in, preferred_element_type=F32)
+            part = (b_acc[n] + part).astype(BF16)
             for j in range(hj):
                 b_buf[s, n, x, j] = part[:, j * LANES:(j + 1) * LANES]
             if not final:
@@ -547,11 +573,7 @@
 
         with scope("bg_b"):
             spread_g(s)
-            if final:
-                release(2)
-
-            @pl.when(s == top - 1)
-            def _():
+            if begin:
                 spread_z(top)
 
         if final:
@@ -616,36 +638,40 @@
         with scope("hop_end"):
             hop(0, half, 1)
             turn(tiles // 2)
+        with scope("b_early"):
+            for l in range(2):
+                g_half(top - 1, l)
+            for n in range(2):
+                b_acc[n] = sum((b_tile(n, d) for d in early), jnp.zeros((8, hn), F32))
         with scope("gather_in"):
             await_last(0)
         li_third()
 
+        application(top - 1, begin=True)
+
         def step(i, carry):
-            application(top - 1 - i, False)
+            application(top - 2 - i)
             return carry
 
-        lax.fori_loop(0, top - 1, step, 0)
-        application(0, True)
+        lax.fori_loop(0, top - 2, step, 0)
+        application(0, final=True)
 
         with scope("t_z0"):
             last_z()
             release(1)
         with scope("t_terms"):
             in_term(1)
-            for t in range(min(top, 4), 2, -1):
+            for t in range(min(top, 3), 2, -1):
                 await_up(t)
                 out_term(t)
         with scope("t_in0"):
             in_term(0)
-        with scope("t_near"):
-            await_bytes(up.at[pl.ds(0, near_tiles - 2)], uz_r.at[0])
-            last_x(0)
+        for i in range(len(groups)):
+            with scope(f"t_last{i}"):
+                last_x(i)
         with scope("t_up2"):
             await_up(2)
             out_term(2)
-        with scope("t_far"):
-            await_bytes(up.at[pl.ds(0, far_tiles)], uz_r.at[nsec])
-            last_x(1)
         with scope("t_up1"):
             await_up(1)
             out_term(1)
@@ -655,7 +681,8 @@
 
     def spread_x(t):
         await_z(t)
-        pl.semaphore_wait(go.at[t], 1)
+        if not isinstance(t, int) or t < top:
+            pl.semaphore_wait(go.at[t], 1)
         src = up.at[pl.ds(slot(t, x), block)]
         for d in x_order:
             send(src, src, out_s.at[0], ux_r.at[t], dev(x_=xat(d)))
@@ -682,31 +709,30 @@
         await_bytes(g_top, top_r.at[4])
         first_in_term()
 
-        def move(i, carry):
-            t = top - i
-            with scope("s_x"):
-                spread_x(t)
-            with scope("s_in"):
-                @pl.when(t < top)
-                def _():
-                    in_term(t)
-
+        def finish_one(t):
             with scope("s_core"):
                 spread_core(t)
             with scope("s_out"):
                 out_term(t)
+
+        def move(i, carry):
+            t = top - 1 - i
+            with scope("s_x"):
+                spread_x(t)
+            with scope("s_in"):
+                in_term(t)
+            finish_one(t + 1)
             return carry
 
+        with scope("s_x7"):
+            spread_x(top)
         lax.fori_loop(0, top - 2, move, 0)
-        with scope("s_x21"):
-            spread_x(2)
+        with scope("s_x1"):
             spread_x(1)
+        finish_one(2)
         with scope("s_in"):
-            for t in (2, 1, 0):
+            for t in (1, 0):
                 in_term(t)
-        with scope("s_core2"):
-            spread_core(2)
-            out_term(2)
         with scope("s_core1"):
             spread_core(1)
         with scope("s_out1"):
@@ -714,12 +740,9 @@
 
         @pl.when(x == 0)
         def _():
-            with scope("s_near"):
-                await_bytes(up.at[pl.ds(0, nx * near_tiles)], ux_r.at[0])
-                last_out(0)
-            with scope("s_far"):
-                await_bytes(up.at[pl.ds(0, nx * far_tiles)], ux_r.at[nsec])
-                last_out(1)
+            for i in range(len(groups)):
+                with scope(f"s_last{i}"):
+                    last_out(i)
 
     def size(*shape):
         return math.prod(shape) // (8 * LANES)
@@ -825,9 +848,10 @@
         dma((2, 2, 2)),
         dma((5,)),
         dma((nsec,)),
-        dma((nsec + 1,)),
-        dma((nsec + 1,)),
         dma((nsec,)),
+        dma((nsec,)),
+        dma((nsec,)),
+        dma((2, 3)),
         pltpu.SemaphoreType.REGULAR((nsec,)),
         pltpu.SemaphoreType.REGULAR((half,)),
     ]

time: 124 us -> 122 us (0.984)
  the two profiles are of different devices: /device:TPU:1 before, /device:TPU:24 now
where the time goes in v6:
time: 122 us; the launch traced here: 120 us
  Pallas kernels  120 us (98%)
    pallas_call x1, Pallas kernels, body(): pl.pallas_call(kernel, out_shape=shapes, in_specs=[hbm] * 5, out_specs=(o...  119 us

profile of v6, /device:TPU:24, one launch (start us, length us, event | category | flops | bytes accessed | tf_op | source)
XLA Modules:
  0.0 120.5 jit_solution(14329110061718980070)
XLA Ops:
  0.6 118.9 %chain.1 = (bf16[16,8,2048]{2,1,0:T(8,128)(2,1)S(1)}, f32[32,2048]{1,0:T(8,128)S(1)}, f32[32,2048]{1,0:T(8,128)S(1)}) custom-call(bf16[128,2048]{1,0:T(8,128)(2,1)} %bitcast.8, bf16[16,8,256]{2,1,0:T(8,128)(2,1)} %bitcast.12, bf16[16,8,2048]{2,1,0:T(8,128)(2,1)} %bitcast.9, bf16[32,2048]{1,0:T(8,128)(2,1)} %bitcast.10, bf16[32,2048]{1,0:T(8,128)(2,1)} %bitcast.11), custom_call_target="tpu_custom_call" | custom-call | tf_op jit(solution)/shard_map/chain/pallas_call | solution.py:871
  119.5 1.0 finish.1

commit v7 on v6

--- a/solution.py
+++ b/solution.py
@@ -32,7 +32,7 @@
     w_own, wbuf, pa, pa_all, pb, pc, slope, pa_t, pre_t, pre_top, hall, li, og,
     a_top, b_top, r_top, q_top, z_top, g_top, g_pass,
     w_t, xs, a_buf, b_buf, a_acc, b_acc, gbuf, gz, gt, up,
-    spare, lsem, out_s, wz_s, wx_r, wd_r, wz_r, st_r, pt_r, top_r, ph_r, li_r, g_r, uz_r, ux_r, ud_r, last_r, go, near,
+    spare, lsem, out_s, wz_s, wx_r, wd_r, wz_r, st_r, pt_r, top_r, ph_r, li_r, g_r, ud_r, flag,
 ):
     nx, nz = lax.axis_size("x"), lax.axis_size("z")
     nsec = 2 * nx
@@ -121,8 +121,8 @@
 
     def meet(r):
         for d in (1, -1):
-            pl.semaphore_signal(near.at[r], inc=1, device_id=dev(z_=zat(d)), device_id_type=MESH_ID)
-        pl.semaphore_wait(near.at[r], 2)
+            pl.semaphore_signal(flag.at[r], inc=1, device_id=dev(z_=zat(d)), device_id_type=MESH_ID)
+        pl.semaphore_wait(flag.at[r], 2)
 
     def pa_first():
         await_bytes(pa.at[1], st_r.at[5])
@@ -150,7 +150,7 @@
         send(mine_, mine_, out_s.at[0], st_r.at[4], dev(y_=yat(2)))
 
     def ring_send(src, m, l, k, way):
-        send(src, src, wz_s.at[way], wz_r.at[k - 1, m, l], dev(z_=zat(1 if way == 0 else -1)))
+        send(src, src, wz_s.at[way], wz_r.at[((k - 1) * 2 + m) * 2 + l], dev(z_=zat(1 if way == 0 else -1)))
 
     swaps = []
     for m in first:
@@ -167,7 +167,7 @@
                 ring_send(wbuf.at[m, ylo, 1, z], m, ylo, 1, way)
 
         dst = wbuf.at[m, ylo, core, z]
-        swaps.append(send(w_own.at[m, :, theirs], dst, out_s.at[0], wx_r.at[core, m], dev(core_=1, y_=partner)))
+        swaps.append(send(w_own.at[m, :, theirs], dst, out_s.at[0], wx_r.at[core * 2 + m], dev(core_=1, y_=partner)))
 
     pa_in.wait()
 
@@ -298,9 +298,9 @@
                 await_bytes(wbuf.at[m, 0, 0, 0], wd_r.at[m])
             else:
                 for c in range(2):
-                    await_bytes(wbuf.at[m, 0, 0, 0], wx_r.at[c, m])
+                    await_bytes(wbuf.at[m, 0, 0, 0], wx_r.at[c * 2 + m])
         if k > 1:
-            await_bytes(wbuf.at[m, 0, :, pl.ds(0, 2)], wz_r.at[k - 2, m, l])
+            await_bytes(wbuf.at[m, 0, :, pl.ds(0, 2)], wz_r.at[((k - 2) * 2 + m) * 2 + l])
         for way, step in ((0, 1), (1, -1)):
             if k == 1 and which == 0:
                 ring_send(wbuf.at[m, l, 0, z], m, l, 1, way)
@@ -311,10 +311,10 @@
 
     def await_last(m):
         for l in range(2):
-            await_bytes(wbuf.at[m, 0, :, 0], wz_r.at[half - 1, m, l])
+            await_bytes(wbuf.at[m, 0, :, 0], wz_r.at[((half - 1) * 2 + m) * 2 + l])
 
     def all_met():
-        pl.semaphore_wait(near.at[half - 1], 1)
+        pl.semaphore_wait(flag.at[half - 1], 1)
 
     def stage_c():
         await_bytes(pc.at[0], st_r.at[1])
@@ -392,7 +392,7 @@
 
         def both(d):
             for to in (partner, y):
-                send(src, dst, out_s.at[0], uz_r.at[t], dev(core_=0, z_=zat(d), y_=to))
+                send(src, dst, out_s.at[0], wz_r.at[t], dev(core_=0, z_=zat(d), y_=to))
 
         both(half)
 
@@ -419,25 +419,41 @@
                 out.append([r, r + 1])
         return out
 
+    owner = [p if min(p, nx - p) <= 1 else 0 for p in range(nx)]
+    owned = {o: [p for p in range(nx) if owner[p] == o] for o in sorted(set(owner))}
+    d_order = [half] + [d for i in range(1, half) for d in (half - i, half + i)] + [0]
+
     def last_z():
-        src = xs.at[nsec, own]
-        for d in [half] + [d for i in range(1, half) for d in (half - i, half + i)] + [0]:
-            r = (nz - d) % nz
-            dst = up.at[pl.ds(slot(0, x, ylo, r), 2)]
-            for to in (partner, y):
-                if d or to is partner:
-                    send(src, dst, out_s.at[0], last_r.at[0, group_of[r]], dev(z_=zat(d), y_=to))
-        up[pl.ds(slot(0, x, ylo, 0), 2)] = src[...]
+        for o, pairs in owned.items():
+            @pl.when(x == o)
+            def _():
+                for d in d_order:
+                    r = (nz - d) % nz
+                    for p in pairs:
+                        src = xs.at[nsec, pl.ds(2 * p, 2)]
+                        dst = up.at[pl.ds(slot(0, p, ylo, r), 2)]
+                        if o:
+                            send(src, dst, out_s.at[0], wx_r.at[group_of[r]], dev(core_=1, z_=zat(d), y_=partner))
+                        if d:
+                            send(src, dst, out_s.at[0], wx_r.at[group_of[r]], dev(core_=1, z_=zat(d)))
+                for p in pairs:
+                    up[pl.ds(slot(0, p, ylo, 0), 2)] = xs[nsec, 2 * p:2 * p + 2]
 
     def last_x(i):
-        await_bytes(up.at[pl.ds(0, 4 * len(groups[i]) - (2 if i == 0 else 0))], last_r.at[0, i])
-        for l in range(2):
-            for a, b in runs(groups[i]):
-                src = up.at[pl.ds(slot(0, x, l, a), 2 * (b - a))]
-                send(src, src, out_s.at[0], last_r.at[1, i], dev(x_=0, core_=0))
+        for o, pairs in owned.items():
+            @pl.when(x == o)
+            def _():
+                per_plane = 4 if o else 2 * len(pairs)
+                here = (2 if o else 2 * len(pairs)) if i == 0 else 0
+                await_bytes(up.at[pl.ds(0, per_plane * len(groups[i]) - here)], wx_r.at[i])
+                for a, b in runs(groups[i]):
+                    for p in pairs:
+                        for l, to in ((0, y), (1, y)) if o else ((ylo, partner), (ylo, y)):
+                            src = up.at[pl.ds(slot(0, p, l, a), 2 * (b - a))]
+                            send(src, src, out_s.at[0], wz_r.at[2 * nsec + i], dev(x_=0, core_=0, y_=to))
 
     def last_out(i):
-        await_bytes(up.at[pl.ds(0, nx * 4 * len(groups[i]))], last_r.at[1, i])
+        await_bytes(up.at[pl.ds(0, nx * 4 * len(groups[i]))], wz_r.at[2 * nsec + i])
         for r in groups[i]:
             row = zat(r)
             for l in range(2):
@@ -494,7 +510,7 @@
             a_buf[top - 1, l, y, :, pl.ds(at, LANES)] = part[:, c * LANES:(c + 1) * LANES].astype(BF16)
 
     def release(t):
-        pl.semaphore_signal(go.at[t], inc=1, device_id=dev(core_=0), device_id_type=MESH_ID)
+        pl.semaphore_signal(flag.at[t], inc=1, device_id=dev(core_=0), device_id_type=MESH_ID)
 
     def await_up(t):
         await_bytes(up.at[pl.ds(0, nx * block)], ud_r.at[t])
@@ -566,10 +582,11 @@
                     send(src, src, out_s.at[0], ph_r.at[1, n, s % 2 if isinstance(s, int) else lax.rem(s, 2)], dev(x_=xat(d)))
         hx = nx // 2
         if final:
-            for d in x_order:
-                to = xat(d)
-                src = b_buf.at[s, to // hx, x, pl.ds(2 * lax.rem(to, hx), 2)]
-                send(src, src, out_s.at[0], ph_r.at[1, 0, s % 2], dev(x_=to))
+            for p in range(nx):
+                @pl.when(x != owner[p])
+                def _():
+                    src = b_buf.at[s, p // hx, x, pl.ds(2 * (p % hx), 2)]
+                    send(src, src, out_s.at[0], ph_r.at[1, 0, s % 2], dev(x_=owner[p]))
 
         with scope("bg_b"):
             spread_g(s)
@@ -577,13 +594,17 @@
                 spread_z(top)
 
         if final:
-            with scope("wait_b"):
-                await_bytes(gz.at[pl.ds(0, 2 * (nx - 1))], ph_r.at[1, 0, s % 2])
-            for c in range(2):
-                total = xs[s, 2 * x + c].astype(F32)
-                for k in range(nx):
-                    total = total + b_buf[s, x // hx, k, 2 * lax.rem(x, hx) + c].astype(F32)
-                xs[nsec, 2 * x + c] = total.astype(BF16)
+            for o, pairs in owned.items():
+                @pl.when(x == o)
+                def _():
+                    with scope("wait_b"):
+                        await_bytes(gz.at[pl.ds(0, 2 * (nx - 1) * len(pairs))], ph_r.at[1, 0, s % 2])
+                    for p in pairs:
+                        for c in range(2):
+                            total = xs[s, 2 * p + c].astype(F32)
+                            for k in range(nx):
+                                total = total + b_buf[s, p // hx, k, 2 * (p % hx) + c].astype(F32)
+                            xs[nsec, 2 * p + c] = total.astype(BF16)
             return
         for n in range(2):
             with scope(f"wait_b{n}"):
@@ -677,27 +698,36 @@
             out_term(1)
 
     def await_z(t):
-        await_bytes(up.at[pl.ds(0, block)], uz_r.at[t])
+        await_bytes(up.at[pl.ds(0, block)], wz_r.at[t])
 
     def spread_x(t):
         await_z(t)
         if not isinstance(t, int) or t < top:
-            pl.semaphore_wait(go.at[t], 1)
+            pl.semaphore_wait(flag.at[t], 1)
         src = up.at[pl.ds(slot(t, x), block)]
         for d in x_order:
-            send(src, src, out_s.at[0], ux_r.at[t], dev(x_=xat(d)))
+            to_sem = wz_r.at[2 * nsec + 3 + d] if isinstance(t, int) and t == 1 else wz_r.at[nsec + t]
+            send(src, src, out_s.at[0], to_sem, dev(x_=xat(d)))
+
+    def to_core(t, x_, blocks):
+        src = up.at[pl.ds(slot(t, x_), blocks * block)]
+        send(src, src, out_s.at[2], ud_r.at[t], dev(core_=1))
 
     def spread_core(t):
-        await_bytes(up.at[pl.ds(0, (nx - 1) * block)], ux_r.at[t])
-        src = up.at[pl.ds(slot(t, 0), nx * block)]
-        send(src, src, out_s.at[2], ud_r.at[t], dev(core_=1))
+        await_bytes(up.at[pl.ds(0, (nx - 1) * block)], wz_r.at[nsec + t])
+        to_core(t, 0, nx)
+
+    def spread_core_last():
+        for d in reversed(x_order):
+            await_bytes(up.at[pl.ds(0, block)], wz_r.at[2 * nsec + 3 + d])
+            to_core(1, xat(-d), 1)
 
     @pl.when(core == 0)
     def _():
         spread_pre()
         for r in range(half - 1):
             meet(r)
-        pl.semaphore_signal(near.at[half - 1], inc=1, device_id=dev(core_=1), device_id_type=MESH_ID)
+        pl.semaphore_signal(flag.at[half - 1], inc=1, device_id=dev(core_=1), device_id_type=MESH_ID)
         pa_first()
         li_first()
         pa_second()
@@ -729,12 +759,13 @@
         lax.fori_loop(0, top - 2, move, 0)
         with scope("s_x1"):
             spread_x(1)
+            to_core(1, x, 1)
         finish_one(2)
         with scope("s_in"):
             for t in (1, 0):
                 in_term(t)
         with scope("s_core1"):
-            spread_core(1)
+            spread_core_last()
         with scope("s_out1"):
             out_term(1)
 
@@ -760,10 +791,8 @@
         + row
         + top * 2 * 3 * size(8, hu)
         + (top - 1) * 2 * (nx - 1) * hj
-        + (nx - 1) * 2
         + top * (2 * nz - 1)
-        + nsec * block - 2
-        + block,
+        + top * block,
     )
     with scope("drain"):
         await_bytes(spare.at[pl.ds(0, (nx + (3 if ring else 1)) * li_block)], out_s.at[1])
@@ -772,7 +801,16 @@
         def _():
             for way in range(2):
                 await_bytes(wbuf.at[0, :, :, pl.ds(0, nz - 1)], wz_s.at[way])
-            await_bytes(spare.at[pl.ds(0, both_cores + by_core[1])], out_s.at[0])
+
+        for o in range(nx):
+            pairs = owned.get(o, [])
+            last_tiles = 2 * sum(owner[p] != o for p in range(nx))
+            if pairs:
+                last_tiles += (block - 2 if o else 2 * len(pairs) * (nz - 1)) + (block if o else block * len(pairs))
+
+            @pl.when((core == 1) & (x == o))
+            def _():
+                await_bytes(spare.at[pl.ds(0, both_cores + by_core[1] + last_tiles)], out_s.at[0])
 
         @pl.when(core == 0)
         def _():
@@ -839,9 +877,9 @@
         vmem((spare, 8, LANES), BF16),
         dma((7,)),
         dma((3,)), dma((2,)),
-        dma((2, 2)),
+        dma((4,)),
         dma((2,)),
-        dma((half, 2, 2)),
+        dma((max(half * 4, 2 * nsec + 3 + nx),)),
         dma((6,)),
         dma((1,)),
         dma((5,)),
@@ -849,11 +887,7 @@
         dma((5,)),
         dma((nsec,)),
         dma((nsec,)),
-        dma((nsec,)),
-        dma((nsec,)),
-        dma((2, 3)),
-        pltpu.SemaphoreType.REGULAR((nsec,)),
-        pltpu.SemaphoreType.REGULAR((half,)),
+        pltpu.SemaphoreType.REGULAR((max(nsec, half),)),
     ]
     hbm, on_chip = pl.BlockSpec(memory_space=pltpu.HBM), pl.BlockSpec(memory_space=pltpu.VMEM)
     shapes = (

time: 122 us -> 121 us (level)
  no operation moved by 1% of the time
where the time goes in v7:
time: 121 us; the launch traced here: 120 us
  Pallas kernels  119 us (98%)
    pallas_call x1, Pallas kernels, body(): pl.pallas_call(kernel, out_shape=shapes, in_specs=[hbm] * 5, out_specs=(o...  118 us

profile of v7, /device:TPU:24, one launch (start us, length us, event | category | flops | bytes accessed | tf_op | source)
XLA Modules:
  0.0 119.9 jit_solution(4605444123200497739)
XLA Ops:
  0.6 118.2 %chain.1 = (bf16[16,8,2048]{2,1,0:T(8,128)(2,1)S(1)}, f32[32,2048]{1,0:T(8,128)S(1)}, f32[32,2048]{1,0:T(8,128)S(1)}) custom-call(bf16[128,2048]{1,0:T(8,128)(2,1)} %bitcast.8, bf16[16,8,256]{2,1,0:T(8,128)(2,1)} %bitcast.12, bf16[16,8,2048]{2,1,0:T(8,128)(2,1)} %bitcast.9, bf16[32,2048]{1,0:T(8,128)(2,1)} %bitcast.10, bf16[32,2048]{1,0:T(8,128)(2,1)} %bitcast.11), custom_call_target="tpu_custom_call" | custom-call | tf_op jit(solution)/shard_map/chain/pallas_call | solution.py:905
  118.9 1.0 finish.1

commit v8 on v7

--- a/solution.py
+++ b/solution.py
@@ -150,7 +150,7 @@
         send(mine_, mine_, out_s.at[0], st_r.at[4], dev(y_=yat(2)))
 
     def ring_send(src, m, l, k, way):
-        send(src, src, wz_s.at[way], wz_r.at[((k - 1) * 2 + m) * 2 + l], dev(z_=zat(1 if way == 0 else -1)))
+        send(src, src, wz_s.at[way], wz_r.at[((k - 1) % 2 * 2 + m) * 2 + l], dev(z_=zat(1 if way == 0 else -1)))
 
     swaps = []
     for m in first:
@@ -300,7 +300,7 @@
                 for c in range(2):
                     await_bytes(wbuf.at[m, 0, 0, 0], wx_r.at[c * 2 + m])
         if k > 1:
-            await_bytes(wbuf.at[m, 0, :, pl.ds(0, 2)], wz_r.at[((k - 2) * 2 + m) * 2 + l])
+            await_bytes(wbuf.at[m, 0, :, pl.ds(0, 2)], wz_r.at[(k % 2 * 2 + m) * 2 + l])
         for way, step in ((0, 1), (1, -1)):
             if k == 1 and which == 0:
                 ring_send(wbuf.at[m, l, 0, z], m, l, 1, way)
@@ -311,7 +311,7 @@
 
     def await_last(m):
         for l in range(2):
-            await_bytes(wbuf.at[m, 0, :, 0], wz_r.at[((half - 1) * 2 + m) * 2 + l])
+            await_bytes(wbuf.at[m, 0, :, 0], wz_r.at[((half - 1) % 2 * 2 + m) * 2 + l])
 
     def all_met():
         pl.semaphore_wait(flag.at[half - 1], 1)
@@ -392,7 +392,7 @@
 
         def both(d):
             for to in (partner, y):
-                send(src, dst, out_s.at[0], wz_r.at[t], dev(core_=0, z_=zat(d), y_=to))
+                send(src, dst, out_s.at[0], ph_r.at[t], dev(core_=0, z_=zat(d), y_=to))
 
         both(half)
 
@@ -450,10 +450,10 @@
                     for p in pairs:
                         for l, to in ((0, y), (1, y)) if o else ((ylo, partner), (ylo, y)):
                             src = up.at[pl.ds(slot(0, p, l, a), 2 * (b - a))]
-                            send(src, src, out_s.at[0], wz_r.at[2 * nsec + i], dev(x_=0, core_=0, y_=to))
+                            send(src, src, out_s.at[0], top_r.at[i], dev(x_=0, core_=0, y_=to))
 
     def last_out(i):
-        await_bytes(up.at[pl.ds(0, nx * 4 * len(groups[i]))], wz_r.at[2 * nsec + i])
+        await_bytes(up.at[pl.ds(0, nx * 4 * len(groups[i]))], top_r.at[i])
         for r in groups[i]:
             row = zat(r)
             for l in range(2):
@@ -489,25 +489,21 @@
         if part is not None:
             a_buf[s, l, y] = part.astype(BF16)
         for d in y_order:
-            send(a_buf.at[s, l, y], a_buf.at[s, l, y], out_s.at[0], ph_r.at[0, l, s % 2 if isinstance(s, int) else lax.rem(s, 2)], dev(y_=yat(d)))
+            send(a_buf.at[s, l, y], a_buf.at[s, l, y], out_s.at[0], ph_r.at[l * 2 + (s % 2 if isinstance(s, int) else lax.rem(s, 2))], dev(y_=yat(d)))
 
     def a_part(s, l, n):
         lhs = jnp.concatenate([xs[s, n * hj + j] for j in range(hj)], axis=1)
         w_out = jnp.concatenate([w_t[l, t, n * hn:(n + 1) * hn] for t in range(2 * tiles)], axis=1)
         return jnp.dot(lhs, w_out, preferred_element_type=F32)
 
-    def a_tile(l, away, turned):
+    def a_tiles(l, aways):
         lhs = jnp.concatenate([xs[top - 1, j] for j in range(nsec)], axis=1)
-        t = lax.rem(z // per_tile + away + tiles, tiles)
-        if turned:
-            w_out = jnp.concatenate([w_t[l, c * tiles + t] for c in range(2)], axis=1)
-            part = jnp.dot(lhs, w_out, preferred_element_type=F32)
-        else:
-            w_out = wbuf[1, l, :, pl.ds(t * per_tile, per_tile)].reshape(2 * LANES, fe)
-            part = lax.dot_general(lhs, w_out, (((1,), (1,)), ((), ())), preferred_element_type=F32)
-        for c in range(2):
-            at = pl.multiple_of((c * tiles + t) * LANES, LANES)
-            a_buf[top - 1, l, y, :, pl.ds(at, LANES)] = part[:, c * LANES:(c + 1) * LANES].astype(BF16)
+        at = [(c, lax.rem(z // per_tile + d + tiles, tiles)) for d in aways for c in range(2)]
+        w_out = jnp.concatenate([wbuf[1, l, c, pl.ds(t * per_tile, per_tile)].reshape(LANES, fe) for c, t in at], axis=0)
+        part = lax.dot_general(lhs, w_out, (((1,), (1,)), ((), ())), preferred_element_type=F32).astype(BF16)
+        for i, (c, t) in enumerate(at):
+            to = pl.ds(pl.multiple_of((c * tiles + t) * LANES, LANES), LANES)
+            a_buf[top - 1, l, y, :, to] = part[:, i * LANES:(i + 1) * LANES]
 
     def release(t):
         pl.semaphore_signal(flag.at[t], inc=1, device_id=dev(core_=0), device_id_type=MESH_ID)
@@ -533,14 +529,14 @@
             def _():
                 in_term(s + 2)
 
-            @pl.when(s <= top - 4)
-            def _():
-                await_up(s + 4)
-                out_term(s + 4)
+            @pl.when(s <= top - 5)
+            def _():
+                await_up(s + 5)
+                out_term(s + 5)
 
     def g_half(s, l):
         with scope(f"wait_a{l}"):
-            await_bytes(a_buf.at[s, l, pl.ds(0, 3)], ph_r.at[0, l, s % 2 if isinstance(s, int) else lax.rem(s, 2)])
+            await_bytes(a_buf.at[s, l, pl.ds(0, 3)], ph_r.at[l * 2 + (s % 2 if isinstance(s, int) else lax.rem(s, 2))])
         back = a_buf[s, l, 0].astype(F32)
         for k in range(1, 4):
             back = back + a_buf[s, l, k].astype(F32)
@@ -579,14 +575,14 @@
             if not final:
                 src = b_buf.at[s, n, x]
                 for d in x_order:
-                    send(src, src, out_s.at[0], ph_r.at[1, n, s % 2 if isinstance(s, int) else lax.rem(s, 2)], dev(x_=xat(d)))
+                    send(src, src, out_s.at[0], ph_r.at[4 + n * 2 + (s % 2 if isinstance(s, int) else lax.rem(s, 2))], dev(x_=xat(d)))
         hx = nx // 2
         if final:
             for p in range(nx):
                 @pl.when(x != owner[p])
                 def _():
                     src = b_buf.at[s, p // hx, x, pl.ds(2 * (p % hx), 2)]
-                    send(src, src, out_s.at[0], ph_r.at[1, 0, s % 2], dev(x_=owner[p]))
+                    send(src, src, out_s.at[0], ph_r.at[4 + s % 2], dev(x_=owner[p]))
 
         with scope("bg_b"):
             spread_g(s)
@@ -598,7 +594,7 @@
                 @pl.when(x == o)
                 def _():
                     with scope("wait_b"):
-                        await_bytes(gz.at[pl.ds(0, 2 * (nx - 1) * len(pairs))], ph_r.at[1, 0, s % 2])
+                        await_bytes(gz.at[pl.ds(0, 2 * (nx - 1) * len(pairs))], ph_r.at[4 + s % 2])
                     for p in pairs:
                         for c in range(2):
                             total = xs[s, 2 * p + c].astype(F32)
@@ -608,7 +604,7 @@
             return
         for n in range(2):
             with scope(f"wait_b{n}"):
-                await_bytes(b_buf.at[s, n, pl.ds(0, nx - 1)], ph_r.at[1, n, s % 2 if isinstance(s, int) else lax.rem(s, 2)])
+                await_bytes(b_buf.at[s, n, pl.ds(0, nx - 1)], ph_r.at[4 + n * 2 + (s % 2 if isinstance(s, int) else lax.rem(s, 2))])
             with scope(f"a_mm{n}"):
                 for j in range(hj):
                     total = xs[s, n * hj + j].astype(F32)
@@ -628,7 +624,7 @@
             (1, top_first), (2, top_second), (2, li_first), (4, all_met), (4, top_third), (5, first_out_term), (6, li_second),
             (6, stage_c), (7, stage_d), (7, top_fourth),
         ]
-        plan += [(half if d else 5, lambda d=d: turn(d)) for d in (0, -1, 1) if d % tiles != tiles // 2]
+        plan += [(5, lambda: turn(0))] if tiles > 1 else []
         for k in range(1, half + 1):
             with scope(f"hop{k}"):
                 if k == 1:
@@ -647,18 +643,20 @@
         with scope("top_end"):
             await_bytes(xs.at[0, pl.ds(0, 2 * (nx - 1))], top_r.at[3])
             for l in range(2):
-                for d in early:
-                    a_tile(l, d, True)
+                if early:
+                    a_tiles(l, early)
         with scope("gather_out"):
             hop(0, half, 0)
             await_last(1)
         with scope("a_first"):
             for l in range(2):
-                a_tile(l, tiles // 2, False)
+                a_tiles(l, (tiles // 2,))
                 a_half(top - 1, l)
         with scope("hop_end"):
             hop(0, half, 1)
-            turn(tiles // 2)
+        with scope("turn"):
+            for d in sorted({1 % tiles, (tiles - 1) % tiles, tiles // 2} - ({0} if tiles > 1 else set())):
+                turn(d)
         with scope("b_early"):
             for l in range(2):
                 g_half(top - 1, l)
@@ -682,7 +680,7 @@
             release(1)
         with scope("t_terms"):
             in_term(1)
-            for t in range(min(top, 3), 2, -1):
+            for t in range(min(top, 4), 3, -1):
                 await_up(t)
                 out_term(t)
         with scope("t_in0"):
@@ -691,35 +689,50 @@
             with scope(f"t_last{i}"):
                 last_x(i)
         with scope("t_up2"):
-            await_up(2)
-            out_term(2)
+            for t in (3, 2):
+                await_up(t)
+                out_term(t)
         with scope("t_up1"):
             await_up(1)
             out_term(1)
 
     def await_z(t):
-        await_bytes(up.at[pl.ds(0, block)], wz_r.at[t])
+        await_bytes(up.at[pl.ds(0, block)], ph_r.at[t])
 
     def spread_x(t):
         await_z(t)
         if not isinstance(t, int) or t < top:
             pl.semaphore_wait(flag.at[t], 1)
         src = up.at[pl.ds(slot(t, x), block)]
-        for d in x_order:
-            to_sem = wz_r.at[2 * nsec + 3 + d] if isinstance(t, int) and t == 1 else wz_r.at[nsec + t]
-            send(src, src, out_s.at[0], to_sem, dev(x_=xat(d)))
+        if isinstance(t, int) and t == 1:
+            for d in x_order:
+                send(src, src, out_s.at[0], wx_r.at[d], dev(x_=xat(d)))
+        else:
+            for d in (1, nx - 1) if ring else x_order:
+                send(src, src, out_s.at[0], ud_r.at[t], dev(x_=xat(d)))
+
+
+    def pass_x(t):
+        if ring:
+            await_bytes(up.at[pl.ds(0, 2 * block)], ud_r.at[t])
+            for l, d in ((0, 1), (1, -1)):
+                src = up.at[pl.ds(slot(t, xat(-d), l), 2 * nz)]
+                send(src, src, out_s.at[0], wz_r.at[t], dev(x_=xat(d)))
 
     def to_core(t, x_, blocks):
         src = up.at[pl.ds(slot(t, x_), blocks * block)]
         send(src, src, out_s.at[2], ud_r.at[t], dev(core_=1))
 
     def spread_core(t):
-        await_bytes(up.at[pl.ds(0, (nx - 1) * block)], wz_r.at[nsec + t])
+        if ring:
+            await_bytes(up.at[pl.ds(0, block)], wz_r.at[t])
+        else:
+            await_bytes(up.at[pl.ds(0, (nx - 1) * block)], ud_r.at[t])
         to_core(t, 0, nx)
 
     def spread_core_last():
         for d in reversed(x_order):
-            await_bytes(up.at[pl.ds(0, block)], wz_r.at[2 * nsec + 3 + d])
+            await_bytes(up.at[pl.ds(0, block)], wx_r.at[d])
             to_core(1, xat(-d), 1)
 
     @pl.when(core == 0)
@@ -752,10 +765,13 @@
             with scope("s_in"):
                 in_term(t)
             finish_one(t + 1)
+            with scope("s_pass"):
+                pass_x(t)
             return carry
 
         with scope("s_x7"):
             spread_x(top)
+            pass_x(top)
         lax.fori_loop(0, top - 2, move, 0)
         with scope("s_x1"):
             spread_x(1)
@@ -879,11 +895,11 @@
         dma((3,)), dma((2,)),
         dma((4,)),
         dma((2,)),
-        dma((max(half * 4, 2 * nsec + 3 + nx),)),
+        dma((max(8, nsec),)),
         dma((6,)),
         dma((1,)),
         dma((5,)),
-        dma((2, 2, 2)),
+        dma((max(8, nsec),)),
         dma((5,)),
         dma((nsec,)),
         dma((nsec,)),

time: 121 us -> 121 us (level)
  no operation moved by 1% of the time
where the time goes in v8:
time: 121 us; the launch traced here: 120 us
  Pallas kernels  119 us (98%)
    pallas_call x1, Pallas kernels, body(): pl.pallas_call(kernel, out_shape=shapes, in_specs=[hbm] * 5, out_specs=(o...  118 us

profile of v8, /device:TPU:24, one launch (start us, length us, event | category | flops | bytes accessed | tf_op | source)
XLA Modules:
  0.0 119.8 jit_solution(3455288835271298206)
XLA Ops:
  0.6 118.1 %chain.1 = (bf16[16,8,2048]{2,1,0:T(8,128)(2,1)S(1)}, f32[32,2048]{1,0:T(8,128)S(1)}, f32[32,2048]{1,0:T(8,128)S(1)}) custom-call(bf16[128,2048]{1,0:T(8,128)(2,1)} %bitcast.8, bf16[16,8,256]{2,1,0:T(8,128)(2,1)} %bitcast.12, bf16[16,8,2048]{2,1,0:T(8,128)(2,1)} %bitcast.9, bf16[32,2048]{1,0:T(8,128)(2,1)} %bitcast.10, bf16[32,2048]{1,0:T(8,128)(2,1)} %bitcast.11), custom_call_target="tpu_custom_call" | custom-call | tf_op jit(solution)/shard_map/chain/pallas_call | solution.py:921
  118.8 1.0 finish.1

commit v9 on v7

--- a/solution.py
+++ b/solution.py
@@ -150,7 +150,7 @@
         send(mine_, mine_, out_s.at[0], st_r.at[4], dev(y_=yat(2)))
 
     def ring_send(src, m, l, k, way):
-        send(src, src, wz_s.at[way], wz_r.at[((k - 1) * 2 + m) * 2 + l], dev(z_=zat(1 if way == 0 else -1)))
+        send(src, src, wz_s.at[way], wz_r.at[((k - 1) % 2 * 2 + m) * 2 + l], dev(z_=zat(1 if way == 0 else -1)))
 
     swaps = []
     for m in first:
@@ -300,7 +300,7 @@
                 for c in range(2):
                     await_bytes(wbuf.at[m, 0, 0, 0], wx_r.at[c * 2 + m])
         if k > 1:
-            await_bytes(wbuf.at[m, 0, :, pl.ds(0, 2)], wz_r.at[((k - 2) * 2 + m) * 2 + l])
+            await_bytes(wbuf.at[m, 0, :, pl.ds(0, 2)], wz_r.at[(k % 2 * 2 + m) * 2 + l])
         for way, step in ((0, 1), (1, -1)):
             if k == 1 and which == 0:
                 ring_send(wbuf.at[m, l, 0, z], m, l, 1, way)
@@ -311,7 +311,7 @@
 
     def await_last(m):
         for l in range(2):
-            await_bytes(wbuf.at[m, 0, :, 0], wz_r.at[((half - 1) * 2 + m) * 2 + l])
+            await_bytes(wbuf.at[m, 0, :, 0], wz_r.at[((half - 1) % 2 * 2 + m) * 2 + l])
 
     def all_met():
         pl.semaphore_wait(flag.at[half - 1], 1)
@@ -392,7 +392,7 @@
 
         def both(d):
             for to in (partner, y):
-                send(src, dst, out_s.at[0], wz_r.at[t], dev(core_=0, z_=zat(d), y_=to))
+                send(src, dst, out_s.at[0], ph_r.at[t], dev(core_=0, z_=zat(d), y_=to))
 
         both(half)
 
@@ -450,10 +450,10 @@
                     for p in pairs:
                         for l, to in ((0, y), (1, y)) if o else ((ylo, partner), (ylo, y)):
                             src = up.at[pl.ds(slot(0, p, l, a), 2 * (b - a))]
-                            send(src, src, out_s.at[0], wz_r.at[2 * nsec + i], dev(x_=0, core_=0, y_=to))
+                            send(src, src, out_s.at[0], top_r.at[i], dev(x_=0, core_=0, y_=to))
 
     def last_out(i):
-        await_bytes(up.at[pl.ds(0, nx * 4 * len(groups[i]))], wz_r.at[2 * nsec + i])
+        await_bytes(up.at[pl.ds(0, nx * 4 * len(groups[i]))], top_r.at[i])
         for r in groups[i]:
             row = zat(r)
             for l in range(2):
@@ -489,7 +489,7 @@
         if part is not None:
             a_buf[s, l, y] = part.astype(BF16)
         for d in y_order:
-            send(a_buf.at[s, l, y], a_buf.at[s, l, y], out_s.at[0], ph_r.at[0, l, s % 2 if isinstance(s, int) else lax.rem(s, 2)], dev(y_=yat(d)))
+            send(a_buf.at[s, l, y], a_buf.at[s, l, y], out_s.at[0], ph_r.at[l * 2 + (s % 2 if isinstance(s, int) else lax.rem(s, 2))], dev(y_=yat(d)))
 
     def a_part(s, l, n):
         lhs = jnp.concatenate([xs[s, n * hj + j] for j in range(hj)], axis=1)
@@ -540,7 +540,7 @@
 
     def g_half(s, l):
         with scope(f"wait_a{l}"):
-            await_bytes(a_buf.at[s, l, pl.ds(0, 3)], ph_r.at[0, l, s % 2 if isinstance(s, int) else lax.rem(s, 2)])
+            await_bytes(a_buf.at[s, l, pl.ds(0, 3)], ph_r.at[l * 2 + (s % 2 if isinstance(s, int) else lax.rem(s, 2))])
         back = a_buf[s, l, 0].astype(F32)
         for k in range(1, 4):
             back = back + a_buf[s, l, k].astype(F32)
@@ -579,14 +579,14 @@
             if not final:
                 src = b_buf.at[s, n, x]
                 for d in x_order:
-                    send(src, src, out_s.at[0], ph_r.at[1, n, s % 2 if isinstance(s, int) else lax.rem(s, 2)], dev(x_=xat(d)))
+                    send(src, src, out_s.at[0], ph_r.at[4 + n * 2 + (s % 2 if isinstance(s, int) else lax.rem(s, 2))], dev(x_=xat(d)))
         hx = nx // 2
         if final:
             for p in range(nx):
                 @pl.when(x != owner[p])
                 def _():
                     src = b_buf.at[s, p // hx, x, pl.ds(2 * (p % hx), 2)]
-                    send(src, src, out_s.at[0], ph_r.at[1, 0, s % 2], dev(x_=owner[p]))
+                    send(src, src, out_s.at[0], ph_r.at[4 + s % 2], dev(x_=owner[p]))
 
         with scope("bg_b"):
             spread_g(s)
@@ -598,7 +598,7 @@
                 @pl.when(x == o)
                 def _():
                     with scope("wait_b"):
-                        await_bytes(gz.at[pl.ds(0, 2 * (nx - 1) * len(pairs))], ph_r.at[1, 0, s % 2])
+                        await_bytes(gz.at[pl.ds(0, 2 * (nx - 1) * len(pairs))], ph_r.at[4 + s % 2])
                     for p in pairs:
                         for c in range(2):
                             total = xs[s, 2 * p + c].astype(F32)
@@ -608,7 +608,7 @@
             return
         for n in range(2):
             with scope(f"wait_b{n}"):
-                await_bytes(b_buf.at[s, n, pl.ds(0, nx - 1)], ph_r.at[1, n, s % 2 if isinstance(s, int) else lax.rem(s, 2)])
+                await_bytes(b_buf.at[s, n, pl.ds(0, nx - 1)], ph_r.at[4 + n * 2 + (s % 2 if isinstance(s, int) else lax.rem(s, 2))])
             with scope(f"a_mm{n}"):
                 for j in range(hj):
                     total = xs[s, n * hj + j].astype(F32)
@@ -698,7 +698,7 @@
             out_term(1)
 
     def await_z(t):
-        await_bytes(up.at[pl.ds(0, block)], wz_r.at[t])
+        await_bytes(up.at[pl.ds(0, block)], ph_r.at[t])
 
     def spread_x(t):
         await_z(t)
@@ -706,7 +706,7 @@
             pl.semaphore_wait(flag.at[t], 1)
         src = up.at[pl.ds(slot(t, x), block)]
         for d in x_order:
-            to_sem = wz_r.at[2 * nsec + 3 + d] if isinstance(t, int) and t == 1 else wz_r.at[nsec + t]
+            to_sem = wx_r.at[d] if isinstance(t, int) and t == 1 else ud_r.at[t]
             send(src, src, out_s.at[0], to_sem, dev(x_=xat(d)))
 
     def to_core(t, x_, blocks):
@@ -714,12 +714,12 @@
         send(src, src, out_s.at[2], ud_r.at[t], dev(core_=1))
 
     def spread_core(t):
-        await_bytes(up.at[pl.ds(0, (nx - 1) * block)], wz_r.at[nsec + t])
+        await_bytes(up.at[pl.ds(0, (nx - 1) * block)], ud_r.at[t])
         to_core(t, 0, nx)
 
     def spread_core_last():
         for d in reversed(x_order):
-            await_bytes(up.at[pl.ds(0, block)], wz_r.at[2 * nsec + 3 + d])
+            await_bytes(up.at[pl.ds(0, block)], wx_r.at[d])
             to_core(1, xat(-d), 1)
 
     @pl.when(core == 0)
@@ -879,11 +879,11 @@
         dma((3,)), dma((2,)),
         dma((4,)),
         dma((2,)),
-        dma((max(half * 4, 2 * nsec + 3 + nx),)),
+        dma((8,)),
         dma((6,)),
         dma((1,)),
         dma((5,)),
-        dma((2, 2, 2)),
+        dma((max(8, nsec),)),
         dma((5,)),
         dma((nsec,)),
         dma((nsec,)),

time: 121 us -> 121 us (level)
  no operation moved by 1% of the time
where the time goes in v9:
time: 121 us; the launch traced here: 120 us
  Pallas kernels  119 us (98%)
    pallas_call x1, Pallas kernels, body(): pl.pallas_call(kernel, out_shape=shapes, in_specs=[hbm] * 5, out_specs=(o...  118 us

profile of v9, /device:TPU:24, one launch (start us, length us, event | category | flops | bytes accessed | tf_op | source)
XLA Modules:
  0.0 119.7 jit_solution(5450124539853582793)
XLA Ops:
  0.6 118.0 %chain.1 = (bf16[16,8,2048]{2,1,0:T(8,128)(2,1)S(1)}, f32[32,2048]{1,0:T(8,128)S(1)}, f32[32,2048]{1,0:T(8,128)S(1)}) custom-call(bf16[128,2048]{1,0:T(8,128)(2,1)} %bitcast.8, bf16[16,8,256]{2,1,0:T(8,128)(2,1)} %bitcast.12, bf16[16,8,2048]{2,1,0:T(8,128)(2,1)} %bitcast.9, bf16[32,2048]{1,0:T(8,128)(2,1)} %bitcast.10, bf16[32,2048]{1,0:T(8,128)(2,1)} %bitcast.11), custom_call_target="tpu_custom_call" | custom-call | tf_op jit(solution)/shard_map/chain/pallas_call | solution.py:905
  118.7 1.0 finish.1

commit v10 on v9

--- a/solution.py
+++ b/solution.py
@@ -457,10 +457,8 @@
         for r in groups[i]:
             row = zat(r)
             for l in range(2):
-                for k in range(nx):
-                    for c in range(2):
-                        at = l * fe + (2 * k + c) * LANES
-                        ig_out[row, :, at:at + LANES] = up[slot(0, k, l, r) + c]
+                parts = [up[slot(0, k, l, r) + c] for k in range(nx) for c in range(2)]
+                ig_out[row, :, l * fe:(l + 1) * fe] = jnp.concatenate(parts, axis=1)
 
     def spread_g(t):
         def to(d, c):
@@ -538,7 +536,7 @@
                 await_up(s + 4)
                 out_term(s + 4)
 
-    def g_half(s, l):
+    def g_half(s, l, keep=True):
         with scope(f"wait_a{l}"):
             await_bytes(a_buf.at[s, l, pl.ds(0, 3)], ph_r.at[l * 2 + (s % 2 if isinstance(s, int) else lax.rem(s, 2))])
         back = a_buf[s, l, 0].astype(F32)
@@ -547,7 +545,8 @@
         g = []
         for t in range(2 * tiles):
             g_tile = (back[:, t * LANES:(t + 1) * LANES] * slope[s, l, t]).astype(BF16)
-            gbuf[s, l, t] = g_tile
+            if keep:
+                gbuf[s, l, t] = g_tile
             g.append(g_tile)
         return jnp.concatenate(g, axis=1)
 
@@ -562,11 +561,11 @@
     def application(s, final=False, begin=False):
         if not begin:
             background_a(s)
-            g_first = g_half(s, 0)
+            g_first = g_half(s, 0, False)
             for n in range(2):
                 w_in = wbuf[0, 0, :, :, :, n * hn:(n + 1) * hn].reshape(hu, hn)
                 b_acc[n] = jnp.dot(g_first, w_in, preferred_element_type=F32)
-            g = g_half(s, 1)
+            g = g_half(s, 1, False)
         for n in range(2):
             if begin:
                 part = b_tile(n, tiles // 2)
@@ -589,6 +588,10 @@
                     send(src, src, out_s.at[0], ph_r.at[4 + s % 2], dev(x_=owner[p]))
 
         with scope("bg_b"):
+            if not begin:
+                for l, part in enumerate((g_first, g)):
+                    for t in range(2 * tiles):
+                        gbuf[s, l, t] = part[:, t * LANES:(t + 1) * LANES]
             spread_g(s)
             if begin:
                 spread_z(top)

time: 121 us -> 121 us (level)
  no operation moved by 1% of the time
where the time goes in v10:
time: 121 us; the launch traced here: 120 us
  Pallas kernels  119 us (98%)
    pallas_call x1, Pallas kernels, body(): pl.pallas_call(kernel, out_shape=shapes, in_specs=[hbm] * 5, out_specs=(o...  118 us

profile of v10, /device:TPU:24, one launch (start us, length us, event | category | flops | bytes accessed | tf_op | source)
XLA Modules:
  0.0 119.7 jit_solution(8878854242430763887)
XLA Ops:
  0.6 118.0 %chain.1 = (bf16[16,8,2048]{2,1,0:T(8,128)(2,1)S(1)}, f32[32,2048]{1,0:T(8,128)S(1)}, f32[32,2048]{1,0:T(8,128)S(1)}) custom-call(bf16[128,2048]{1,0:T(8,128)(2,1)} %bitcast.8, bf16[16,8,256]{2,1,0:T(8,128)(2,1)} %bitcast.12, bf16[16,8,2048]{2,1,0:T(8,128)(2,1)} %bitcast.9, bf16[32,2048]{1,0:T(8,128)(2,1)} %bitcast.10, bf16[32,2048]{1,0:T(8,128)(2,1)} %bitcast.11), custom_call_target="tpu_custom_call" | custom-call | tf_op jit(solution)/shard_map/chain/pallas_call | solution.py:908
  118.7 1.0 finish.1

commit v11 on v7

--- a/solution.py
+++ b/solution.py
@@ -290,7 +290,8 @@
         rows = gt[pl.ds(pl.multiple_of(lax.rem(z, per_tile) * fb, fb), fb), :].astype(BF16)
         gi_out[...] += jnp.dot(rows, li[lax.rem(t, 2), t // 2], preferred_element_type=F32)
 
-    hu, hn, hj = 2 * nz * fb, fe // 2, nsec // 2
+    nb = 4 if nx % 4 == 0 else 2
+    hu, hn, hj = 2 * nz * fb, fe // nb, nsec // nb
     def hop(m, k, which):
         l = ylo if which == 0 else other
         if k == 1:
@@ -563,11 +564,11 @@
         if not begin:
             background_a(s)
             g_first = g_half(s, 0)
-            for n in range(2):
+            for n in range(nb):
                 w_in = wbuf[0, 0, :, :, :, n * hn:(n + 1) * hn].reshape(hu, hn)
                 b_acc[n] = jnp.dot(g_first, w_in, preferred_element_type=F32)
             g = g_half(s, 1)
-        for n in range(2):
+        for n in range(nb):
             if begin:
                 part = b_tile(n, tiles // 2)
             else:
@@ -580,7 +581,7 @@
                 src = b_buf.at[s, n, x]
                 for d in x_order:
                     send(src, src, out_s.at[0], ph_r.at[1, n, s % 2 if isinstance(s, int) else lax.rem(s, 2)], dev(x_=xat(d)))
-        hx = nx // 2
+        hx = nx // nb
         if final:
             for p in range(nx):
                 @pl.when(x != owner[p])
@@ -606,7 +607,7 @@
                                 total = total + b_buf[s, p // hx, k, 2 * (p % hx) + c].astype(F32)
                             xs[nsec, 2 * p + c] = total.astype(BF16)
             return
-        for n in range(2):
+        for n in range(nb):
             with scope(f"wait_b{n}"):
                 await_bytes(b_buf.at[s, n, pl.ds(0, nx - 1)], ph_r.at[1, n, s % 2 if isinstance(s, int) else lax.rem(s, 2)])
             with scope(f"a_mm{n}"):
@@ -615,12 +616,13 @@
                     for k in range(nx):
                         total = total + b_buf[s, n, k, j].astype(F32)
                     xs[s - 1, n * hj + j] = total.astype(BF16)
-                if n == 0:
+                if n < nb - 1:
                     for l in range(2):
-                        a_acc[l] = a_part(s - 1, l, 0)
+                        part = a_part(s - 1, l, n)
+                        a_acc[l] = a_acc[l] + part if n else part
         for l in range(2):
             with scope(f"a_last{l}"):
-                a_half(s - 1, l, a_acc[l] + a_part(s - 1, l, 1))
+                a_half(s - 1, l, a_acc[l] + a_part(s - 1, l, nb - 1))
 
     @pl.when(core == 1)
     def _():
@@ -662,7 +664,7 @@
         with scope("b_early"):
             for l in range(2):
                 g_half(top - 1, l)
-            for n in range(2):
+            for n in range(nb):
                 b_acc[n] = sum((b_tile(n, d) for d in early), jnp.zeros((8, hn), F32))
         with scope("gather_in"):
             await_last(0)
@@ -790,7 +792,7 @@
         + (nx - 1) * 2
         + row
         + top * 2 * 3 * size(8, hu)
-        + (top - 1) * 2 * (nx - 1) * hj
+        + (top - 1) * nb * (nx - 1) * hj
         + top * (2 * nz - 1)
         + top * block,
     )
@@ -842,6 +844,7 @@
     half = nz // 2
     dma = pltpu.SemaphoreType.DMA
     vmem = pltpu.VMEM
+    nb = 4 if nx % 4 == 0 else 2
     spare = 2048
     scratch = [
         vmem((2, fb, width), BF16),
@@ -867,9 +870,9 @@
         vmem((2, 2 * tiles, fe, LANES), BF16),
         vmem((nsec + 1, nsec, 8, LANES), BF16),
         vmem((nsec, 2, 4, 8, 2 * nz * fb), BF16),
-        vmem((nsec, 2, nx, nx, 8, LANES), BF16),
+        vmem((nsec, nb, nx, nsec // nb, 8, LANES), BF16),
         vmem((2, 8, 2 * nz * fb), F32),
-        vmem((2, 8, fe // 2), F32),
+        vmem((nb, 8, fe // nb), F32),
         vmem((nsec, 2, 2 * tiles, 8, LANES), BF16),
         vmem((nsec * nz, 8, LANES), BF16),
         vmem((LANES, tok), F32),
@@ -883,7 +886,7 @@
         dma((6,)),
         dma((1,)),
         dma((5,)),
-        dma((2, 2, 2)),
+        dma((2, 4, 2)),
         dma((5,)),
         dma((nsec,)),
         dma((nsec,)),

time: 121 us -> 121 us (level)
  no operation moved by 1% of the time
where the time goes in v11:
time: 121 us; the launch traced here: 120 us
  Pallas kernels  119 us (98%)
    pallas_call x1, Pallas kernels, body(): pl.pallas_call(kernel, out_shape=shapes, in_specs=[hbm] * 5, out_specs=(o...  118 us

profile of v11, /device:TPU:24, one launch (start us, length us, event | category | flops | bytes accessed | tf_op | source)
XLA Modules:
  0.0 120.0 jit_solution(7689919175451176146)
XLA Ops:
  0.6 118.3 %chain.1 = (bf16[16,8,2048]{2,1,0:T(8,128)(2,1)S(1)}, f32[32,2048]{1,0:T(8,128)S(1)}, f32[32,2048]{1,0:T(8,128)S(1)}) custom-call(bf16[128,2048]{1,0:T(8,128)(2,1)} %bitcast.8, bf16[16,8,256]{2,1,0:T(8,128)(2,1)} %bitcast.12, bf16[16,8,2048]{2,1,0:T(8,128)(2,1)} %bitcast.9, bf16[32,2048]{1,0:T(8,128)(2,1)} %bitcast.10, bf16[32,2048]{1,0:T(8,128)(2,1)} %bitcast.11), custom_call_target="tpu_custom_call" | custom-call | tf_op jit(solution)/shard_map/chain/pallas_call | solution.py:908
  119.0 1.0 finish.1

commit v12 on v7

--- a/solution.py
+++ b/solution.py
@@ -78,8 +78,8 @@
     def yat(d):
         return lax.rem(y + d, 4)
 
-    y_order = (2, 1, 3)
-    x_order = sorted(range(1, nx), key=lambda d: -min(d, nx - d))
+    y_order = (2, 3, 1)
+    x_order = sorted(range(1, nx), key=lambda d: (-min(d, nx - d), -d))
     z_order = sorted(range(1, nz), key=lambda d: -min(d, nz - d))
     sections = [(d, False) for d in x_order] + [(d, True) for d in x_order] + [(0, True)]
 

time: 121 us -> 121 us (level)
  no operation moved by 1% of the time
where the time goes in v12:
time: 121 us; the launch traced here: 120 us
  Pallas kernels  119 us (98%)
    pallas_call x1, Pallas kernels, body(): pl.pallas_call(kernel, out_shape=shapes, in_specs=[hbm] * 5, out_specs=(o...  118 us

profile of v12, /device:TPU:24, one launch (start us, length us, event | category | flops | bytes accessed | tf_op | source)
XLA Modules:
  0.0 119.9 jit_solution(6494338346428438494)
XLA Ops:
  0.6 118.2 %chain.1 = (bf16[16,8,2048]{2,1,0:T(8,128)(2,1)S(1)}, f32[32,2048]{1,0:T(8,128)S(1)}, f32[32,2048]{1,0:T(8,128)S(1)}) custom-call(bf16[128,2048]{1,0:T(8,128)(2,1)} %bitcast.8, bf16[16,8,256]{2,1,0:T(8,128)(2,1)} %bitcast.12, bf16[16,8,2048]{2,1,0:T(8,128)(2,1)} %bitcast.9, bf16[32,2048]{1,0:T(8,128)(2,1)} %bitcast.10, bf16[32,2048]{1,0:T(8,128)(2,1)} %bitcast.11), custom_call_target="tpu_custom_call" | custom-call | tf_op jit(solution)/shard_map/chain/pallas_call | solution.py:905
  118.9 1.0 finish.1
